TPU v7x, 128 devices: a whole 4x4x4 slice. The times are simulated.
128 devices in a mesh: pair: 16 (over x, z_lo, core), ga: 8 (over z_hi, y).
Axes of the slice: x: 4, y: 4, z: 4 (z_hi: 2, z_lo: 2; z = z_hi * 2 + z_lo), core: 2. Of those that a mesh axis runs over, the one named last changes fastest.
Arguments:
- densities: bfloat16 [24576, 4096], P('pair', 'ga'), may hold values from -6 to 6
- val_band: int32 [24576], P('pair'), may hold values from 0 to 127
- cond_band: int32 [24576], P('pair'), may hold values from 0 to 255
- val_energy: float32 [128], replicated, may hold values from -12 to -1
- cond_energy: float32 [256], replicated, may hold values from 1 to 12
Outputs:
- chi: float32 [4096, 4096], P('ga', 'pair')
All inputs are finite; a program needn't handle non-finite values.
Results may differ from a plain program's by a relative error of at most 0.0012.
Values may be sent and summed in bfloat16 or wider, within the bound.
No kernel may reach another device: no remote copies, remote signals or barrier semaphores. Data moves between devices by JAX's collectives and lax.ppermute only.
A program may use at most 128 MiB of HBM per device.

v0:
```python
import math

import jax
import jax.numpy as jnp
import numpy as np
from jax import lax
from jax.sharding import PartitionSpec as P


AXES = ("pair", "ga")
CUTS = (384, 384, 384, 384)
GAIN = 4.0

O, N, S, Z = (0, 0), (1, 0), (3, 0), (1, 1)
EARLY = ((O, O), (O, N), (O, S), (S, N))
LATE = ((O, Z), (Z, O), (Z, N), (Z, S))
PLAN = (
    ((0, 3, 2, 1), (1, 3, 0, 2), (0, 1, 1, 1)),
    ((2, 3, 1, 0), (1, 3, 2, 0), (1, 0, 0, 1)),
    ((2, 0, 3, 1), (3, 1, 2, 0), (1, 0, 1, 1)),
    ((1, 2, 0, 3), (2, 3, 1, 0), (0, 0, 1, 0)),
    ((1, 3, 0, 2), (0, 2, 1, 3), (0, 1, 0, 1)),
    ((3, 0, 2, 1), (1, 0, 3, 2), (1, 1, 0, 0)),
    ((1, 3, 2, 0), (2, 0, 3, 1), (1, 0, 1, 0)),
    ((0, 1, 3, 2), (0, 2, 3, 1), (1, 0, 0, 1)),
)


def index(x, y, z, core):
    x, y, z = x % 4, y % 4, z % 4
    return (4 * x + 2 * (z % 2) + core) * 8 + 4 * (z // 2) + y


def devices():
    for x in range(4):
        for y in range(4):
            for z in range(4):
                for core in range(2):
                    yield x, y, z, core


def shift(value, dx=0, dy=0, dz=0, swap=False):
    pairs = [
        (index(x, y, z, c), index(x + dx, y + dy, z + dz, 1 - c if swap else c))
        for x, y, z, c in devices()
    ]
    return lax.ppermute(value, AXES, pairs)


def swap_z_lo(value):
    pairs = [(index(x, y, z, c), index(x, y, z ^ 1, c)) for x, y, z, c in devices()]
    return lax.ppermute(value, AXES, pairs)


def to_owner(value):
    pairs = []
    for x, y, z, c in devices():
        early, late, keeper = PLAN[4 * (z // 2) + y]
        keeps = keeper[x] == z % 2
        row, col = EARLY[early[x]] if keeps else LATE[late[x]]
        row_y, row_hi = (y + row[0]) % 4, (z // 2 + row[1]) % 2
        block = 4 * ((z // 2 + col[1]) % 2) + (y + col[0]) % 4
        pairs.append(
            (index(x, y, z, c), index(block // 2, row_y, 2 * row_hi + block % 2, c))
        )
    return lax.ppermute(value, AXES, pairs)


def table():
    rows = []
    for pair in range(16):
        x, z_lo = pair // 4, pair // 2 % 2
        for ga in range(8):
            early, late, keeper = PLAN[ga]
            rows.append(
                [early[(x + d) % 4] for d in range(4)]
                + [late[(x + d) % 4] for d in range(4)]
                + [int(keeper[x] == z_lo)]
            )
    return np.array(rows, np.int32)


def lookup(bands, energy):
    levels = lax.broadcasted_iota(jnp.int32, (1, energy.shape[0]), 1)
    onehot = (bands[:, None] == levels).astype(jnp.float32)
    return jnp.sum(onehot * energy[None, :], axis=1)


def product(left, right):
    return lax.dot_general(
        left, right, (((0,), (0,)), ((), ())), preferred_element_type=jnp.float32
    )


def body(own, val_band, cond_band, val_energy, cond_energy):
    pairs_total = own.shape[0] * lax.axis_size("pair")
    pair, ga = lax.axis_index("pair"), lax.axis_index("ga")
    core = pair % 2
    plan = lax.dynamic_slice(jnp.asarray(table()), (pair * 8 + ga, 0), (1, 9))[0]
    half = own.shape[1] // 2
    starts = np.cumsum((0,) + CUTS)

    def rows(block, k):
        return block[starts[k] : starts[k + 1]]

    norths, farther = [], []
    for k in range(len(CUTS)):
        norths.append(shift(rows(own, k), dy=-1))
        if k == 0:
            south = shift(own, dy=1)
    for k in range(len(CUTS)):
        farther.append(shift(norths[k], dz=2))

    gap = lookup(val_band, val_energy) - lookup(cond_band, cond_energy)
    weight = (4.0 * GAIN) / (gap * math.sqrt(pairs_total))

    def scale(block, weight):
        return (weight[:, None] * block.astype(jnp.float32)).astype(jnp.bfloat16)

    def cols(block, side):
        return lax.dynamic_slice(block, (0, side * half), (block.shape[0], half))

    def swap(products):
        theirs = [product(left, cols(right, 1 - core)) for left, right in products]
        theirs = jnp.stack([t.astype(jnp.float16) for t in theirs])
        theirs = shift(theirs, swap=True)
        mine = jnp.stack([product(left, cols(right, core)) for left, right in products])
        return mine, theirs

    def over_x(mine, theirs, which):
        def pick(d):
            at = (which[d], 0, 0)
            size = (1,) + mine.shape[1:]
            return (
                lax.dynamic_slice(mine, at, size)[0]
                + lax.dynamic_slice(theirs, at, size)[0].astype(jnp.float32)
            )

        got = []
        for d in (1, 3, 2):
            got.append(shift(pick(d).astype(jnp.float16), dx=d))
        return pick(0), got

    north = jnp.concatenate(norths, 0)
    scaled = scale(own, weight)
    left = [scaled, scaled, scaled, scale(south, weight)]
    early = swap(list(zip(left, [own, north, south, north])))
    early, early_got = over_x(*early, plan[:4])

    far = jnp.concatenate(farther, 0)
    scaled_far = scale(far, weight)
    left = [scaled, scaled_far, scaled_far, scaled_far]
    late = swap(list(zip(left, [far, own, north, south])))
    late, late_got = over_x(*late, plan[4:8])

    early = early + sum(g.astype(jnp.float32) for g in early_got)
    late = late + sum(g.astype(jnp.float32) for g in late_got)
    keeps = plan[8] == 1
    kept = jnp.where(keeps, early, late)
    got = swap_z_lo(jnp.where(keeps, late, early).astype(jnp.float16))
    total = kept + got.astype(jnp.float32)
    total = to_owner(total.astype(jnp.float16))
    return total.astype(jnp.float32) * (1.0 / GAIN)


def solution(mesh):
    placed = (P("pair", "ga"), P("pair"), P("pair"), P(), P())
    return jax.shard_map(
        body, mesh=mesh, in_specs=placed, out_specs=P("ga", "pair"), check_vma=False
    )
```

profile of v0, /device:TPU:62, one launch (start us, length us, event | category | flops | bytes accessed | tf_op | source)
XLA Modules:
  0.0 136.3 jit_solution(17592178419389384338)
XLA Ops:
  0.3 1.5 %fusion.46 = (bf16[384,512]{1,0:T(8,128)(2,1)S(1)}, bf16[384,512]{1,0:T(8,128)(2,1)S(1)}, bf16[384,512]{1,0:T(8,128)(2,1)S(1)}, bf16[384,512]{1,0:T(8,128)(2,1)S(1)}) fusion(bf16[1536,512]{1,0:T(8,128)(2,1)} %param.6), kind=kLoop, calls=%fused_computation.94 | loop fusion | bytes 3145728 | tf_op jit(solution)/shard_map/slice | solution.py:104
  1.8 1.9 %collective-permute-start = (bf16[384,512]{1,0:T(8,128)(2,1)S(1)}, bf16[384,512]{1,0:T(8,128)(2,1)}, u32[]{:S(2)}, u32[]{:S(2)}) collective-permute-start(bf16[384,512]{1,0:T(8,128)(2,1)S(1)} %get-tuple-element.17), channel_id=1, source_target_pairs={{0,3},{8,11},{16,19},{24,27},{4,7},{12,15},{20,23},{28,31},{1,0},{... | collective-permute-start | bytes 1179656 | tf_op jit(solution)/shard_map/ppermute | solution.py:47
  3.6 0.7 collective-permute-start.1
  4.8 1.7 %collective-permute-start.3 = (bf16[384,512]{1,0:T(8,128)(2,1)S(1)}, bf16[384,512]{1,0:T(8,128)(2,1)S(1)}, u32[]{:S(2)}, u32[]{:S(2)}) collective-permute-start(bf16[384,512]{1,0:T(8,128)(2,1)S(1)} %get-tuple-element.14), channel_id=1, source_target_pairs={{0,3},{8,11},{16,19},{24,27},{4,7},{12,15},{20,23},{28,31},{1,0},{... | collective-permute-start | bytes 1179656 | tf_op jit(solution)/shard_map/ppermute | solution.py:47
  6.5 1.2 select_reduce_fusion
  7.7 1.2 select_reduce_fusion.1
  8.9 1.6 %fusion = f16[1,512,256]{2,1,0:T(8,128)(2,1)} fusion(bf16[1536,512]{1,0:T(8,128)(2,1)S(1)} %copy-done.1, s32[]{:T(128)S(6)} %select_n.79, f32[1536]{0:T(1024)S(1)} %multiply_divide_fusion), kind=kOutput, calls=%fused_computation.23 | convolution fusion | flops 405143552 | bytes 2629636 | tf_op jit(solution)/shard_map/dot_general | solution.py:90
  10.5 1.7 %convolution_bitcast_fusion.7 = f32[1,512,256]{2,1,0:T(8,128)} fusion(bf16[1536,512]{1,0:T(8,128)(2,1)S(1)} %copy-done.1, s32[]{:T(128)S(6)} %select_n.77, f32[1536]{0:T(1024)S(1)} %multiply_divide_fusion), kind=kOutput, calls=%fused_computation.14 | convolution fusion | flops 405012480 | bytes 2891780 | tf_op jit(solution)/shard_map/dot_general | solution.py:90
  24.7 3.1 %collective-permute-start.9 = (bf16[384,512]{1,0:T(8,128)(2,1)}, bf16[384,512]{1,0:T(8,128)(2,1)S(1)}, u32[]{:S(2)}, u32[]{:S(2)}) collective-permute-start(bf16[384,512]{1,0:T(8,128)(2,1)} %collective-permute-done), channel_id=1, source_target_pairs={{0,4},{8,12},{16,20},{24,28},{4,0},{12,8},{20,16},{28,24},{1,5},{9... | collective-permute-start | bytes 1179656 | tf_op jit(solution)/shard_map/ppermute | solution.py:47
  28.3 1.0 constant_dynamic-update-slice_fusion.3
  29.4 1.0 constant_dynamic-update-slice_fusion.2
  30.4 1.6 %collective-permute-done.2 = bf16[384,512]{1,0:T(8,128)(2,1)} collective-permute-done((bf16[384,512]{1,0:T(8,128)(2,1)S(1)}, bf16[384,512]{1,0:T(8,128)(2,1)}, u32[]{:S(2)}, u32[]{:S(2)}) %collective-permute-start.2) | collective-permute-done | bytes 393248 | tf_op jit(solution)/shard_map/ppermute | solution.py:47
  32.0 1.0 constant_dynamic-update-slice_fusion.1
  33.0 6.1 %collective-permute-done.3 = bf16[384,512]{1,0:T(8,128)(2,1)S(1)} collective-permute-done((bf16[384,512]{1,0:T(8,128)(2,1)S(1)}, bf16[384,512]{1,0:T(8,128)(2,1)S(1)}, u32[]{:S(2)}, u32[]{:S(2)}) %collective-permute-start.3) | collective-permute-done | bytes 393248 | tf_op jit(solution)/shard_map/ppermute | solution.py:47
  39.1 0.9 fusion.1
  40.0 3.1 %collective-permute-start.11 = (bf16[384,512]{1,0:T(8,128)(2,1)}, bf16[384,512]{1,0:T(8,128)(2,1)S(1)}, u32[]{:S(2)}, u32[]{:S(2)}) collective-permute-start(bf16[384,512]{1,0:T(8,128)(2,1)} %collective-permute-done.2), channel_id=1, source_target_pairs={{0,4},{8,12},{16,20},{24,28},{4,0},{12,8},{20,16},{28,24},{1,5},{9... | collective-permute-start | bytes 1179656 | tf_op jit(solution)/shard_map/ppermute | solution.py:47
  43.6 0.9 convolution_bitcast_fusion.6
  44.6 1.2 collective-permute-done.10
  45.8 8.4 %collective-permute-done.11 = bf16[384,512]{1,0:T(8,128)(2,1)S(1)} collective-permute-done((bf16[384,512]{1,0:T(8,128)(2,1)}, bf16[384,512]{1,0:T(8,128)(2,1)S(1)}, u32[]{:S(2)}, u32[]{:S(2)}) %collective-permute-start.11) | collective-permute-done | bytes 393248 | tf_op jit(solution)/shard_map/ppermute | solution.py:47
  54.2 7.2 %collective-permute-done.12 = bf16[384,512]{1,0:T(8,128)(2,1)S(1)} collective-permute-done((bf16[384,512]{1,0:T(8,128)(2,1)S(1)}, bf16[384,512]{1,0:T(8,128)(2,1)S(1)}, u32[]{:S(2)}, u32[]{:S(2)}) %collective-permute-start.12) | collective-permute-done | bytes 393248 | tf_op jit(solution)/shard_map/ppermute | solution.py:47
  61.4 0.9 fusion.6
  62.4 1.0 fusion.4
  63.3 1.0 fusion.5
  64.3 0.9 convolution_bitcast_fusion.1
  65.2 0.9 convolution_bitcast_fusion.2
  66.2 0.9 convolution_bitcast_fusion.3
  67.1 2.1 %fusion.7 = f16[1,512,256]{2,1,0:T(8,128)(2,1)S(1)} fusion(bf16[1536,512]{1,0:T(8,128)(2,1)} %collective-permute-done.4, s32[]{:T(128)S(6)} %select_n.79, bf16[1536,512]{1,0:T(8,128)(2,1)S(1)} %constant_dynamic-update-slice_fusion.4, f32[1536]{0:T(1024)S(1)} %multiply_divide_fusion), kind=kOutput, calls=%fused_computation.30 | convolution fusion | flops 405143552 | bytes 2627588 | tf_op jit(solution)/shard_map/dot_general | solution.py:90
  69.6 2.3 %fusion.3 = f16[1,512,256]{2,1,0:T(8,128)(2,1)S(1)} fusion(bf16[1536,512]{1,0:T(8,128)(2,1)} %collective-permute-done.4, f32[1536]{0:T(1024)S(1)} %multiply_divide_fusion, bf16[1536,512]{1,0:T(8,128)(2,1)S(1)} %constant_dynamic-update-slice_fusion, s32[]{:T(128)S(6)} %select_n.79), kind=kOutput, calls=%fused_computation.26 | convolution fusion | flops 405143552 | bytes 2629636 | tf_op jit(solution)/shard_map/dot_general | solution.py:90
  71.9 2.1 %fusion.2 = f16[1,512,256]{2,1,0:T(8,128)(2,1)S(1)} fusion(bf16[1536,512]{1,0:T(8,128)(2,1)} %collective-permute-done.4, s32[]{:T(128)S(6)} %select_n.79, bf16[1536,512]{1,0:T(8,128)(2,1)S(1)} %copy-done.1, f32[1536]{0:T(1024)S(1)} %multiply_divide_fusion), kind=kOutput, calls=%fused_computation.25 | convolution fusion | flops 405143552 | bytes 2627588 | tf_op jit(solution)/shard_map/dot_general | solution.py:90
  74.4 0.8 collective-permute-start.5
  75.2 2.0 %convolution_bitcast_fusion = f32[1,512,256]{2,1,0:T(8,128)S(1)} fusion(bf16[1536,512]{1,0:T(8,128)(2,1)} %collective-permute-done.4, s32[]{:T(128)S(6)} %select_n.77, bf16[1536,512]{1,0:T(8,128)(2,1)S(1)} %constant_dynamic-update-slice_fusion.4, f32[1536]{0:T(1024)S(1)} %multiply_divide_fusion), kind=kOutput, calls=%fused_computation.7 | convolution fusion | flops 405012480 | bytes 2889732 | tf_op jit(solution)/shard_map/dot_general | solution.py:90
  77.4 2.5 %convolution_bitcast_fusion.4 = f32[1,512,256]{2,1,0:T(8,128)S(1)} fusion(bf16[1536,512]{1,0:T(8,128)(2,1)} %collective-permute-done.4, f32[1536]{0:T(1024)S(1)} %multiply_divide_fusion, bf16[1536,512]{1,0:T(8,128)(2,1)S(1)} %constant_dynamic-update-slice_fusion, s32[]{:T(128)S(6)} %select_n.77), kind=kOutput, calls=%fused_computation.11 | convolution fusion | flops 405012480 | bytes 2891780 | tf_op jit(solution)/shard_map/dot_general | solution.py:90
  79.9 2.0 %convolution_bitcast_fusion.5 = f32[1,512,256]{2,1,0:T(8,128)S(1)} fusion(bf16[1536,512]{1,0:T(8,128)(2,1)} %collective-permute-done.4, s32[]{:T(128)S(6)} %select_n.77, bf16[1536,512]{1,0:T(8,128)(2,1)S(1)} %copy-done.2, f32[1536]{0:T(1024)S(1)} %multiply_divide_fusion), kind=kOutput, calls=%fused_computation.12 | convolution fusion | flops 405012480 | bytes 2889732 | tf_op jit(solution)/shard_map/dot_general | solution.py:90
  82.0 0.9 fusion.27
  83.5 1.6 %collective-permute-start.15 = (f16[512,256]{1,0:T(8,128)(2,1)}, f16[512,256]{1,0:T(8,128)(2,1)}, u32[]{:S(2)}, u32[]{:S(2)}) collective-permute-start(f16[512,256]{1,0:T(8,128)(2,1)} %get-tuple-element.10), channel_id=1, source_target_pairs={{0,96},{8,104},{16,112},{24,120},{4,100},{12,108},{20,116},{28,124... | collective-permute-start | bytes 786440 | tf_op jit(solution)/shard_map/ppermute | solution.py:47
  85.1 1.4 %collective-permute-start.16 = (f16[512,256]{1,0:T(8,128)(2,1)S(1)}, f16[512,256]{1,0:T(8,128)(2,1)}, u32[]{:S(2)}, u32[]{:S(2)}) collective-permute-start(f16[512,256]{1,0:T(8,128)(2,1)S(1)} %get-tuple-element.9), channel_id=1, source_target_pairs={{0,64},{8,72},{16,80},{24,88},{4,68},{12,76},{20,84},{28,92},{1,65... | collective-permute-start | bytes 786440 | tf_op jit(solution)/shard_map/ppermute | solution.py:47
  86.6 1.2 fusion.24
  87.8 2.1 %collective-permute-start.6 = (f16[512,256]{1,0:T(8,128)(2,1)}, f16[512,256]{1,0:T(8,128)(2,1)}, u32[]{:S(2)}, u32[]{:S(2)}) collective-permute-start(f16[512,256]{1,0:T(8,128)(2,1)} %get-tuple-element.11), channel_id=1, source_target_pairs={{0,32},{8,40},{16,48},{24,56},{4,36},{12,44},{20,52},{28,60},{1,33... | collective-permute-start | bytes 786440 | tf_op jit(solution)/shard_map/ppermute | solution.py:47
  89.9 2.2 %collective-permute-done.14 = f16[512,256]{1,0:T(8,128)(2,1)} collective-permute-done((f16[512,256]{1,0:T(8,128)(2,1)S(1)}, f16[512,256]{1,0:T(8,128)(2,1)}, u32[]{:S(2)}, u32[]{:S(2)}) %collective-permute-start.14) | collective-permute-done | bytes 262176 | tf_op jit(solution)/shard_map/ppermute | solution.py:47
  92.2 5.4 %collective-permute-start.8 = (f16[512,256]{1,0:T(8,128)(2,1)}, f16[512,256]{1,0:T(8,128)(2,1)}, u32[]{:S(2)}, u32[]{:S(2)}) collective-permute-start(f16[512,256]{1,0:T(8,128)(2,1)} %get-tuple-element.12), channel_id=1, source_target_pairs={{0,64},{8,72},{16,80},{24,88},{4,68},{12,76},{20,84},{28,92},{1,65... | collective-permute-start | bytes 786440 | tf_op jit(solution)/shard_map/ppermute | solution.py:47
  102.0 1.4 %collective-permute-done.6 = f16[512,256]{1,0:T(8,128)(2,1)} collective-permute-done((f16[512,256]{1,0:T(8,128)(2,1)}, f16[512,256]{1,0:T(8,128)(2,1)}, u32[]{:S(2)}, u32[]{:S(2)}) %collective-permute-start.6) | collective-permute-done | bytes 262176 | tf_op jit(solution)/shard_map/ppermute | solution.py:47
  103.5 6.4 %collective-permute-done.7 = f16[512,256]{1,0:T(8,128)(2,1)} collective-permute-done((f16[512,256]{1,0:T(8,128)(2,1)}, f16[512,256]{1,0:T(8,128)(2,1)}, u32[]{:S(2)}, u32[]{:S(2)}) %collective-permute-start.7) | collective-permute-done | bytes 262176 | tf_op jit(solution)/shard_map/ppermute | solution.py:47
  109.9 1.9 %select_convert_fusion = (f16[512,256]{1,0:T(8,128)(2,1)S(1)}, f32[512,256]{1,0:T(8,128)S(1)}, f32[512,256]{1,0:T(8,128)S(1)}) fusion(pred[]{:T(512)} %bitcast, f16[512,256]{1,0:T(8,128)(2,1)} %collective-permute-done.8, f16[512,256]{1,0:T(8,128)(2,1)} %collective-permute-done.7, f16[512,256]{1,0:T(8,128)(2,1)} %collective-permute-done.6, ...), kind=kLoop, calls=%fused_computation.55 | loop fusion | flops 2359296 | bytes 4456457 | tf_op jit(solution)/shard_map/convert_element_type | solution.py:160
  111.8 0.8 collective-permute-start.17
  112.6 6.1 %collective-permute-done.17 = f16[512,256]{1,0:T(8,128)(2,1)S(1)} collective-permute-done((f16[512,256]{1,0:T(8,128)(2,1)S(1)}, f16[512,256]{1,0:T(8,128)(2,1)S(1)}, u32[]{:S(2)}, u32[]{:S(2)}) %collective-permute-start.17) | collective-permute-done | bytes 262176 | tf_op jit(solution)/shard_map/ppermute | solution.py:52
  118.9 1.9 %collective-permute-start.18 = (f16[512,256]{1,0:T(8,128)(2,1)S(1)}, f16[512,256]{1,0:T(8,128)(2,1)S(1)}, u32[]{:S(2)}, u32[]{:S(2)}) collective-permute-start(f16[512,256]{1,0:T(8,128)(2,1)S(1)} %add_convert_fusion), channel_id=1, source_target_pairs={{0,0},{8,8},{16,5},{24,13},{4,84},{12,92},{20,20},{28,28},{1,22},{... | collective-permute-start | bytes 786440 | tf_op jit(solution)/shard_map/ppermute | solution.py:66
  120.8 14.6 %collective-permute-done.18 = f16[512,256]{1,0:T(8,128)(2,1)S(1)} collective-permute-done((f16[512,256]{1,0:T(8,128)(2,1)S(1)}, f16[512,256]{1,0:T(8,128)(2,1)S(1)}, u32[]{:S(2)}, u32[]{:S(2)}) %collective-permute-start.18) | collective-permute-done | bytes 262176 | tf_op jit(solution)/shard_map/ppermute | solution.py:66
  135.4 0.8 convert_multiply_fusion
  (45 shorter events, 5.1 us)
Async XLA Ops:
  0.0 8.9 %copy-start.1 = (bf16[1536,512]{1,0:T(8,128)(2,1)S(1)}, bf16[1536,512]{1,0:T(8,128)(2,1)}, u32[]{:S(2)}) copy-start(bf16[1536,512]{1,0:T(8,128)(2,1)} %param.6) | copy-start | bytes 4718596
  0.0 6.5 %copy-start.6 = (s32[1536]{0:T(1024)S(1)}, s32[1536]{0:T(1024)}, u32[]{:S(2)}) copy-start(s32[1536]{0:T(1024)} %param.8) | copy-start | bytes 18436
  0.0 7.7 %copy-start.7 = (s32[1536]{0:T(1024)S(1)}, s32[1536]{0:T(1024)}, u32[]{:S(2)}) copy-start(s32[1536]{0:T(1024)} %param.7) | copy-start | bytes 18436
  0.0 67.1 %collective-permute-start.4 = (bf16[1536,512]{1,0:T(8,128)(2,1)}, bf16[1536,512]{1,0:T(8,128)(2,1)}, u32[]{:S(2)}, u32[]{:S(2)}) collective-permute-start(bf16[1536,512]{1,0:T(8,128)(2,1)} %param.6), channel_id=1, source_target_pairs={{0,1},{8,9},{16,17},{24,25},{4,5},{12,13},{20,21},{28,29},{1,2},{9... | collective-permute-start | bytes 4718600 | tf_op jit(solution)/shard_map/ppermute | solution.py:47
  1.8 22.9 %collective-permute-start = (bf16[384,512]{1,0:T(8,128)(2,1)S(1)}, bf16[384,512]{1,0:T(8,128)(2,1)}, u32[]{:S(2)}, u32[]{:S(2)}) collective-permute-start(bf16[384,512]{1,0:T(8,128)(2,1)S(1)} %get-tuple-element.17), channel_id=1, source_target_pairs={{0,3},{8,11},{16,19},{24,27},{4,7},{12,15},{20,23},{28,31},{1,0},{... | collective-permute-start | bytes 1179656 | tf_op jit(solution)/shard_map/ppermute | solution.py:47
  3.6 24.1 %collective-permute-start.1 = (bf16[384,512]{1,0:T(8,128)(2,1)S(1)}, bf16[384,512]{1,0:T(8,128)(2,1)}, u32[]{:S(2)}, u32[]{:S(2)}) collective-permute-start(bf16[384,512]{1,0:T(8,128)(2,1)S(1)} %get-tuple-element.16), channel_id=1, source_target_pairs={{0,3},{8,11},{16,19},{24,27},{4,7},{12,15},{20,23},{28,31},{1,0},{... | collective-permute-start | bytes 1179656 | tf_op jit(solution)/shard_map/ppermute | solution.py:47
  4.4 27.6 %collective-permute-start.2 = (bf16[384,512]{1,0:T(8,128)(2,1)S(1)}, bf16[384,512]{1,0:T(8,128)(2,1)}, u32[]{:S(2)}, u32[]{:S(2)}) collective-permute-start(bf16[384,512]{1,0:T(8,128)(2,1)S(1)} %get-tuple-element.15), channel_id=1, source_target_pairs={{0,3},{8,11},{16,19},{24,27},{4,7},{12,15},{20,23},{28,31},{1,0},{... | collective-permute-start | bytes 1179656 | tf_op jit(solution)/shard_map/ppermute | solution.py:47
  4.8 34.2 %collective-permute-start.3 = (bf16[384,512]{1,0:T(8,128)(2,1)S(1)}, bf16[384,512]{1,0:T(8,128)(2,1)S(1)}, u32[]{:S(2)}, u32[]{:S(2)}) collective-permute-start(bf16[384,512]{1,0:T(8,128)(2,1)S(1)} %get-tuple-element.14), channel_id=1, source_target_pairs={{0,3},{8,11},{16,19},{24,27},{4,7},{12,15},{20,23},{28,31},{1,0},{... | collective-permute-start | bytes 1179656 | tf_op jit(solution)/shard_map/ppermute | solution.py:47
  24.7 19.9 %collective-permute-start.9 = (bf16[384,512]{1,0:T(8,128)(2,1)}, bf16[384,512]{1,0:T(8,128)(2,1)S(1)}, u32[]{:S(2)}, u32[]{:S(2)}) collective-permute-start(bf16[384,512]{1,0:T(8,128)(2,1)} %collective-permute-done), channel_id=1, source_target_pairs={{0,4},{8,12},{16,20},{24,28},{4,0},{12,8},{20,16},{28,24},{1,5},{9... | collective-permute-start | bytes 1179656 | tf_op jit(solution)/shard_map/ppermute | solution.py:47
  27.8 18.0 %collective-permute-start.10 = (bf16[384,512]{1,0:T(8,128)(2,1)}, bf16[384,512]{1,0:T(8,128)(2,1)S(1)}, u32[]{:S(2)}, u32[]{:S(2)}) collective-permute-start(bf16[384,512]{1,0:T(8,128)(2,1)} %collective-permute-done.1), channel_id=1, source_target_pairs={{0,4},{8,12},{16,20},{24,28},{4,0},{12,8},{20,16},{28,24},{1,5},{9... | collective-permute-start | bytes 1179656 | tf_op jit(solution)/shard_map/ppermute | solution.py:47
  40.0 14.2 %collective-permute-start.11 = (bf16[384,512]{1,0:T(8,128)(2,1)}, bf16[384,512]{1,0:T(8,128)(2,1)S(1)}, u32[]{:S(2)}, u32[]{:S(2)}) collective-permute-start(bf16[384,512]{1,0:T(8,128)(2,1)} %collective-permute-done.2), channel_id=1, source_target_pairs={{0,4},{8,12},{16,20},{24,28},{4,0},{12,8},{20,16},{28,24},{1,5},{9... | collective-permute-start | bytes 1179656 | tf_op jit(solution)/shard_map/ppermute | solution.py:47
  43.1 18.3 %collective-permute-start.12 = (bf16[384,512]{1,0:T(8,128)(2,1)S(1)}, bf16[384,512]{1,0:T(8,128)(2,1)S(1)}, u32[]{:S(2)}, u32[]{:S(2)}) collective-permute-start(bf16[384,512]{1,0:T(8,128)(2,1)S(1)} %collective-permute-done.3), channel_id=1, source_target_pairs={{0,4},{8,12},{16,20},{24,28},{4,0},{12,8},{20,16},{28,24},{1,5},{9... | collective-permute-start | bytes 1179656 | tf_op jit(solution)/shard_map/ppermute | solution.py:47
  69.5 12.5 %collective-permute-start.13 = (f16[4,512,256]{2,1,0:T(8,128)(2,1)S(1)}, f16[4,512,256]{2,1,0:T(8,128)(2,1)S(1)}, u32[]{:S(2)}, u32[]{:S(2)}) collective-permute-start(f16[4,512,256]{2,1,0:T(8,128)(2,1)S(1)} %pad_maximum_fusion.3), channel_id=1, source_target_pairs={{0,8},{8,0},{16,24},{24,16},{4,12},{12,4},{20,28},{28,20},{1,9},{9... | collective-permute-start | bytes 3145736 | tf_op jit(solution)/shard_map/ppermute | solution.py:47
  71.9 2.1 %copy-start.5 = (f16[1,512,256]{2,1,0:T(8,128)(2,1)S(1)}, f16[1,512,256]{2,1,0:T(8,128)(2,1)}, u32[]{:S(2)}) copy-start(f16[1,512,256]{2,1,0:T(8,128)(2,1)} %fusion) | copy-start | bytes 786436
  74.4 12.2 %collective-permute-start.5 = (f16[4,512,256]{2,1,0:T(8,128)(2,1)S(1)}, f16[4,512,256]{2,1,0:T(8,128)(2,1)S(1)}, u32[]{:S(2)}, u32[]{:S(2)}) collective-permute-start(f16[4,512,256]{2,1,0:T(8,128)(2,1)S(1)} %pad_maximum_fusion.2), channel_id=1, source_target_pairs={{0,8},{8,0},{16,24},{24,16},{4,12},{12,4},{20,28},{28,20},{1,9},{9... | collective-permute-start | bytes 3145736 | tf_op jit(solution)/shard_map/ppermute | solution.py:47
  77.4 2.5 %copy-start.2 = (bf16[1536,512]{1,0:T(8,128)(2,1)S(1)}, bf16[1536,512]{1,0:T(8,128)(2,1)}, u32[]{:S(2)}) copy-start(bf16[1536,512]{1,0:T(8,128)(2,1)} %param.6) | copy-start | bytes 4718596
  81.9 1.4 %copy-start.4 = (f32[1,512,256]{2,1,0:T(8,128)S(1)}, f32[1,512,256]{2,1,0:T(8,128)}, u32[]{:S(2)}) copy-start(f32[1,512,256]{2,1,0:T(8,128)} %convolution_bitcast_fusion.7) | copy-start | bytes 1572868
  82.9 9.3 %collective-permute-start.14 = (f16[512,256]{1,0:T(8,128)(2,1)S(1)}, f16[512,256]{1,0:T(8,128)(2,1)}, u32[]{:S(2)}, u32[]{:S(2)}) collective-permute-start(f16[512,256]{1,0:T(8,128)(2,1)S(1)} %get-tuple-element.8), channel_id=1, source_target_pairs={{0,32},{8,40},{16,48},{24,56},{4,36},{12,44},{20,52},{28,60},{1,33... | collective-permute-start | bytes 786440 | tf_op jit(solution)/shard_map/ppermute | solution.py:47
  83.5 4.3 %copy-start = (f32[4,512,256]{2,1,0:T(8,128)}, f32[4,512,256]{2,1,0:T(8,128)S(1)}, u32[]{:S(2)}) copy-start(f32[4,512,256]{2,1,0:T(8,128)S(1)} %pad_maximum_fusion) | copy-start | bytes 6291460
  83.5 18.5 %collective-permute-start.15 = (f16[512,256]{1,0:T(8,128)(2,1)}, f16[512,256]{1,0:T(8,128)(2,1)}, u32[]{:S(2)}, u32[]{:S(2)}) collective-permute-start(f16[512,256]{1,0:T(8,128)(2,1)} %get-tuple-element.10), channel_id=1, source_target_pairs={{0,96},{8,104},{16,112},{24,120},{4,100},{12,108},{20,116},{28,124... | collective-permute-start | bytes 786440 | tf_op jit(solution)/shard_map/ppermute | solution.py:47
  85.1 16.9 %collective-permute-start.16 = (f16[512,256]{1,0:T(8,128)(2,1)S(1)}, f16[512,256]{1,0:T(8,128)(2,1)}, u32[]{:S(2)}, u32[]{:S(2)}) collective-permute-start(f16[512,256]{1,0:T(8,128)(2,1)S(1)} %get-tuple-element.9), channel_id=1, source_target_pairs={{0,64},{8,72},{16,80},{24,88},{4,68},{12,76},{20,84},{28,92},{1,65... | collective-permute-start | bytes 786440 | tf_op jit(solution)/shard_map/ppermute | solution.py:47
  86.6 1.3 copy-start.3
  87.8 15.6 %collective-permute-start.6 = (f16[512,256]{1,0:T(8,128)(2,1)}, f16[512,256]{1,0:T(8,128)(2,1)}, u32[]{:S(2)}, u32[]{:S(2)}) collective-permute-start(f16[512,256]{1,0:T(8,128)(2,1)} %get-tuple-element.11), channel_id=1, source_target_pairs={{0,32},{8,40},{16,48},{24,56},{4,36},{12,44},{20,52},{28,60},{1,33... | collective-permute-start | bytes 786440 | tf_op jit(solution)/shard_map/ppermute | solution.py:47
  89.9 19.9 %collective-permute-start.7 = (f16[512,256]{1,0:T(8,128)(2,1)}, f16[512,256]{1,0:T(8,128)(2,1)}, u32[]{:S(2)}, u32[]{:S(2)}) collective-permute-start(f16[512,256]{1,0:T(8,128)(2,1)} %get-tuple-element.13), channel_id=1, source_target_pairs={{0,96},{8,104},{16,112},{24,120},{4,100},{12,108},{20,116},{28,124... | collective-permute-start | bytes 786440 | tf_op jit(solution)/shard_map/ppermute | solution.py:47
  92.2 17.7 %collective-permute-start.8 = (f16[512,256]{1,0:T(8,128)(2,1)}, f16[512,256]{1,0:T(8,128)(2,1)}, u32[]{:S(2)}, u32[]{:S(2)}) collective-permute-start(f16[512,256]{1,0:T(8,128)(2,1)} %get-tuple-element.12), channel_id=1, source_target_pairs={{0,64},{8,72},{16,80},{24,88},{4,68},{12,76},{20,84},{28,92},{1,65... | collective-permute-start | bytes 786440 | tf_op jit(solution)/shard_map/ppermute | solution.py:47
  111.8 7.0 %collective-permute-start.17 = (f16[512,256]{1,0:T(8,128)(2,1)S(1)}, f16[512,256]{1,0:T(8,128)(2,1)S(1)}, u32[]{:S(2)}, u32[]{:S(2)}) collective-permute-start(f16[512,256]{1,0:T(8,128)(2,1)S(1)} %get-tuple-element.5), channel_id=1, source_target_pairs={{0,16},{8,24},{16,0},{24,8},{4,20},{12,28},{20,4},{28,12},{1,17},{... | collective-permute-start | bytes 786440 | tf_op jit(solution)/shard_map/ppermute | solution.py:52
  118.9 16.5 %collective-permute-start.18 = (f16[512,256]{1,0:T(8,128)(2,1)S(1)}, f16[512,256]{1,0:T(8,128)(2,1)S(1)}, u32[]{:S(2)}, u32[]{:S(2)}) collective-permute-start(f16[512,256]{1,0:T(8,128)(2,1)S(1)} %add_convert_fusion), channel_id=1, source_target_pairs={{0,0},{8,8},{16,5},{24,13},{4,84},{12,92},{20,20},{28,28},{1,22},{... | collective-permute-start | bytes 786440 | tf_op jit(solution)/shard_map/ppermute | solution.py:66
where the time goes:
time: 137 us; the launch traced here: 136 us
  waiting for transfers between devices  55.2 us (40%)
  starting transfers between devices  26.9 us (20%)
  matrix products  23.8 us (17%)
  between operations  15.9 us (12%)
  other arithmetic  8.31 us (6%)
  local copies, waits for them, and re-layouts  6.12 us (4%)
    ppermute x17, waiting for transfers between devices, shift(): return lax.ppermute(value, AXES, pairs)  34.5 us
    ppermute x17, starting transfers between devices, shift(): return lax.ppermute(value, AXES, pairs)  24.2 us
    dot_general x16, matrix products, product(): lax.dot_general(left, right, (((0,), (0,)), ((), ())), preferred_element_...  23.8 us
    ppermute x1, waiting for transfers between devices, to_owner(): return lax.ppermute(value, AXES, pairs)  14.6 us
    ppermute x1, waiting for transfers between devices, swap_z_lo(): return lax.ppermute(value, AXES, pairs)  6.13 us
    unnamed x22, local copies, waits for them, and re-layouts  3.25 us
  transfers between devices with their start and end apart: 19, of which 10 were waited for; matrix products, arithmetic and copies ran while one was open for 24% of the time, Pallas kernels for 0%

commit v1 on v0

v1 whole, which is shorter than its diff:
```python
import math

import jax
import jax.numpy as jnp
import numpy as np
from jax import lax
from jax.experimental import pallas as pl
from jax.experimental.pallas import tpu as pltpu
from jax.sharding import PartitionSpec as P


AXES = ("pair", "ga")
CUTS = (384,) * 4
GAIN = 4.0

O, N, S, Z = (0, 0), (1, 0), (3, 0), (1, 1)
EARLY = ((O, O), (O, N), (O, S), (S, N))
LATE = ((O, Z), (Z, O), (Z, N), (S, Z))
PLAN = (
    ((3, 0, 2, 1), (1, 0, 3, 2), (0, 0, 1, 1)),
    ((2, 3, 1, 0), (1, 2, 3, 0), (1, 0, 0, 1)),
    ((1, 0, 3, 2), (3, 1, 2, 0), (0, 0, 1, 1)),
    ((1, 2, 0, 3), (2, 1, 3, 0), (0, 0, 1, 0)),
    ((2, 3, 1, 0), (0, 1, 2, 3), (0, 0, 1, 0)),
    ((1, 2, 0, 3), (3, 0, 1, 2), (1, 1, 1, 0)),
    ((1, 0, 2, 3), (0, 3, 1, 2), (1, 0, 0, 1)),
    ((0, 3, 1, 2), (0, 3, 2, 1), (1, 1, 0, 1)),
)


def index(x, y, z, core):
    x, y, z = x % 4, y % 4, z % 4
    return (4 * x + 2 * (z % 2) + core) * 8 + 4 * (z // 2) + y


def devices():
    for x in range(4):
        for y in range(4):
            for z in range(4):
                for core in range(2):
                    yield x, y, z, core


def shift(value, dx=0, dy=0, dz=0, swap=False):
    pairs = [
        (index(x, y, z, c), index(x + dx, y + dy, z + dz, 1 - c if swap else c))
        for x, y, z, c in devices()
    ]
    return lax.ppermute(value, AXES, pairs)


def swap_z_lo(value):
    pairs = [(index(x, y, z, c), index(x, y, z ^ 1, c)) for x, y, z, c in devices()]
    return lax.ppermute(value, AXES, pairs)


def to_owner(value):
    pairs = []
    for x, y, z, c in devices():
        early, late, keeper = PLAN[4 * (z // 2) + y]
        keeps = keeper[x] == z % 2
        row, col = EARLY[early[x]] if keeps else LATE[late[x]]
        row_y, row_hi = (y + row[0]) % 4, (z // 2 + row[1]) % 2
        block = 4 * ((z // 2 + col[1]) % 2) + (y + col[0]) % 4
        pairs.append(
            (index(x, y, z, c), index(block // 2, row_y, 2 * row_hi + block % 2, c))
        )
    return lax.ppermute(value, AXES, pairs)


def planned(pair, ga):
    x, z_lo = pair >> 2, (pair >> 1) & 1
    word = jnp.int32(0)
    for k, (early, late, keeper) in enumerate(PLAN):
        code = sum(v << 2 * i for i, v in enumerate(early + late))
        code += sum(v << 16 + i for i, v in enumerate(keeper))
        word = jnp.where(ga == k, code, word)

    def entry(d, base):
        return (word >> (2 * ((x + d) & 3) + base)) & 3

    early, late = ([entry(d, base) for d in range(4)] for base in (0, 8))
    return early, late, ((word >> (16 + x)) & 1) == z_lo


def lookup(bands, energy):
    levels = lax.broadcasted_iota(jnp.int32, (1, energy.shape[0]), 1)
    onehot = (bands[:, None] == levels).astype(jnp.float32)
    return jnp.sum(onehot * energy[None, :], axis=1)


def placing(which):
    return [sum(jnp.where(w == s, d, 0) for d, w in enumerate(which)) for s in range(4)]


def chunk(k):
    return slice(sum(CUTS[:k]), sum(CUTS[: k + 1]))


def fetch(sources, targets, sems):
    copies = [
        pltpu.make_async_copy(s, t, sems.at[i])
        for i, (s, t) in enumerate(zip(sources, targets))
    ]
    for copy in copies:
        copy.start()
    return copies


def matmul(left, right):
    return jnp.dot(left, right, preferred_element_type=jnp.float32)


def put(total, at, core, theirs, mine):
    low, high = total[:, : total.shape[1] // 2], total[:, total.shape[1] // 2 :]
    theirs[at] = jnp.where(core == 0, high, low)
    mine[at] = jnp.where(core == 0, low, high)


def scaled_transpose(weight, block):
    return (weight * block.astype(jnp.float32)).astype(jnp.bfloat16).T


COUNT = len(CUTS)


def early_kernel(*refs):
    sources, refs = refs[: 2 * COUNT + 3], refs[2 * COUNT + 3 :]
    theirs, mine, south_t = refs[:3]
    held, sems = refs[3:-1], refs[-1]
    copies = fetch(sources, held, sems)
    weight, own_t, own = held[:3]
    north, south = held[3 : 3 + COUNT], held[3 + COUNT :]
    pair, ga = lax.axis_index("pair"), lax.axis_index("ga")
    core, at = pair & 1, placing(planned(pair, ga)[0])
    for copy in copies[:3]:
        copy.wait()
    put(matmul(own_t[...], own[...]), at[0], core, theirs, mine)
    for copy in copies[3 : 3 + COUNT]:
        copy.wait()
    total = sum(matmul(own_t[:, chunk(k)], north[k][...]) for k in range(COUNT))
    put(total, at[1], core, theirs, mine)
    for copy in copies[3 + COUNT :]:
        copy.wait()
    total = sum(matmul(own_t[:, chunk(k)], south[k][...]) for k in range(COUNT))
    put(total, at[2], core, theirs, mine)
    for k in range(COUNT):
        south_t[:, chunk(k)] = scaled_transpose(weight[chunk(k), :], south[k][...])
    total = sum(matmul(south_t[:, chunk(k)], north[k][...]) for k in range(COUNT))
    put(total, at[3], core, theirs, mine)


def late_kernel(*refs):
    sources, refs = refs[: 2 * COUNT + 4], refs[2 * COUNT + 4 :]
    theirs, mine = refs[:2]
    held, far_t, sems = refs[2:-2], refs[-2], refs[-1]
    copies = fetch(sources, held, sems)
    weight, own_t, own, south_t = held[:4]
    north, far = held[4 : 4 + COUNT], held[4 + COUNT :]
    pair, ga = lax.axis_index("pair"), lax.axis_index("ga")
    core, at = pair & 1, placing(planned(pair, ga)[1])
    for copy in copies:
        copy.wait()
    total = sum(matmul(own_t[:, chunk(k)], far[k][...]) for k in range(COUNT))
    put(total, at[0], core, theirs, mine)
    for k in range(COUNT):
        far_t[:, chunk(k)] = scaled_transpose(weight[chunk(k), :], far[k][...])
    put(matmul(far_t[...], own[...]), at[1], core, theirs, mine)
    total = sum(matmul(far_t[:, chunk(k)], north[k][...]) for k in range(COUNT))
    put(total, at[2], core, theirs, mine)
    total = sum(matmul(south_t[:, chunk(k)], far[k][...]) for k in range(COUNT))
    put(total, at[3], core, theirs, mine)


def run_kernel(kernel, sources, outs, scratch):
    held = [pltpu.VMEM(s.shape, s.dtype) for s in sources]
    wide = sources[1].shape
    return pl.pallas_call(
        kernel,
        out_shape=outs,
        in_specs=[pl.BlockSpec(memory_space=pl.ANY)] * len(sources),
        out_specs=[pl.BlockSpec(memory_space=pltpu.VMEM)] * len(outs),
        scratch_shapes=[*held, *scratch, pltpu.SemaphoreType.DMA((len(sources),))],
        compiler_params=pltpu.CompilerParams(vmem_limit_bytes=32 * 2**20),
        cost_estimate=pl.CostEstimate(
            flops=8 * wide[0] * wide[0] * wide[1], bytes_accessed=2**23, transcendentals=0
        ),
    )(*sources)


def body(own, val_band, cond_band, val_energy, cond_energy):
    pairs_total = own.shape[0] * lax.axis_size("pair")
    pair, ga = lax.axis_index("pair"), lax.axis_index("ga")
    starts = np.cumsum((0,) + CUTS)

    def rows(block, k):
        return block[starts[k] : starts[k + 1]]

    norths, souths, farther = [], [], []
    first = rows(own, 0)
    rest = lax.optimization_barrier((own, first))[0]
    for k in range(len(CUTS)):
        piece = rows(rest, k) if k else first
        norths.append(shift(piece, dy=-1))
        souths.append(shift(piece, dy=1))
        farther.append(shift(norths[k], dz=2))

    gap = lookup(val_band, val_energy) - lookup(cond_band, cond_energy)
    weight = (4.0 * GAIN) / (gap * math.sqrt(pairs_total))

    size = own.shape[1]
    half = jax.ShapeDtypeStruct((4, size, size // 2), jnp.float32)
    flipped = jax.ShapeDtypeStruct(own.shape[::-1], own.dtype)

    def over_x(theirs, mine):
        theirs = shift(theirs.astype(jnp.float16), swap=True)

        def joined(d):
            return mine[d] + theirs[d].astype(jnp.float32)

        got, sent = [], [joined(d).astype(jnp.float16) for d in (1, 3, 2)]
        for d, value in zip((1, 3, 2), sent):
            got.append(shift(value, dx=d))
        return joined(0), got, sent

    column = weight[:, None]
    own_t = (column * own.astype(jnp.float32)).astype(jnp.bfloat16).T
    column, own_t = lax.optimization_barrier((column, own_t))

    *products, south_t = run_kernel(
        early_kernel,
        [column, own_t, own, *norths, *souths],
        [half, half, flipped],
        [],
    )
    early, early_got, _ = over_x(*products)

    products = run_kernel(
        late_kernel,
        [column, own_t, own, south_t, *norths, *farther],
        [half, half],
        [pltpu.VMEM(flipped.shape, flipped.dtype)],
    )
    late, late_got, _ = over_x(*products)

    early = early + sum(g.astype(jnp.float32) for g in early_got)
    early = lax.optimization_barrier(early)
    late = late + sum(g.astype(jnp.float32) for g in late_got)
    keeps = planned(pair, ga)[2]
    kept = jnp.where(keeps, early, late)
    got = swap_z_lo(jnp.where(keeps, late, early).astype(jnp.float16))
    total = kept + got.astype(jnp.float32)
    total = to_owner(total.astype(jnp.float16))
    return total.astype(jnp.float32) * (1.0 / GAIN)


def solution(mesh):
    placed = (P("pair", "ga"), P("pair"), P("pair"), P(), P())
    return jax.shard_map(
        body, mesh=mesh, in_specs=placed, out_specs=P("ga", "pair"), check_vma=False
    )
```

time: 137 us -> 138 us (level)
  the two profiles are of different devices: /device:TPU:62 before, /device:TPU:5 now
where the time goes in v1:
time: 138 us; the launch traced here: 137 us
  waiting for transfers between devices  65.2 us (47%)
  starting transfers between devices  36.9 us (27%)
  Pallas kernels  12.4 us (9%)
  other arithmetic  11.5 us (8%)
  local copies, waits for them, and re-layouts  10.7 us (8%)
    ppermute x20, waiting for transfers between devices, shift(): return lax.ppermute(value, AXES, pairs)  51.4 us
    ppermute x20, starting transfers between devices, shift(): return lax.ppermute(value, AXES, pairs)  29.7 us
    pallas_call x2, Pallas kernels, run_kernel(): pl.pallas_call(kernel, out_shape=outs, in_specs=[pl.BlockSpec(memory_spac...  12.4 us
    ppermute x1, waiting for transfers between devices, to_owner(): return lax.ppermute(value, AXES, pairs)  7.44 us
    ppermute x1, waiting for transfers between devices, swap_z_lo(): return lax.ppermute(value, AXES, pairs)  6.36 us
    unnamed x25, local copies, waits for them, and re-layouts  6.35 us
    ppermute x1, starting transfers between devices, to_owner(): return lax.ppermute(value, AXES, pairs)  6.15 us
    slice x2, local copies, waits for them, and re-layouts, rows(): return block[starts[k]:starts[k + 1]]  4.08 us
  transfers between devices with their start and end apart: 22, of which 14 were waited for; matrix products, arithmetic and copies ran while one was open for 11% of the time, Pallas kernels for 9%

profile of v1, /device:TPU:5, one launch (start us, length us, event | category | flops | bytes accessed | tf_op | source)
XLA Modules:
  0.0 136.8 jit_solution(15125043281486593146)
XLA Ops:
  0.0 1.9 %slice.60 = bf16[384,512]{1,0:T(8,128)(2,1)} slice(bf16[1536,512]{1,0:T(8,128)(2,1)} %refs_2_.3), slice={[0:384], [0:512]} | slice | bytes 786432 | tf_op jit(solution)/shard_map/slice | solution.py:197
  1.9 2.7 %collective-permute-start = (bf16[384,512]{1,0:T(8,128)(2,1)}, bf16[384,512]{1,0:T(8,128)(2,1)S(1)}, u32[]{:S(2)}, u32[]{:S(2)}) collective-permute-start(bf16[384,512]{1,0:T(8,128)(2,1)} %slice.60), channel_id=1, source_target_pairs={{0,3},{8,11},{16,19},{24,27},{4,7},{12,15},{20,23},{28,31},{1,0},{... | collective-permute-start | bytes 1179656 | tf_op jit(solution)/shard_map/ppermute | solution.py:49
  4.6 2.2 %fusion.7 = (bf16[384,512]{1,0:T(8,128)(2,1)S(1)}, bf16[384,512]{1,0:T(8,128)(2,1)}, bf16[384,512]{1,0:T(8,128)(2,1)}) fusion(bf16[1536,512]{1,0:T(8,128)(2,1)} %refs_2_.3), kind=kLoop, calls=%fused_computation.24 | loop fusion | bytes 2359296 | tf_op jit(solution)/shard_map/slice | solution.py:197
  6.8 0.5 collective-permute-start.1
  7.3 1.0 collective-permute-start.4
  8.3 2.7 %collective-permute-start.2 = (bf16[384,512]{1,0:T(8,128)(2,1)}, bf16[384,512]{1,0:T(8,128)(2,1)}, u32[]{:S(2)}, u32[]{:S(2)}) collective-permute-start(bf16[384,512]{1,0:T(8,128)(2,1)} %get-tuple-element.28), channel_id=1, source_target_pairs={{0,3},{8,11},{16,19},{24,27},{4,7},{12,15},{20,23},{28,31},{1,0},{... | collective-permute-start | bytes 1179656 | tf_op jit(solution)/shard_map/ppermute | solution.py:49
  11.0 1.8 %collective-permute-done.refs_3_.refs_4_ = bf16[384,512]{1,0:T(8,128)(2,1)S(1)} collective-permute-done((bf16[384,512]{1,0:T(8,128)(2,1)}, bf16[384,512]{1,0:T(8,128)(2,1)S(1)}, u32[]{:S(2)}, u32[]{:S(2)}) %collective-permute-start) | collective-permute-done | bytes 393248 | tf_op jit(solution)/shard_map/ppermute | solution.py:49
  12.7 0.7 collective-permute-start.6
  13.4 7.8 %collective-permute-done.1.refs_4_.refs_5_ = bf16[384,512]{1,0:T(8,128)(2,1)S(1)} collective-permute-done((bf16[384,512]{1,0:T(8,128)(2,1)}, bf16[384,512]{1,0:T(8,128)(2,1)S(1)}, u32[]{:S(2)}, u32[]{:S(2)}) %collective-permute-start.1) | collective-permute-done | bytes 393248 | tf_op jit(solution)/shard_map/ppermute | solution.py:49
  21.2 3.3 %collective-permute-start.3 = (bf16[384,512]{1,0:T(8,128)(2,1)S(1)}, bf16[384,512]{1,0:T(8,128)(2,1)}, u32[]{:S(2)}, u32[]{:S(2)}) collective-permute-start(bf16[384,512]{1,0:T(8,128)(2,1)S(1)} %get-tuple-element.27), channel_id=1, source_target_pairs={{0,3},{8,11},{16,19},{24,27},{4,7},{12,15},{20,23},{28,31},{1,0},{... | collective-permute-start | bytes 1179656 | tf_op jit(solution)/shard_map/ppermute | solution.py:49
  24.5 0.5 select_reduce_fusion.1
  25.0 1.6 %copy.10 = bf16[1536,512]{0,1:T(8,128)(2,1)} copy(bf16[1536,512]{1,0:T(8,128)(2,1)S(1)} %copy-done) | data formatting | bytes 3145728 | tf_op args[0]
  26.6 1.2 select_reduce_fusion
  27.8 1.8 %collective-permute-done.2.refs_5_.refs_6_ = bf16[384,512]{1,0:T(8,128)(2,1)} collective-permute-done((bf16[384,512]{1,0:T(8,128)(2,1)}, bf16[384,512]{1,0:T(8,128)(2,1)}, u32[]{:S(2)}, u32[]{:S(2)}) %collective-permute-start.2) | collective-permute-done | bytes 393248 | tf_op jit(solution)/shard_map/ppermute | solution.py:49
  29.6 0.8 collective-permute-start.7
  30.4 7.6 %collective-permute-done.3.refs_6_.refs_7_ = bf16[384,512]{1,0:T(8,128)(2,1)} collective-permute-done((bf16[384,512]{1,0:T(8,128)(2,1)S(1)}, bf16[384,512]{1,0:T(8,128)(2,1)}, u32[]{:S(2)}, u32[]{:S(2)}) %collective-permute-start.3) | collective-permute-done | bytes 393248 | tf_op jit(solution)/shard_map/ppermute | solution.py:49
  37.9 3.6 %collective-permute-start.12 = (bf16[384,512]{1,0:T(8,128)(2,1)S(1)}, bf16[384,512]{1,0:T(8,128)(2,1)}, u32[]{:S(2)}, u32[]{:S(2)}) collective-permute-start(bf16[384,512]{1,0:T(8,128)(2,1)S(1)} %collective-permute-done.refs_3_.refs_4_), channel_id=1, source_target_pairs={{0,4},{8,12},{16,20},{24,28},{4,0},{12,8},{20,16},{28,24},{1,5},{9... | collective-permute-start | bytes 1179656 | tf_op jit(solution)/shard_map/ppermute | solution.py:49
  41.6 2.9 %collective-permute-start.14 = (bf16[384,512]{1,0:T(8,128)(2,1)}, bf16[384,512]{1,0:T(8,128)(2,1)}, u32[]{:S(2)}, u32[]{:S(2)}) collective-permute-start(bf16[384,512]{1,0:T(8,128)(2,1)} %collective-permute-done.2.refs_5_.refs_6_), channel_id=1, source_target_pairs={{0,4},{8,12},{16,20},{24,28},{4,0},{12,8},{20,16},{28,24},{1,5},{9... | collective-permute-start | bytes 1179656 | tf_op jit(solution)/shard_map/ppermute | solution.py:49
  44.6 2.9 %fusion.refs_1_ = bf16[512,1536]{1,0:T(8,128)(2,1)} fusion(bf16[1536,512]{0,1:T(8,128)(2,1)} %copy.10, f32[1536]{0:T(1024)S(1)} %multiply_divide_fusion), kind=kLoop, calls=%fused_computation.1 | loop fusion | flops 2359296 | bytes 3151872 | tf_op jit(solution)/shard_map/transpose | solution.py:227
  47.8 1.4 %copy-done.4 = bf16[512,1536]{1,0:T(8,128)(2,1)S(1)} copy-done((bf16[512,1536]{1,0:T(8,128)(2,1)S(1)}, bf16[512,1536]{1,0:T(8,128)(2,1)}, u32[]{:S(2)}) %copy-start.4) | copy-done | bytes 1572888
  49.2 1.0 copy-done.6
  50.2 1.0 copy-done.8
  51.2 5.7 %shard_map.55 = (f32[4,512,256]{2,1,0:T(8,128)S(1)}, f32[4,512,256]{2,1,0:T(8,128)S(1)}, bf16[512,1536]{1,0:T(8,128)(2,1)S(1)}) custom-call(f32[1536,1]{1,0:T(8,128)S(1)} %copy.11.refs_0_, bf16[512,1536]{1,0:T(8,128)(2,1)S(1)} %copy-done.4, bf16[1536,512]{1,0:T(8,128)(2,1)S(1)} %copy-done, bf16[384,512]{1,0:T(8,128)(2,1)S(1)} %collective-permute-done.refs_3_.refs_4_, ...), custom_call_target="tpu_custom_call" | custom-call | flops 3221225472 | bytes 8388608 | tf_op jit(solution)/shard_map/pallas_call | solution.py:178
  56.9 1.3 convert_element_type.114
  58.2 2.4 %collective-permute-start.8 = (f16[4,512,256]{2,1,0:T(8,128)(2,1)}, f16[4,512,256]{2,1,0:T(8,128)(2,1)}, u32[]{:S(2)}, u32[]{:S(2)}) collective-permute-start(f16[4,512,256]{2,1,0:T(8,128)(2,1)} %convert_element_type.114), channel_id=1, source_target_pairs={{0,8},{8,0},{16,24},{24,16},{4,12},{12,4},{20,28},{28,20},{1,9},{9... | collective-permute-start | bytes 3145736 | tf_op jit(solution)/shard_map/ppermute | solution.py:49
  60.6 5.8 %collective-permute-done.14.refs_10_ = bf16[384,512]{1,0:T(8,128)(2,1)} collective-permute-done((bf16[384,512]{1,0:T(8,128)(2,1)}, bf16[384,512]{1,0:T(8,128)(2,1)}, u32[]{:S(2)}, u32[]{:S(2)}) %collective-permute-start.14) | collective-permute-done | bytes 393248 | tf_op jit(solution)/shard_map/ppermute | solution.py:49
  66.4 8.4 %collective-permute-done.15.refs_11_ = bf16[384,512]{1,0:T(8,128)(2,1)} collective-permute-done((bf16[384,512]{1,0:T(8,128)(2,1)}, bf16[384,512]{1,0:T(8,128)(2,1)}, u32[]{:S(2)}, u32[]{:S(2)}) %collective-permute-start.15) | collective-permute-done | bytes 393248 | tf_op jit(solution)/shard_map/ppermute | solution.py:49
  74.9 6.7 %shard_map.56 = (f32[4,512,256]{2,1,0:T(8,128)S(1)}, f32[4,512,256]{2,1,0:T(8,128)S(1)}) custom-call(f32[1536,1]{1,0:T(8,128)S(1)} %copy.11.refs_0_, bf16[512,1536]{1,0:T(8,128)(2,1)S(1)} %copy-done.4, bf16[1536,512]{1,0:T(8,128)(2,1)S(1)} %copy-done, bf16[512,1536]{1,0:T(8,128)(2,1)S(1)} %get-tuple-element.18.refs_3_, ...), custom_call_target="tpu_custom_call" | custom-call | flops 3221225472 | bytes 8388608 | tf_op jit(solution)/shard_map/pallas_call | solution.py:178
  81.5 1.3 copy-done.1
  82.8 1.1 convert_element_type.128
  84.0 2.1 %collective-permute-start.16 = (f16[4,512,256]{2,1,0:T(8,128)(2,1)}, f16[4,512,256]{2,1,0:T(8,128)(2,1)S(1)}, u32[]{:S(2)}, u32[]{:S(2)}) collective-permute-start(f16[4,512,256]{2,1,0:T(8,128)(2,1)} %convert_element_type.128), channel_id=1, source_target_pairs={{0,8},{8,0},{16,24},{24,16},{4,12},{12,4},{20,28},{28,20},{1,9},{9... | collective-permute-start | bytes 3145736 | tf_op jit(solution)/shard_map/ppermute | solution.py:49
  86.1 1.8 %fusion.1 = (f16[512,256]{1,0:T(8,128)(2,1)S(1)}, f16[512,256]{1,0:T(8,128)(2,1)S(1)}, f16[512,256]{1,0:T(8,128)(2,1)S(1)}) fusion(f32[4,512,256]{2,1,0:T(8,128)} %copy-done.3, f16[4,512,256]{2,1,0:T(8,128)(2,1)} %collective-permute-done.8), kind=kLoop, calls=%fused_computation.17 | loop fusion | flops 1179648 | bytes 3145728 | tf_op jit(solution)/shard_map/convert_element_type | solution.py:221
  88.2 1.9 %collective-permute-start.10 = (f16[512,256]{1,0:T(8,128)(2,1)S(1)}, f16[512,256]{1,0:T(8,128)(2,1)S(1)}, u32[]{:S(2)}, u32[]{:S(2)}) collective-permute-start(f16[512,256]{1,0:T(8,128)(2,1)S(1)} %get-tuple-element.26), channel_id=1, source_target_pairs={{0,96},{8,104},{16,112},{24,120},{4,100},{12,108},{20,116},{28,124... | collective-permute-start | bytes 786440 | tf_op jit(solution)/shard_map/ppermute | solution.py:49
  90.3 2.4 %collective-permute-start.19 = (f16[512,256]{1,0:T(8,128)(2,1)S(1)}, f16[512,256]{1,0:T(8,128)(2,1)S(1)}, u32[]{:S(2)}, u32[]{:S(2)}) collective-permute-start(f16[512,256]{1,0:T(8,128)(2,1)S(1)} %get-tuple-element.22), channel_id=1, source_target_pairs={{0,64},{8,72},{16,80},{24,88},{4,68},{12,76},{20,84},{28,92},{1,65... | collective-permute-start | bytes 786440 | tf_op jit(solution)/shard_map/ppermute | solution.py:49
  92.7 1.5 %collective-permute-start.18 = (f16[512,256]{1,0:T(8,128)(2,1)S(1)}, f16[512,256]{1,0:T(8,128)(2,1)S(1)}, u32[]{:S(2)}, u32[]{:S(2)}) collective-permute-start(f16[512,256]{1,0:T(8,128)(2,1)S(1)} %get-tuple-element.23), channel_id=1, source_target_pairs={{0,96},{8,104},{16,112},{24,120},{4,100},{12,108},{20,116},{28,124... | collective-permute-start | bytes 786440 | tf_op jit(solution)/shard_map/ppermute | solution.py:49
  94.2 3.0 %collective-permute-done.11 = f16[512,256]{1,0:T(8,128)(2,1)S(1)} collective-permute-done((f16[512,256]{1,0:T(8,128)(2,1)S(1)}, f16[512,256]{1,0:T(8,128)(2,1)S(1)}, u32[]{:S(2)}, u32[]{:S(2)}) %collective-permute-start.11) | collective-permute-done | bytes 262176 | tf_op jit(solution)/shard_map/ppermute | solution.py:49
  97.2 0.9 collective-permute-start.17
  98.1 3.8 %collective-permute-done.10 = f16[512,256]{1,0:T(8,128)(2,1)S(1)} collective-permute-done((f16[512,256]{1,0:T(8,128)(2,1)S(1)}, f16[512,256]{1,0:T(8,128)(2,1)S(1)}, u32[]{:S(2)}, u32[]{:S(2)}) %collective-permute-start.10) | collective-permute-done | bytes 262176 | tf_op jit(solution)/shard_map/ppermute | solution.py:49
  101.9 1.9 %collective-permute-done.9 = f16[512,256]{1,0:T(8,128)(2,1)S(1)} collective-permute-done((f16[512,256]{1,0:T(8,128)(2,1)S(1)}, f16[512,256]{1,0:T(8,128)(2,1)S(1)}, u32[]{:S(2)}, u32[]{:S(2)}) %collective-permute-start.9) | collective-permute-done | bytes 262176 | tf_op jit(solution)/shard_map/ppermute | solution.py:49
  103.8 1.3 bitcast_add_fusion.1
  105.1 3.4 %collective-permute-done.19 = f16[512,256]{1,0:T(8,128)(2,1)S(1)} collective-permute-done((f16[512,256]{1,0:T(8,128)(2,1)S(1)}, f16[512,256]{1,0:T(8,128)(2,1)S(1)}, u32[]{:S(2)}, u32[]{:S(2)}) %collective-permute-start.19) | collective-permute-done | bytes 262176 | tf_op jit(solution)/shard_map/ppermute | solution.py:49
  108.5 4.7 %collective-permute-done.18 = f16[512,256]{1,0:T(8,128)(2,1)S(1)} collective-permute-done((f16[512,256]{1,0:T(8,128)(2,1)S(1)}, f16[512,256]{1,0:T(8,128)(2,1)S(1)}, u32[]{:S(2)}, u32[]{:S(2)}) %collective-permute-start.18) | collective-permute-done | bytes 262176 | tf_op jit(solution)/shard_map/ppermute | solution.py:49
  113.2 1.4 collective-permute-done.17
  114.7 1.1 collective-permute-start.20
  115.8 6.4 %collective-permute-done.20 = f16[512,256]{1,0:T(8,128)(2,1)S(1)} collective-permute-done((f16[512,256]{1,0:T(8,128)(2,1)S(1)}, f16[512,256]{1,0:T(8,128)(2,1)S(1)}, u32[]{:S(2)}, u32[]{:S(2)}) %collective-permute-start.20) | collective-permute-done | bytes 262176 | tf_op jit(solution)/shard_map/ppermute | solution.py:54
  122.4 6.1 %collective-permute-start.21 = (f16[512,256]{1,0:T(8,128)(2,1)S(1)}, f16[512,256]{1,0:T(8,128)(2,1)S(1)}, u32[]{:S(2)}, u32[]{:S(2)}) collective-permute-start(f16[512,256]{1,0:T(8,128)(2,1)S(1)} %add_convert_fusion), channel_id=1, source_target_pairs={{0,19},{8,27},{16,5},{24,13},{4,116},{12,124},{20,20},{28,28},{1,2... | collective-permute-start | bytes 786440 | tf_op jit(solution)/shard_map/ppermute | solution.py:68
  128.6 7.4 %collective-permute-done.21 = f16[512,256]{1,0:T(8,128)(2,1)S(1)} collective-permute-done((f16[512,256]{1,0:T(8,128)(2,1)S(1)}, f16[512,256]{1,0:T(8,128)(2,1)S(1)}, u32[]{:S(2)}, u32[]{:S(2)}) %collective-permute-start.21) | collective-permute-done | bytes 262176 | tf_op jit(solution)/shard_map/ppermute | solution.py:68
  136.0 0.8 convert_multiply_fusion
  (39 shorter events, 1.5 us)
Async XLA Ops:
  0.0 25.0 %copy-start = (bf16[1536,512]{1,0:T(8,128)(2,1)S(1)}, bf16[1536,512]{1,0:T(8,128)(2,1)}, u32[]{:S(2)}) copy-start(bf16[1536,512]{1,0:T(8,128)(2,1)} %refs_2_.3) | copy-start | bytes 4718596
  0.0 24.5 %copy-start.11 = (f32[128]{0:T(128)S(1)}, f32[128]{0:T(128)}, u32[]{:S(2)}) copy-start(f32[128]{0:T(128)} %param.8) | copy-start | bytes 1540
  0.0 24.5 %copy-start.9 = (s32[1536]{0:T(1024)S(1)}, s32[1536]{0:T(1024)}, u32[]{:S(2)}) copy-start(s32[1536]{0:T(1024)} %param.6) | copy-start | bytes 18436
  1.9 10.8 %collective-permute-start = (bf16[384,512]{1,0:T(8,128)(2,1)}, bf16[384,512]{1,0:T(8,128)(2,1)S(1)}, u32[]{:S(2)}, u32[]{:S(2)}) collective-permute-start(bf16[384,512]{1,0:T(8,128)(2,1)} %slice.60), channel_id=1, source_target_pairs={{0,3},{8,11},{16,19},{24,27},{4,7},{12,15},{20,23},{28,31},{1,0},{... | collective-permute-start | bytes 1179656 | tf_op jit(solution)/shard_map/ppermute | solution.py:49
  6.8 19.8 %copy-start.10 = (s32[1536]{0:T(1024)S(1)}, s32[1536]{0:T(1024)}, u32[]{:S(2)}) copy-start(s32[1536]{0:T(1024)} %param.7) | copy-start | bytes 18436
  6.8 14.3 %collective-permute-start.1 = (bf16[384,512]{1,0:T(8,128)(2,1)}, bf16[384,512]{1,0:T(8,128)(2,1)S(1)}, u32[]{:S(2)}, u32[]{:S(2)}) collective-permute-start(bf16[384,512]{1,0:T(8,128)(2,1)} %get-tuple-element.29), channel_id=1, source_target_pairs={{0,3},{8,11},{16,19},{24,27},{4,7},{12,15},{20,23},{28,31},{1,0},{... | collective-permute-start | bytes 1179656 | tf_op jit(solution)/shard_map/ppermute | solution.py:49
  7.3 34.2 %collective-permute-start.4 = (bf16[384,512]{1,0:T(8,128)(2,1)}, bf16[384,512]{1,0:T(8,128)(2,1)S(1)}, u32[]{:S(2)}, u32[]{:S(2)}) collective-permute-start(bf16[384,512]{1,0:T(8,128)(2,1)} %slice.60), channel_id=1, source_target_pairs={{0,1},{8,9},{16,17},{24,25},{4,5},{12,13},{20,21},{28,29},{1,2},{9... | collective-permute-start | bytes 1179656 | tf_op jit(solution)/shard_map/ppermute | solution.py:49
  8.3 33.3 %collective-permute-start.5 = (bf16[384,512]{1,0:T(8,128)(2,1)}, bf16[384,512]{1,0:T(8,128)(2,1)S(1)}, u32[]{:S(2)}, u32[]{:S(2)}) collective-permute-start(bf16[384,512]{1,0:T(8,128)(2,1)} %get-tuple-element.29), channel_id=1, source_target_pairs={{0,1},{8,9},{16,17},{24,25},{4,5},{12,13},{20,21},{28,29},{1,2},{9... | collective-permute-start | bytes 1179656 | tf_op jit(solution)/shard_map/ppermute | solution.py:49
  8.3 21.3 %collective-permute-start.2 = (bf16[384,512]{1,0:T(8,128)(2,1)}, bf16[384,512]{1,0:T(8,128)(2,1)}, u32[]{:S(2)}, u32[]{:S(2)}) collective-permute-start(bf16[384,512]{1,0:T(8,128)(2,1)} %get-tuple-element.28), channel_id=1, source_target_pairs={{0,3},{8,11},{16,19},{24,27},{4,7},{12,15},{20,23},{28,31},{1,0},{... | collective-permute-start | bytes 1179656 | tf_op jit(solution)/shard_map/ppermute | solution.py:49
  12.7 31.8 %collective-permute-start.6 = (bf16[384,512]{1,0:T(8,128)(2,1)}, bf16[384,512]{1,0:T(8,128)(2,1)}, u32[]{:S(2)}, u32[]{:S(2)}) collective-permute-start(bf16[384,512]{1,0:T(8,128)(2,1)} %get-tuple-element.28), channel_id=1, source_target_pairs={{0,1},{8,9},{16,17},{24,25},{4,5},{12,13},{20,21},{28,29},{1,2},{9... | collective-permute-start | bytes 1179656 | tf_op jit(solution)/shard_map/ppermute | solution.py:49
  21.2 16.7 %collective-permute-start.3 = (bf16[384,512]{1,0:T(8,128)(2,1)S(1)}, bf16[384,512]{1,0:T(8,128)(2,1)}, u32[]{:S(2)}, u32[]{:S(2)}) collective-permute-start(bf16[384,512]{1,0:T(8,128)(2,1)S(1)} %get-tuple-element.27), channel_id=1, source_target_pairs={{0,3},{8,11},{16,19},{24,27},{4,7},{12,15},{20,23},{28,31},{1,0},{... | collective-permute-start | bytes 1179656 | tf_op jit(solution)/shard_map/ppermute | solution.py:49
  29.6 18.2 %collective-permute-start.7 = (bf16[384,512]{1,0:T(8,128)(2,1)S(1)}, bf16[384,512]{1,0:T(8,128)(2,1)}, u32[]{:S(2)}, u32[]{:S(2)}) collective-permute-start(bf16[384,512]{1,0:T(8,128)(2,1)S(1)} %get-tuple-element.27), channel_id=1, source_target_pairs={{0,1},{8,9},{16,17},{24,25},{4,5},{12,13},{20,21},{28,29},{1,2},{9... | collective-permute-start | bytes 1179656 | tf_op jit(solution)/shard_map/ppermute | solution.py:49
  37.9 22.7 %collective-permute-start.12 = (bf16[384,512]{1,0:T(8,128)(2,1)S(1)}, bf16[384,512]{1,0:T(8,128)(2,1)}, u32[]{:S(2)}, u32[]{:S(2)}) collective-permute-start(bf16[384,512]{1,0:T(8,128)(2,1)S(1)} %collective-permute-done.refs_3_.refs_4_), channel_id=1, source_target_pairs={{0,4},{8,12},{16,20},{24,28},{4,0},{12,8},{20,16},{28,24},{1,5},{9... | collective-permute-start | bytes 1179656 | tf_op jit(solution)/shard_map/ppermute | solution.py:49
  41.5 5.9 %copy-start.5 = (bf16[384,512]{1,0:T(8,128)(2,1)}, bf16[384,512]{1,0:T(8,128)(2,1)S(1)}, u32[]{:S(2)}) copy-start(bf16[384,512]{1,0:T(8,128)(2,1)S(1)} %collective-permute-done.4.refs_7_) | copy-start | bytes 1179652
  41.5 19.1 %collective-permute-start.13 = (bf16[384,512]{1,0:T(8,128)(2,1)S(1)}, bf16[384,512]{1,0:T(8,128)(2,1)}, u32[]{:S(2)}, u32[]{:S(2)}) collective-permute-start(bf16[384,512]{1,0:T(8,128)(2,1)S(1)} %collective-permute-done.1.refs_4_.refs_5_), channel_id=1, source_target_pairs={{0,4},{8,12},{16,20},{24,28},{4,0},{12,8},{20,16},{28,24},{1,5},{9... | collective-permute-start | bytes 1179656 | tf_op jit(solution)/shard_map/ppermute | solution.py:49
  41.6 5.9 %copy-start.7 = (bf16[384,512]{1,0:T(8,128)(2,1)}, bf16[384,512]{1,0:T(8,128)(2,1)S(1)}, u32[]{:S(2)}) copy-start(bf16[384,512]{1,0:T(8,128)(2,1)S(1)} %collective-permute-done.5.refs_8_) | copy-start | bytes 1179652
  41.6 24.8 %collective-permute-start.14 = (bf16[384,512]{1,0:T(8,128)(2,1)}, bf16[384,512]{1,0:T(8,128)(2,1)}, u32[]{:S(2)}, u32[]{:S(2)}) collective-permute-start(bf16[384,512]{1,0:T(8,128)(2,1)} %collective-permute-done.2.refs_5_.refs_6_), channel_id=1, source_target_pairs={{0,4},{8,12},{16,20},{24,28},{4,0},{12,8},{20,16},{28,24},{1,5},{9... | collective-permute-start | bytes 1179656 | tf_op jit(solution)/shard_map/ppermute | solution.py:49
  44.5 30.4 %collective-permute-start.15 = (bf16[384,512]{1,0:T(8,128)(2,1)}, bf16[384,512]{1,0:T(8,128)(2,1)}, u32[]{:S(2)}, u32[]{:S(2)}) collective-permute-start(bf16[384,512]{1,0:T(8,128)(2,1)} %collective-permute-done.3.refs_6_.refs_7_), channel_id=1, source_target_pairs={{0,4},{8,12},{16,20},{24,28},{4,0},{12,8},{20,16},{28,24},{1,5},{9... | collective-permute-start | bytes 1179656 | tf_op jit(solution)/shard_map/ppermute | solution.py:49
  47.8 1.4 %copy-start.4 = (bf16[512,1536]{1,0:T(8,128)(2,1)S(1)}, bf16[512,1536]{1,0:T(8,128)(2,1)}, u32[]{:S(2)}) copy-start(bf16[512,1536]{1,0:T(8,128)(2,1)} %fusion.refs_1_) | copy-start | bytes 4718596
  49.2 1.0 copy-start.6
  50.2 1.0 copy-start.8
  56.9 18.0 %copy-start.3 = (f32[4,512,256]{2,1,0:T(8,128)}, f32[4,512,256]{2,1,0:T(8,128)S(1)}, u32[]{:S(2)}) copy-start(f32[4,512,256]{2,1,0:T(8,128)S(1)} %get-tuple-element.16) | copy-start | bytes 6291460
  58.2 27.9 %collective-permute-start.8 = (f16[4,512,256]{2,1,0:T(8,128)(2,1)}, f16[4,512,256]{2,1,0:T(8,128)(2,1)}, u32[]{:S(2)}, u32[]{:S(2)}) collective-permute-start(f16[4,512,256]{2,1,0:T(8,128)(2,1)} %convert_element_type.114), channel_id=1, source_target_pairs={{0,8},{8,0},{16,24},{24,16},{4,12},{12,4},{20,28},{28,20},{1,9},{9... | collective-permute-start | bytes 3145736 | tf_op jit(solution)/shard_map/ppermute | solution.py:49
  81.5 1.3 copy-start.1
  84.0 6.1 %copy-start.2 = (f32[4,512,256]{2,1,0:T(8,128)S(1)}, f32[4,512,256]{2,1,0:T(8,128)}, u32[]{:S(2)}) copy-start(f32[4,512,256]{2,1,0:T(8,128)} %copy-done.1) | copy-start | bytes 6291460
  84.0 6.1 %collective-permute-start.16 = (f16[4,512,256]{2,1,0:T(8,128)(2,1)}, f16[4,512,256]{2,1,0:T(8,128)(2,1)S(1)}, u32[]{:S(2)}, u32[]{:S(2)}) collective-permute-start(f16[4,512,256]{2,1,0:T(8,128)(2,1)} %convert_element_type.128), channel_id=1, source_target_pairs={{0,8},{8,0},{16,24},{24,16},{4,12},{12,4},{20,28},{28,20},{1,9},{9... | collective-permute-start | bytes 3145736 | tf_op jit(solution)/shard_map/ppermute | solution.py:49
  87.9 9.3 %collective-permute-start.11 = (f16[512,256]{1,0:T(8,128)(2,1)S(1)}, f16[512,256]{1,0:T(8,128)(2,1)S(1)}, u32[]{:S(2)}, u32[]{:S(2)}) collective-permute-start(f16[512,256]{1,0:T(8,128)(2,1)S(1)} %get-tuple-element.25), channel_id=1, source_target_pairs={{0,64},{8,72},{16,80},{24,88},{4,68},{12,76},{20,84},{28,92},{1,65... | collective-permute-start | bytes 786440 | tf_op jit(solution)/shard_map/ppermute | solution.py:49
  88.2 13.7 %collective-permute-start.10 = (f16[512,256]{1,0:T(8,128)(2,1)S(1)}, f16[512,256]{1,0:T(8,128)(2,1)S(1)}, u32[]{:S(2)}, u32[]{:S(2)}) collective-permute-start(f16[512,256]{1,0:T(8,128)(2,1)S(1)} %get-tuple-element.26), channel_id=1, source_target_pairs={{0,96},{8,104},{16,112},{24,120},{4,100},{12,108},{20,116},{28,124... | collective-permute-start | bytes 786440 | tf_op jit(solution)/shard_map/ppermute | solution.py:49
  90.1 13.7 %collective-permute-start.9 = (f16[512,256]{1,0:T(8,128)(2,1)S(1)}, f16[512,256]{1,0:T(8,128)(2,1)S(1)}, u32[]{:S(2)}, u32[]{:S(2)}) collective-permute-start(f16[512,256]{1,0:T(8,128)(2,1)S(1)} %get-tuple-element.24), channel_id=1, source_target_pairs={{0,32},{8,40},{16,48},{24,56},{4,36},{12,44},{20,52},{28,60},{1,33... | collective-permute-start | bytes 786440 | tf_op jit(solution)/shard_map/ppermute | solution.py:49
  90.3 18.2 %collective-permute-start.19 = (f16[512,256]{1,0:T(8,128)(2,1)S(1)}, f16[512,256]{1,0:T(8,128)(2,1)S(1)}, u32[]{:S(2)}, u32[]{:S(2)}) collective-permute-start(f16[512,256]{1,0:T(8,128)(2,1)S(1)} %get-tuple-element.22), channel_id=1, source_target_pairs={{0,64},{8,72},{16,80},{24,88},{4,68},{12,76},{20,84},{28,92},{1,65... | collective-permute-start | bytes 786440 | tf_op jit(solution)/shard_map/ppermute | solution.py:49
  92.7 20.5 %collective-permute-start.18 = (f16[512,256]{1,0:T(8,128)(2,1)S(1)}, f16[512,256]{1,0:T(8,128)(2,1)S(1)}, u32[]{:S(2)}, u32[]{:S(2)}) collective-permute-start(f16[512,256]{1,0:T(8,128)(2,1)S(1)} %get-tuple-element.23), channel_id=1, source_target_pairs={{0,96},{8,104},{16,112},{24,120},{4,100},{12,108},{20,116},{28,124... | collective-permute-start | bytes 786440 | tf_op jit(solution)/shard_map/ppermute | solution.py:49
  97.2 17.3 %collective-permute-start.17 = (f16[512,256]{1,0:T(8,128)(2,1)S(1)}, f16[512,256]{1,0:T(8,128)(2,1)S(1)}, u32[]{:S(2)}, u32[]{:S(2)}) collective-permute-start(f16[512,256]{1,0:T(8,128)(2,1)S(1)} %get-tuple-element.21), channel_id=1, source_target_pairs={{0,32},{8,40},{16,48},{24,56},{4,36},{12,44},{20,52},{28,60},{1,33... | collective-permute-start | bytes 786440 | tf_op jit(solution)/shard_map/ppermute | solution.py:49
  114.7 7.5 %collective-permute-start.20 = (f16[512,256]{1,0:T(8,128)(2,1)S(1)}, f16[512,256]{1,0:T(8,128)(2,1)S(1)}, u32[]{:S(2)}, u32[]{:S(2)}) collective-permute-start(f16[512,256]{1,0:T(8,128)(2,1)S(1)} %select_convert_fusion), channel_id=1, source_target_pairs={{0,16},{8,24},{16,0},{24,8},{4,20},{12,28},{20,4},{28,12},{1,17},{... | collective-permute-start | bytes 786440 | tf_op jit(solution)/shard_map/ppermute | solution.py:54
  122.4 13.6 %collective-permute-start.21 = (f16[512,256]{1,0:T(8,128)(2,1)S(1)}, f16[512,256]{1,0:T(8,128)(2,1)S(1)}, u32[]{:S(2)}, u32[]{:S(2)}) collective-permute-start(f16[512,256]{1,0:T(8,128)(2,1)S(1)} %add_convert_fusion), channel_id=1, source_target_pairs={{0,19},{8,27},{16,5},{24,13},{4,116},{12,124},{20,20},{28,28},{1,2... | collective-permute-start | bytes 786440 | tf_op jit(solution)/shard_map/ppermute | solution.py:68

commit v2 on v1

v2 whole, which is shorter than its diff:
```python
import functools
import math

import jax
import jax.numpy as jnp
import numpy as np
from jax import lax
from jax.experimental import pallas as pl
from jax.experimental.pallas import tpu as pltpu
from jax.sharding import PartitionSpec as P


AXES = ("pair", "ga")
CUTS = (384,) * 4
GAIN = 4.0

O, N, S, Z = (0, 0), (1, 0), (3, 0), (1, 1)
EARLY = ((O, O), (O, N), (O, S), (S, N))
LATE = ((O, Z), (Z, O), (Z, N), (S, Z))
PLAN = (
    ((3, 0, 2, 1), (1, 0, 3, 2), (0, 0, 1, 1)),
    ((2, 3, 1, 0), (1, 2, 3, 0), (1, 0, 0, 1)),
    ((1, 0, 3, 2), (3, 1, 2, 0), (0, 0, 1, 1)),
    ((1, 2, 0, 3), (2, 1, 3, 0), (0, 0, 1, 0)),
    ((2, 3, 1, 0), (0, 1, 2, 3), (0, 0, 1, 0)),
    ((1, 2, 0, 3), (3, 0, 1, 2), (1, 1, 1, 0)),
    ((1, 0, 2, 3), (0, 3, 1, 2), (1, 0, 0, 1)),
    ((0, 3, 1, 2), (0, 3, 2, 1), (1, 1, 0, 1)),
)


def index(x, y, z, core):
    x, y, z = x % 4, y % 4, z % 4
    return (4 * x + 2 * (z % 2) + core) * 8 + 4 * (z // 2) + y


def devices():
    for x in range(4):
        for y in range(4):
            for z in range(4):
                for core in range(2):
                    yield x, y, z, core


def shift(value, dx=0, dy=0, dz=0, swap=False):
    pairs = [
        (index(x, y, z, c), index(x + dx, y + dy, z + dz, 1 - c if swap else c))
        for x, y, z, c in devices()
    ]
    return lax.ppermute(value, AXES, pairs)


def swap_z_lo(value):
    pairs = [(index(x, y, z, c), index(x, y, z ^ 1, c)) for x, y, z, c in devices()]
    return lax.ppermute(value, AXES, pairs)


def to_owner(value):
    pairs = []
    for x, y, z, c in devices():
        early, late, keeper = PLAN[4 * (z // 2) + y]
        keeps = keeper[x] == z % 2
        row, col = EARLY[early[x]] if keeps else LATE[late[x]]
        row_y, row_hi = (y + row[0]) % 4, (z // 2 + row[1]) % 2
        block = 4 * ((z // 2 + col[1]) % 2) + (y + col[0]) % 4
        pairs.append(
            (index(x, y, z, c), index(block // 2, row_y, 2 * row_hi + block % 2, c))
        )
    return lax.ppermute(value, AXES, pairs)


def planned(pair, ga):
    x, z_lo = pair >> 2, (pair >> 1) & 1
    word = jnp.int32(0)
    for k, (early, late, keeper) in enumerate(PLAN):
        code = sum(v << 2 * i for i, v in enumerate(early + late))
        code += sum(v << 16 + i for i, v in enumerate(keeper))
        word = jnp.where(ga == k, code, word)

    def entry(d, base):
        return (word >> (2 * ((x + d) & 3) + base)) & 3

    early, late = ([entry(d, base) for d in range(4)] for base in (0, 8))
    return early, late, ((word >> (16 + x)) & 1) == z_lo


def lookup(bands, energy):
    levels = lax.broadcasted_iota(jnp.int32, (1, energy.shape[0]), 1)
    onehot = (bands[:, None] == levels).astype(jnp.float32)
    return jnp.sum(onehot * energy[None, :], axis=1)


def placing(which):
    return [sum(jnp.where(w == s, d, 0) for d, w in enumerate(which)) for s in range(4)]


def chunk(k):
    return slice(sum(CUTS[:k]), sum(CUTS[: k + 1]))


COUNT = len(CUTS)
SPLIT = 2


def stage_kernel(late, lo, hi, n_in, *refs):
    first, last = lo == 0, hi == COUNT
    sources, refs = refs[:n_in], refs[n_in:]
    n_out = (2 if last else 1) + (not late)
    outs, (row, own_t, own, north, far, *rest, sems) = refs[:n_out], refs[n_out:]
    rows = slice(chunk(lo).start, chunk(hi - 1).stop)
    spans = [slice(chunk(k).start - rows.start, chunk(k).stop - rows.start) for k in range(lo, hi)]
    pairs = [
        (sources[0].at[:, rows], row),
        (sources[1].at[:, rows], own_t),
        (sources[2].at[rows, :], own),
        *((s, north.at[c]) for s, c in zip(sources[3:], spans)),
        *((s, far.at[c]) for s, c in zip(sources[3 + hi - lo :], spans)),
    ]
    extra = sources[len(pairs) :]
    if late:
        south_t, flipped = rest
        edge = chunk(SPLIT).start
        pairs += [(extra[0], south_t.at[:, :edge]), (extra[1], south_t.at[:, edge:])]
    else:
        flipped = outs[-1]
        pairs += zip(extra, rest)
    copies = [
        pltpu.make_async_copy(s, t, sems.at[i]) for i, (s, t) in enumerate(pairs)
    ]
    for copy in copies:
        copy.start()
    pair, ga = lax.axis_index("pair"), lax.axis_index("ga")
    core, at = pair & 1, placing(planned(pair, ga)[int(late)])
    half = own.shape[1] // 2

    def put(i, left, right):
        total = jnp.dot(left[...], right[...], preferred_element_type=jnp.float32)
        if not first:
            total = total + rest[0][i]
        if last:
            low, high = total[:, :half], total[:, half:]
            outs[0][at[i]] = jnp.where(core == 0, high, low)
            outs[1][at[i]] = jnp.where(core == 0, low, high)
        else:
            outs[0][i] = total

    for copy in copies:
        copy.wait()
    if late:
        put(0, own_t, far)
    else:
        put(0, own_t, own)
        put(1, own_t, north)
        put(2, own_t, far)
    flipped[...] = (row[...] * far[...].T.astype(jnp.float32)).astype(flipped.dtype)
    if late:
        put(1, flipped, own)
        put(2, flipped, north)
        put(3, south_t, far)
    else:
        put(3, flipped, north)


def run_stage(late, lo, hi, sources):
    size, _ = sources[1].shape
    rows = sum(CUTS[lo:hi])
    tall, wide = ((rows, size), jnp.bfloat16), ((size, rows), jnp.bfloat16)
    held = [((1, rows), jnp.float32), wide, tall, tall, tall]
    outs = [((4, size, size), jnp.float32)]
    if late:
        held += [wide, wide]
    elif lo:
        held += outs
    if hi == COUNT:
        outs = [((4, size, size // 2), jnp.float32)] * 2
    if not late:
        outs.append(wide)
    return pl.pallas_call(
        functools.partial(stage_kernel, late, lo, hi, len(sources)),
        out_shape=[jax.ShapeDtypeStruct(*o) for o in outs],
        in_specs=[pl.BlockSpec(memory_space=pl.ANY)] * len(sources),
        out_specs=[pl.BlockSpec(memory_space=pltpu.VMEM)] * len(outs),
        scratch_shapes=[
            *(pltpu.VMEM(*h) for h in held),
            pltpu.SemaphoreType.DMA((len(sources),)),
        ],
        compiler_params=pltpu.CompilerParams(vmem_limit_bytes=28 * 2**20),
        cost_estimate=pl.CostEstimate(
            flops=8 * size * size * rows, bytes_accessed=2**23, transcendentals=0
        ),
    )(*sources)


def body(own, val_band, cond_band, val_energy, cond_energy):
    pairs_total = own.shape[0] * lax.axis_size("pair")
    pair, ga = lax.axis_index("pair"), lax.axis_index("ga")
    starts = np.cumsum((0,) + CUTS)

    def rows(block, k):
        return block[starts[k] : starts[k + 1]]

    norths, souths, farther = [], [], []
    first = rows(own, 0)
    rest = lax.optimization_barrier((own, first))[0]
    for k in range(len(CUTS)):
        piece = rows(rest, k) if k else first
        norths.append(shift(piece, dy=-1))
        souths.append(shift(piece, dy=1))
        farther.append(shift(norths[k], dz=2))

    def over_x(theirs, mine):
        theirs = shift(theirs.astype(jnp.float16), swap=True)
        joined = [mine[d] + theirs[d].astype(jnp.float32) for d in range(4)]
        kept, *sent = lax.optimization_barrier(
            [joined[0]] + [joined[d].astype(jnp.float16) for d in (1, 3, 2)]
        )
        got = []
        for d, value in zip((1, 3, 2), sent):
            got.append(shift(value, dx=d))
        return kept, got

    gap = lookup(val_band, val_energy) - lookup(cond_band, cond_energy)
    weight = (4.0 * GAIN) / (gap * math.sqrt(pairs_total))
    row = weight[None, :]
    own_t = (row * own.T.astype(jnp.float32)).astype(jnp.bfloat16)
    row, own_t = lax.optimization_barrier((row, own_t))
    base = [row, own_t, own]
    one, two = slice(0, SPLIT), slice(SPLIT, COUNT)

    early_sum, south_a = run_stage(False, 0, SPLIT, base + norths[one] + souths[one])
    *early, south_b = run_stage(
        False, SPLIT, COUNT, base + norths[two] + souths[two] + [early_sum]
    )
    early, early_got = over_x(*early)
    late = run_stage(
        True, 0, COUNT, base + norths + farther + [south_a, south_b]
    )
    late, late_got = over_x(*late)

    early = early + sum(g.astype(jnp.float32) for g in early_got)
    early = lax.optimization_barrier(early)
    late = late + sum(g.astype(jnp.float32) for g in late_got)
    keeps = planned(pair, ga)[2]
    kept = jnp.where(keeps, early, late)
    got = swap_z_lo(jnp.where(keeps, late, early).astype(jnp.float16))
    total = kept + got.astype(jnp.float32)
    total = to_owner(total.astype(jnp.float16))
    return total.astype(jnp.float32) * (1.0 / GAIN)


def solution(mesh):
    placed = (P("pair", "ga"), P("pair"), P("pair"), P(), P())
    return jax.shard_map(
        body, mesh=mesh, in_specs=placed, out_specs=P("ga", "pair"), check_vma=False
    )
```

time: 138 us -> 130 us (0.942)
  waiting for transfers between devices: 65.2 us -> 60.4 us
  local copies, waits for them, and re-layouts: 10.7 us -> 6.45 us
  starting transfers between devices: 36.9 us -> 40.1 us
  other arithmetic: 11.5 us -> 9.28 us
    ppermute x20, waiting for transfers between devices: 51.4 us -> 46.6 us  [shift(): return lax.ppermute(value, AXES, pairs)]
    unnamed x25 -> x19, local copies, waits for them, and re-layouts: 6.35 us -> 2.37 us
    ppermute x20, starting transfers between devices: 29.7 us -> 33 us  [shift(): return lax.ppermute(value, AXES, pairs)]
    transpose x1 -> x0, other arithmetic: 2.85 us -> none  [body(): own_t = (column * own.astype(jnp.float32)).astype(jnp.bfloat16).T]
    convert_element_type x2 -> x3, other arithmetic: 2.02 us -> 3.65 us  [the longest x2 1.98 us: over_x(): joined[d].astype(jnp.float16)]
    pallas_call x2 -> x3, Pallas kernels: 12.4 us -> 11.9 us  [run_stage(): pl.pallas_call(functools.partial(stage_kernel, late, lo, hi, len(sources)...]
  transfers between devices with their start and end apart: 22 -> 22, of which waited for: 14 -> 14; matrix products, arithmetic and copies ran while one was open for 11% -> 7% of each run, Pallas kernels for 9% -> 9%
where the time goes in v2:
time: 130 us; the launch traced here: 128 us
  waiting for transfers between devices  60.4 us (46%)
  starting transfers between devices  40.1 us (31%)
  Pallas kernels  11.9 us (9%)
  other arithmetic  9.28 us (7%)
  local copies, waits for them, and re-layouts  6.45 us (5%)
    ppermute x20, waiting for transfers between devices, shift(): return lax.ppermute(value, AXES, pairs)  46.6 us
    ppermute x20, starting transfers between devices, shift(): return lax.ppermute(value, AXES, pairs)  33 us
    pallas_call x3, Pallas kernels, run_stage(): pl.pallas_call(functools.partial(stage_kernel, late, lo, hi, len(sources)...  11.9 us
    ppermute x1, waiting for transfers between devices, to_owner(): return lax.ppermute(value, AXES, pairs)  7.44 us
    ppermute x1, waiting for transfers between devices, swap_z_lo(): return lax.ppermute(value, AXES, pairs)  6.36 us
    ppermute x1, starting transfers between devices, to_owner(): return lax.ppermute(value, AXES, pairs)  5.94 us
    slice x2, local copies, waits for them, and re-layouts, rows(): return block[starts[k]:starts[k + 1]]  4.08 us
  transfers between devices with their start and end apart: 22, of which 14 were waited for; matrix products, arithmetic and copies ran while one was open for 7% of the time, Pallas kernels for 9%

profile of v2, /device:TPU:5, one launch (start us, length us, event | category | flops | bytes accessed | tf_op | source)
XLA Modules:
  0.0 128.2 jit_solution(11698889083706329696)
XLA Ops:
  0.0 1.9 %slice.60 = bf16[384,512]{1,0:T(8,128)(2,1)} slice(bf16[1536,512]{1,0:T(8,128)(2,1)} %refs_2_.5), slice={[0:384], [0:512]} | slice | bytes 786432 | tf_op jit(solution)/shard_map/slice | solution.py:200
  1.9 2.2 %fusion.7 = (bf16[384,512]{1,0:T(8,128)(2,1)}, bf16[384,512]{1,0:T(8,128)(2,1)S(1)}, bf16[384,512]{1,0:T(8,128)(2,1)}) fusion(bf16[1536,512]{1,0:T(8,128)(2,1)} %refs_2_.5), kind=kLoop, calls=%fused_computation.26 | loop fusion | bytes 2359296 | tf_op jit(solution)/shard_map/slice | solution.py:200
  4.1 2.7 %collective-permute-start = (bf16[384,512]{1,0:T(8,128)(2,1)}, bf16[384,512]{1,0:T(8,128)(2,1)S(1)}, u32[]{:S(2)}, u32[]{:S(2)}) collective-permute-start(bf16[384,512]{1,0:T(8,128)(2,1)} %get-tuple-element.51), channel_id=1, source_target_pairs={{0,3},{8,11},{16,19},{24,27},{4,7},{12,15},{20,23},{28,31},{1,0},{... | collective-permute-start | bytes 1179656 | tf_op jit(solution)/shard_map/ppermute | solution.py:50
  6.8 0.5 collective-permute-start.1
  7.3 1.0 collective-permute-start.2
  8.3 1.7 %collective-permute-start.4 = (bf16[384,512]{1,0:T(8,128)(2,1)}, bf16[384,512]{1,0:T(8,128)(2,1)S(1)}, u32[]{:S(2)}, u32[]{:S(2)}) collective-permute-start(bf16[384,512]{1,0:T(8,128)(2,1)} %slice.60), channel_id=1, source_target_pairs={{0,3},{8,11},{16,19},{24,27},{4,7},{12,15},{20,23},{28,31},{1,0},{... | collective-permute-start | bytes 1179656 | tf_op jit(solution)/shard_map/ppermute | solution.py:50
  10.0 5.0 %collective-permute-done.refs_3_.refs_5_ = bf16[384,512]{1,0:T(8,128)(2,1)S(1)} collective-permute-done((bf16[384,512]{1,0:T(8,128)(2,1)}, bf16[384,512]{1,0:T(8,128)(2,1)S(1)}, u32[]{:S(2)}, u32[]{:S(2)}) %collective-permute-start) | collective-permute-done | bytes 393248 | tf_op jit(solution)/shard_map/ppermute | solution.py:50
  14.9 3.3 %collective-permute-start.5 = (bf16[384,512]{1,0:T(8,128)(2,1)}, bf16[384,512]{1,0:T(8,128)(2,1)S(1)}, u32[]{:S(2)}, u32[]{:S(2)}) collective-permute-start(bf16[384,512]{1,0:T(8,128)(2,1)} %get-tuple-element.49), channel_id=1, source_target_pairs={{0,3},{8,11},{16,19},{24,27},{4,7},{12,15},{20,23},{28,31},{1,0},{... | collective-permute-start | bytes 1179656 | tf_op jit(solution)/shard_map/ppermute | solution.py:50
  18.2 5.0 %collective-permute-done.1.refs_4_.refs_6_ = bf16[384,512]{1,0:T(8,128)(2,1)S(1)} collective-permute-done((bf16[384,512]{1,0:T(8,128)(2,1)S(1)}, bf16[384,512]{1,0:T(8,128)(2,1)S(1)}, u32[]{:S(2)}, u32[]{:S(2)}) %collective-permute-start.1) | collective-permute-done | bytes 393248 | tf_op jit(solution)/shard_map/ppermute | solution.py:50
  23.3 0.9 collective-permute-start.7
  24.1 0.5 select_reduce_fusion.1
  24.7 1.6 %copy.7 = bf16[1536,512]{0,1:T(8,128)(2,1)} copy(bf16[1536,512]{1,0:T(8,128)(2,1)S(1)} %copy-done) | data formatting | bytes 3145728 | tf_op args[0]
  26.3 1.2 select_reduce_fusion
  27.5 1.4 %collective-permute-start.3 = (bf16[384,512]{1,0:T(8,128)(2,1)}, bf16[384,512]{1,0:T(8,128)(2,1)S(1)}, u32[]{:S(2)}, u32[]{:S(2)}) collective-permute-start(bf16[384,512]{1,0:T(8,128)(2,1)} %copy-done.5), channel_id=1, source_target_pairs={{0,1},{8,9},{16,17},{24,25},{4,5},{12,13},{20,21},{28,29},{1,2},{9... | collective-permute-start | bytes 1179656 | tf_op jit(solution)/shard_map/ppermute | solution.py:50
  28.9 2.9 %collective-permute-done.4.refs_3_ = bf16[384,512]{1,0:T(8,128)(2,1)S(1)} collective-permute-done((bf16[384,512]{1,0:T(8,128)(2,1)}, bf16[384,512]{1,0:T(8,128)(2,1)S(1)}, u32[]{:S(2)}, u32[]{:S(2)}) %collective-permute-start.4) | collective-permute-done | bytes 393248 | tf_op jit(solution)/shard_map/ppermute | solution.py:50
  31.8 3.6 %collective-permute-start.12 = (bf16[384,512]{1,0:T(8,128)(2,1)S(1)}, bf16[384,512]{1,0:T(8,128)(2,1)S(1)}, u32[]{:S(2)}, u32[]{:S(2)}) collective-permute-start(bf16[384,512]{1,0:T(8,128)(2,1)S(1)} %collective-permute-done.4.refs_3_), channel_id=1, source_target_pairs={{0,4},{8,12},{16,20},{24,28},{4,0},{12,8},{20,16},{28,24},{1,5},{9... | collective-permute-start | bytes 1179656 | tf_op jit(solution)/shard_map/ppermute | solution.py:50
  35.4 4.8 %collective-permute-done.5.refs_4_ = bf16[384,512]{1,0:T(8,128)(2,1)S(1)} collective-permute-done((bf16[384,512]{1,0:T(8,128)(2,1)}, bf16[384,512]{1,0:T(8,128)(2,1)S(1)}, u32[]{:S(2)}, u32[]{:S(2)}) %collective-permute-start.5) | collective-permute-done | bytes 393248 | tf_op jit(solution)/shard_map/ppermute | solution.py:50
  40.2 3.6 %collective-permute-start.13 = (bf16[384,512]{1,0:T(8,128)(2,1)S(1)}, bf16[384,512]{1,0:T(8,128)(2,1)S(1)}, u32[]{:S(2)}, u32[]{:S(2)}) collective-permute-start(bf16[384,512]{1,0:T(8,128)(2,1)S(1)} %collective-permute-done.5.refs_4_), channel_id=1, source_target_pairs={{0,4},{8,12},{16,20},{24,28},{4,0},{12,8},{20,16},{28,24},{1,5},{9... | collective-permute-start | bytes 1179656 | tf_op jit(solution)/shard_map/ppermute | solution.py:50
  43.8 3.0 %collective-permute-start.15 = (bf16[384,512]{1,0:T(8,128)(2,1)S(1)}, bf16[384,512]{1,0:T(8,128)(2,1)S(1)}, u32[]{:S(2)}, u32[]{:S(2)}) collective-permute-start(bf16[384,512]{1,0:T(8,128)(2,1)S(1)} %collective-permute-done.1.refs_4_.refs_6_), channel_id=1, source_target_pairs={{0,4},{8,12},{16,20},{24,28},{4,0},{12,8},{20,16},{28,24},{1,5},{9... | collective-permute-start | bytes 1179656 | tf_op jit(solution)/shard_map/ppermute | solution.py:50
  46.8 1.7 %fusion.refs_1_ = bf16[512,1536]{1,0:T(8,128)(2,1)S(1)} fusion(bf16[1536,512]{0,1:T(8,128)(2,1)} %copy.7, f32[1536]{0:T(1024)S(1)} %multiply_divide_fusion), kind=kLoop, calls=%fused_computation.1 | loop fusion | flops 2359296 | bytes 3151872 | tf_op jit(solution)/shard_map/convert_element_type | solution.py:225
  48.5 3.5 %shard_map.55 = (f32[4,512,512]{2,1,0:T(8,128)S(1)}, bf16[512,768]{1,0:T(8,128)(2,1)S(1)}) custom-call(f32[1,1536]{1,0:T(1,128)S(1)} %div.19.refs_0_, bf16[512,1536]{1,0:T(8,128)(2,1)S(1)} %fusion.refs_1_, bf16[1536,512]{1,0:T(8,128)(2,1)S(1)} %copy-done, bf16[384,512]{1,0:T(8,128)(2,1)S(1)} %collective-permute-done.4.refs_3_, ...), custom_call_target="tpu_custom_call" | custom-call | flops 1610612736 | bytes 8388608 | tf_op jit(solution)/shard_map/pallas_call | solution.py:178
  52.0 3.0 %shard_map.56 = (f32[4,512,256]{2,1,0:T(8,128)S(1)}, f32[4,512,256]{2,1,0:T(8,128)S(1)}, bf16[512,768]{1,0:T(8,128)(2,1)S(1)}) custom-call(f32[1,1536]{1,0:T(1,128)S(1)} %div.19.refs_0_, bf16[512,1536]{1,0:T(8,128)(2,1)S(1)} %fusion.refs_1_, bf16[1536,512]{1,0:T(8,128)(2,1)S(1)} %copy-done, bf16[384,512]{1,0:T(8,128)(2,1)S(1)} %collective-permute-done.refs_3_.refs_5_, ...), custom_call_target="tpu_custom_call" | custom-call | flops 1610612736 | bytes 8388608 | tf_op jit(solution)/shard_map/pallas_call | solution.py:178
  55.0 1.4 %convert_element_type.119 = f16[4,512,256]{2,1,0:T(8,128)(2,1)} convert(f32[4,512,256]{2,1,0:T(8,128)S(1)} %get-tuple-element.28) | non-fusion elementwise | flops 524288 | bytes 3145728 | tf_op jit(solution)/shard_map/convert_element_type | solution.py:212
  56.6 2.4 %collective-permute-start.8 = (f16[4,512,256]{2,1,0:T(8,128)(2,1)}, f16[4,512,256]{2,1,0:T(8,128)(2,1)}, u32[]{:S(2)}, u32[]{:S(2)}) collective-permute-start(f16[4,512,256]{2,1,0:T(8,128)(2,1)} %convert_element_type.119), channel_id=1, source_target_pairs={{0,8},{8,0},{16,24},{24,16},{4,12},{12,4},{20,28},{28,20},{1,9},{9... | collective-permute-start | bytes 3145736 | tf_op jit(solution)/shard_map/ppermute | solution.py:50
  59.0 1.2 collective-permute-done.14.refs_9_
  60.2 8.4 %collective-permute-done.15.refs_10_ = bf16[384,512]{1,0:T(8,128)(2,1)S(1)} collective-permute-done((bf16[384,512]{1,0:T(8,128)(2,1)S(1)}, bf16[384,512]{1,0:T(8,128)(2,1)S(1)}, u32[]{:S(2)}, u32[]{:S(2)}) %collective-permute-start.15) | collective-permute-done | bytes 393248 | tf_op jit(solution)/shard_map/ppermute | solution.py:50
  68.6 5.4 %shard_map.57 = (f32[4,512,256]{2,1,0:T(8,128)S(1)}, f32[4,512,256]{2,1,0:T(8,128)S(1)}) custom-call(f32[1,1536]{1,0:T(1,128)S(1)} %div.19.refs_0_, bf16[512,1536]{1,0:T(8,128)(2,1)S(1)} %fusion.refs_1_, bf16[1536,512]{1,0:T(8,128)(2,1)S(1)} %copy-done, bf16[384,512]{1,0:T(8,128)(2,1)S(1)} %collective-permute-done.4.refs_3_, ...), custom_call_target="tpu_custom_call" | custom-call | flops 3221225472 | bytes 8388608 | tf_op jit(solution)/shard_map/pallas_call | solution.py:178
  74.1 1.2 convert_element_type.133
  75.2 0.5 copy-done.3
  75.7 2.1 %collective-permute-start.16 = (f16[4,512,256]{2,1,0:T(8,128)(2,1)}, f16[4,512,256]{2,1,0:T(8,128)(2,1)S(1)}, u32[]{:S(2)}, u32[]{:S(2)}) collective-permute-start(f16[4,512,256]{2,1,0:T(8,128)(2,1)} %convert_element_type.133), channel_id=1, source_target_pairs={{0,8},{8,0},{16,24},{24,16},{4,12},{12,4},{20,28},{28,20},{1,9},{9... | collective-permute-start | bytes 3145736 | tf_op jit(solution)/shard_map/ppermute | solution.py:50
  77.8 1.6 %fusion.3 = (f16[512,256]{1,0:T(8,128)(2,1)S(1)}, f16[512,256]{1,0:T(8,128)(2,1)S(1)}, f16[512,256]{1,0:T(8,128)(2,1)S(1)}, f32[512,256]{1,0:T(8,128)S(1)}) fusion(f32[4,512,256]{2,1,0:T(8,128)S(1)} %copy-done.2, f16[4,512,256]{2,1,0:T(8,128)(2,1)} %collective-permute-done.8), kind=kLoop, calls=%fused_computation.21 | loop fusion | flops 1441792 | bytes 4456448 | tf_op jit(solution)/shard_map/convert_element_type | solution.py:215
  79.4 0.3 collective-permute-start.11
  79.7 1.9 %collective-permute-start.10 = (f16[512,256]{1,0:T(8,128)(2,1)S(1)}, f16[512,256]{1,0:T(8,128)(2,1)S(1)}, u32[]{:S(2)}, u32[]{:S(2)}) collective-permute-start(f16[512,256]{1,0:T(8,128)(2,1)S(1)} %get-tuple-element.31), channel_id=1, source_target_pairs={{0,96},{8,104},{16,112},{24,120},{4,100},{12,108},{20,116},{28,124... | collective-permute-start | bytes 786440 | tf_op jit(solution)/shard_map/ppermute | solution.py:50
  81.6 0.4 fusion.6
  82.0 2.4 %collective-permute-start.19 = (f16[512,256]{1,0:T(8,128)(2,1)S(1)}, f16[512,256]{1,0:T(8,128)(2,1)S(1)}, u32[]{:S(2)}, u32[]{:S(2)}) collective-permute-start(f16[512,256]{1,0:T(8,128)(2,1)S(1)} %get-tuple-element.40), channel_id=1, source_target_pairs={{0,64},{8,72},{16,80},{24,88},{4,68},{12,76},{20,84},{28,92},{1,65... | collective-permute-start | bytes 786440 | tf_op jit(solution)/shard_map/ppermute | solution.py:50
  84.4 1.5 %collective-permute-start.18 = (f16[512,256]{1,0:T(8,128)(2,1)S(1)}, f16[512,256]{1,0:T(8,128)(2,1)S(1)}, u32[]{:S(2)}, u32[]{:S(2)}) collective-permute-start(f16[512,256]{1,0:T(8,128)(2,1)S(1)} %get-tuple-element.39), channel_id=1, source_target_pairs={{0,96},{8,104},{16,112},{24,120},{4,100},{12,108},{20,116},{28,124... | collective-permute-start | bytes 786440 | tf_op jit(solution)/shard_map/ppermute | solution.py:50
  85.9 2.0 %collective-permute-done.11 = f16[512,256]{1,0:T(8,128)(2,1)S(1)} collective-permute-done((f16[512,256]{1,0:T(8,128)(2,1)S(1)}, f16[512,256]{1,0:T(8,128)(2,1)S(1)}, u32[]{:S(2)}, u32[]{:S(2)}) %collective-permute-start.11) | collective-permute-done | bytes 262176 | tf_op jit(solution)/shard_map/ppermute | solution.py:50
  87.8 0.9 collective-permute-start.17
  88.8 5.0 %collective-permute-done.10 = f16[512,256]{1,0:T(8,128)(2,1)S(1)} collective-permute-done((f16[512,256]{1,0:T(8,128)(2,1)S(1)}, f16[512,256]{1,0:T(8,128)(2,1)S(1)}, u32[]{:S(2)}, u32[]{:S(2)}) %collective-permute-start.10) | collective-permute-done | bytes 262176 | tf_op jit(solution)/shard_map/ppermute | solution.py:50
  93.8 2.4 %collective-permute-done.9 = f16[512,256]{1,0:T(8,128)(2,1)S(1)} collective-permute-done((f16[512,256]{1,0:T(8,128)(2,1)S(1)}, f16[512,256]{1,0:T(8,128)(2,1)S(1)}, u32[]{:S(2)}, u32[]{:S(2)}) %collective-permute-start.9) | collective-permute-done | bytes 262176 | tf_op jit(solution)/shard_map/ppermute | solution.py:50
  96.4 2.8 %collective-permute-done.19 = f16[512,256]{1,0:T(8,128)(2,1)S(1)} collective-permute-done((f16[512,256]{1,0:T(8,128)(2,1)S(1)}, f16[512,256]{1,0:T(8,128)(2,1)S(1)}, u32[]{:S(2)}, u32[]{:S(2)}) %collective-permute-start.19) | collective-permute-done | bytes 262176 | tf_op jit(solution)/shard_map/ppermute | solution.py:50
  99.1 5.0 %collective-permute-done.18 = f16[512,256]{1,0:T(8,128)(2,1)S(1)} collective-permute-done((f16[512,256]{1,0:T(8,128)(2,1)S(1)}, f16[512,256]{1,0:T(8,128)(2,1)S(1)}, u32[]{:S(2)}, u32[]{:S(2)}) %collective-permute-start.18) | collective-permute-done | bytes 262176 | tf_op jit(solution)/shard_map/ppermute | solution.py:50
  104.2 1.9 %collective-permute-done.17 = f16[512,256]{1,0:T(8,128)(2,1)S(1)} collective-permute-done((f16[512,256]{1,0:T(8,128)(2,1)S(1)}, f16[512,256]{1,0:T(8,128)(2,1)S(1)}, u32[]{:S(2)}, u32[]{:S(2)}) %collective-permute-start.17) | collective-permute-done | bytes 262176 | tf_op jit(solution)/shard_map/ppermute | solution.py:50
  106.3 1.1 collective-permute-start.20
  107.4 6.4 %collective-permute-done.20 = f16[512,256]{1,0:T(8,128)(2,1)S(1)} collective-permute-done((f16[512,256]{1,0:T(8,128)(2,1)S(1)}, f16[512,256]{1,0:T(8,128)(2,1)S(1)}, u32[]{:S(2)}, u32[]{:S(2)}) %collective-permute-start.20) | collective-permute-done | bytes 262176 | tf_op jit(solution)/shard_map/ppermute | solution.py:55
  114.0 5.9 %collective-permute-start.21 = (f16[512,256]{1,0:T(8,128)(2,1)S(1)}, f16[512,256]{1,0:T(8,128)(2,1)S(1)}, u32[]{:S(2)}, u32[]{:S(2)}) collective-permute-start(f16[512,256]{1,0:T(8,128)(2,1)S(1)} %add_convert_fusion), channel_id=1, source_target_pairs={{0,19},{8,27},{16,5},{24,13},{4,116},{12,124},{20,20},{28,28},{1,2... | collective-permute-start | bytes 786440 | tf_op jit(solution)/shard_map/ppermute | solution.py:69
  120.0 7.4 %collective-permute-done.21 = f16[512,256]{1,0:T(8,128)(2,1)S(1)} collective-permute-done((f16[512,256]{1,0:T(8,128)(2,1)S(1)}, f16[512,256]{1,0:T(8,128)(2,1)S(1)}, u32[]{:S(2)}, u32[]{:S(2)}) %collective-permute-start.21) | collective-permute-done | bytes 262176 | tf_op jit(solution)/shard_map/ppermute | solution.py:69
  127.4 0.8 convert_multiply_fusion
  (33 shorter events, 0.9 us)
Async XLA Ops:
  0.0 24.6 %copy-start = (bf16[1536,512]{1,0:T(8,128)(2,1)S(1)}, bf16[1536,512]{1,0:T(8,128)(2,1)}, u32[]{:S(2)}) copy-start(bf16[1536,512]{1,0:T(8,128)(2,1)} %refs_2_.5) | copy-start | bytes 4718596
  0.0 24.1 %copy-start.8 = (f32[128]{0:T(128)S(1)}, f32[128]{0:T(128)}, u32[]{:S(2)}) copy-start(f32[128]{0:T(128)} %param.8) | copy-start | bytes 1540
  0.0 24.1 %copy-start.6 = (s32[1536]{0:T(1024)S(1)}, s32[1536]{0:T(1024)}, u32[]{:S(2)}) copy-start(s32[1536]{0:T(1024)} %param.6) | copy-start | bytes 18436
  4.1 19.2 %copy-start.5 = (bf16[384,512]{1,0:T(8,128)(2,1)}, bf16[384,512]{1,0:T(8,128)(2,1)S(1)}, u32[]{:S(2)}) copy-start(bf16[384,512]{1,0:T(8,128)(2,1)S(1)} %get-tuple-element.50) | copy-start | bytes 1179652
  4.1 10.8 %collective-permute-start = (bf16[384,512]{1,0:T(8,128)(2,1)}, bf16[384,512]{1,0:T(8,128)(2,1)S(1)}, u32[]{:S(2)}, u32[]{:S(2)}) collective-permute-start(bf16[384,512]{1,0:T(8,128)(2,1)} %get-tuple-element.51), channel_id=1, source_target_pairs={{0,3},{8,11},{16,19},{24,27},{4,7},{12,15},{20,23},{28,31},{1,0},{... | collective-permute-start | bytes 1179656 | tf_op jit(solution)/shard_map/ppermute | solution.py:50
  6.8 16.4 %collective-permute-start.1 = (bf16[384,512]{1,0:T(8,128)(2,1)S(1)}, bf16[384,512]{1,0:T(8,128)(2,1)S(1)}, u32[]{:S(2)}, u32[]{:S(2)}) collective-permute-start(bf16[384,512]{1,0:T(8,128)(2,1)S(1)} %get-tuple-element.50), channel_id=1, source_target_pairs={{0,3},{8,11},{16,19},{24,27},{4,7},{12,15},{20,23},{28,31},{1,0},{... | collective-permute-start | bytes 1179656 | tf_op jit(solution)/shard_map/ppermute | solution.py:50
  7.3 20.2 %collective-permute-start.2 = (bf16[384,512]{1,0:T(8,128)(2,1)}, bf16[384,512]{1,0:T(8,128)(2,1)S(1)}, u32[]{:S(2)}, u32[]{:S(2)}) collective-permute-start(bf16[384,512]{1,0:T(8,128)(2,1)} %get-tuple-element.51), channel_id=1, source_target_pairs={{0,1},{8,9},{16,17},{24,25},{4,5},{12,13},{20,21},{28,29},{1,2},{9... | collective-permute-start | bytes 1179656 | tf_op jit(solution)/shard_map/ppermute | solution.py:50
  8.3 23.5 %collective-permute-start.4 = (bf16[384,512]{1,0:T(8,128)(2,1)}, bf16[384,512]{1,0:T(8,128)(2,1)S(1)}, u32[]{:S(2)}, u32[]{:S(2)}) collective-permute-start(bf16[384,512]{1,0:T(8,128)(2,1)} %slice.60), channel_id=1, source_target_pairs={{0,3},{8,11},{16,19},{24,27},{4,7},{12,15},{20,23},{28,31},{1,0},{... | collective-permute-start | bytes 1179656 | tf_op jit(solution)/shard_map/ppermute | solution.py:50
  10.0 33.9 %collective-permute-start.6 = (bf16[384,512]{1,0:T(8,128)(2,1)}, bf16[384,512]{1,0:T(8,128)(2,1)}, u32[]{:S(2)}, u32[]{:S(2)}) collective-permute-start(bf16[384,512]{1,0:T(8,128)(2,1)} %slice.60), channel_id=1, source_target_pairs={{0,1},{8,9},{16,17},{24,25},{4,5},{12,13},{20,21},{28,29},{1,2},{9... | collective-permute-start | bytes 1179656 | tf_op jit(solution)/shard_map/ppermute | solution.py:50
  14.9 25.3 %collective-permute-start.5 = (bf16[384,512]{1,0:T(8,128)(2,1)}, bf16[384,512]{1,0:T(8,128)(2,1)S(1)}, u32[]{:S(2)}, u32[]{:S(2)}) collective-permute-start(bf16[384,512]{1,0:T(8,128)(2,1)} %get-tuple-element.49), channel_id=1, source_target_pairs={{0,3},{8,11},{16,19},{24,27},{4,7},{12,15},{20,23},{28,31},{1,0},{... | collective-permute-start | bytes 1179656 | tf_op jit(solution)/shard_map/ppermute | solution.py:50
  23.3 20.6 %collective-permute-start.7 = (bf16[384,512]{1,0:T(8,128)(2,1)}, bf16[384,512]{1,0:T(8,128)(2,1)}, u32[]{:S(2)}, u32[]{:S(2)}) collective-permute-start(bf16[384,512]{1,0:T(8,128)(2,1)} %get-tuple-element.49), channel_id=1, source_target_pairs={{0,1},{8,9},{16,17},{24,25},{4,5},{12,13},{20,21},{28,29},{1,2},{9... | collective-permute-start | bytes 1179656 | tf_op jit(solution)/shard_map/ppermute | solution.py:50
  24.6 1.6 %copy-start.7 = (s32[1536]{0:T(1024)S(1)}, s32[1536]{0:T(1024)}, u32[]{:S(2)}) copy-start(s32[1536]{0:T(1024)} %param.7) | copy-start | bytes 18436
  27.5 24.4 %collective-permute-start.3 = (bf16[384,512]{1,0:T(8,128)(2,1)}, bf16[384,512]{1,0:T(8,128)(2,1)S(1)}, u32[]{:S(2)}, u32[]{:S(2)}) collective-permute-start(bf16[384,512]{1,0:T(8,128)(2,1)} %copy-done.5), channel_id=1, source_target_pairs={{0,1},{8,9},{16,17},{24,25},{4,5},{12,13},{20,21},{28,29},{1,2},{9... | collective-permute-start | bytes 1179656 | tf_op jit(solution)/shard_map/ppermute | solution.py:50
  31.8 27.2 %collective-permute-start.12 = (bf16[384,512]{1,0:T(8,128)(2,1)S(1)}, bf16[384,512]{1,0:T(8,128)(2,1)S(1)}, u32[]{:S(2)}, u32[]{:S(2)}) collective-permute-start(bf16[384,512]{1,0:T(8,128)(2,1)S(1)} %collective-permute-done.4.refs_3_), channel_id=1, source_target_pairs={{0,4},{8,12},{16,20},{24,28},{4,0},{12,8},{20,16},{28,24},{1,5},{9... | collective-permute-start | bytes 1179656 | tf_op jit(solution)/shard_map/ppermute | solution.py:50
  40.2 18.8 %collective-permute-start.13 = (bf16[384,512]{1,0:T(8,128)(2,1)S(1)}, bf16[384,512]{1,0:T(8,128)(2,1)S(1)}, u32[]{:S(2)}, u32[]{:S(2)}) collective-permute-start(bf16[384,512]{1,0:T(8,128)(2,1)S(1)} %collective-permute-done.5.refs_4_), channel_id=1, source_target_pairs={{0,4},{8,12},{16,20},{24,28},{4,0},{12,8},{20,16},{28,24},{1,5},{9... | collective-permute-start | bytes 1179656 | tf_op jit(solution)/shard_map/ppermute | solution.py:50
  43.8 16.4 %collective-permute-start.14 = (bf16[384,512]{1,0:T(8,128)(2,1)S(1)}, bf16[384,512]{1,0:T(8,128)(2,1)S(1)}, u32[]{:S(2)}, u32[]{:S(2)}) collective-permute-start(bf16[384,512]{1,0:T(8,128)(2,1)S(1)} %collective-permute-done.refs_3_.refs_5_), channel_id=1, source_target_pairs={{0,4},{8,12},{16,20},{24,28},{4,0},{12,8},{20,16},{28,24},{1,5},{9... | collective-permute-start | bytes 1179656 | tf_op jit(solution)/shard_map/ppermute | solution.py:50
  43.8 24.8 %collective-permute-start.15 = (bf16[384,512]{1,0:T(8,128)(2,1)S(1)}, bf16[384,512]{1,0:T(8,128)(2,1)S(1)}, u32[]{:S(2)}, u32[]{:S(2)}) collective-permute-start(bf16[384,512]{1,0:T(8,128)(2,1)S(1)} %collective-permute-done.1.refs_4_.refs_6_), channel_id=1, source_target_pairs={{0,4},{8,12},{16,20},{24,28},{4,0},{12,8},{20,16},{28,24},{1,5},{9... | collective-permute-start | bytes 1179656 | tf_op jit(solution)/shard_map/ppermute | solution.py:50
  55.0 1.6 %copy-start.1 = (f32[4,512,256]{2,1,0:T(8,128)}, f32[4,512,256]{2,1,0:T(8,128)S(1)}, u32[]{:S(2)}) copy-start(f32[4,512,256]{2,1,0:T(8,128)S(1)} %get-tuple-element.27) | copy-start | bytes 6291460
  56.6 21.2 %collective-permute-start.8 = (f16[4,512,256]{2,1,0:T(8,128)(2,1)}, f16[4,512,256]{2,1,0:T(8,128)(2,1)}, u32[]{:S(2)}, u32[]{:S(2)}) collective-permute-start(f16[4,512,256]{2,1,0:T(8,128)(2,1)} %convert_element_type.119), channel_id=1, source_target_pairs={{0,8},{8,0},{16,24},{24,16},{4,12},{12,4},{20,28},{28,20},{1,9},{9... | collective-permute-start | bytes 3145736 | tf_op jit(solution)/shard_map/ppermute | solution.py:50
  74.0 1.7 %copy-start.3 = (f32[4,512,256]{2,1,0:T(8,128)}, f32[4,512,256]{2,1,0:T(8,128)S(1)}, u32[]{:S(2)}) copy-start(f32[4,512,256]{2,1,0:T(8,128)S(1)} %get-tuple-element.35) | copy-start | bytes 6291460
  74.0 3.8 %copy-start.2 = (f32[4,512,256]{2,1,0:T(8,128)S(1)}, f32[4,512,256]{2,1,0:T(8,128)}, u32[]{:S(2)}) copy-start(f32[4,512,256]{2,1,0:T(8,128)} %copy-done.1) | copy-start | bytes 6291460
  75.7 5.9 %collective-permute-start.16 = (f16[4,512,256]{2,1,0:T(8,128)(2,1)}, f16[4,512,256]{2,1,0:T(8,128)(2,1)S(1)}, u32[]{:S(2)}, u32[]{:S(2)}) collective-permute-start(f16[4,512,256]{2,1,0:T(8,128)(2,1)} %convert_element_type.133), channel_id=1, source_target_pairs={{0,8},{8,0},{16,24},{24,16},{4,12},{12,4},{20,28},{28,20},{1,9},{9... | collective-permute-start | bytes 3145736 | tf_op jit(solution)/shard_map/ppermute | solution.py:50
  77.8 3.8 %copy-start.4 = (f32[4,512,256]{2,1,0:T(8,128)S(1)}, f32[4,512,256]{2,1,0:T(8,128)}, u32[]{:S(2)}) copy-start(f32[4,512,256]{2,1,0:T(8,128)} %copy-done.3) | copy-start | bytes 6291460
  79.4 8.4 %collective-permute-start.11 = (f16[512,256]{1,0:T(8,128)(2,1)S(1)}, f16[512,256]{1,0:T(8,128)(2,1)S(1)}, u32[]{:S(2)}, u32[]{:S(2)}) collective-permute-start(f16[512,256]{1,0:T(8,128)(2,1)S(1)} %get-tuple-element.32), channel_id=1, source_target_pairs={{0,64},{8,72},{16,80},{24,88},{4,68},{12,76},{20,84},{28,92},{1,65... | collective-permute-start | bytes 786440 | tf_op jit(solution)/shard_map/ppermute | solution.py:50
  79.7 14.1 %collective-permute-start.10 = (f16[512,256]{1,0:T(8,128)(2,1)S(1)}, f16[512,256]{1,0:T(8,128)(2,1)S(1)}, u32[]{:S(2)}, u32[]{:S(2)}) collective-permute-start(f16[512,256]{1,0:T(8,128)(2,1)S(1)} %get-tuple-element.31), channel_id=1, source_target_pairs={{0,96},{8,104},{16,112},{24,120},{4,100},{12,108},{20,116},{28,124... | collective-permute-start | bytes 786440 | tf_op jit(solution)/shard_map/ppermute | solution.py:50
  81.6 14.6 %collective-permute-start.9 = (f16[512,256]{1,0:T(8,128)(2,1)S(1)}, f16[512,256]{1,0:T(8,128)(2,1)S(1)}, u32[]{:S(2)}, u32[]{:S(2)}) collective-permute-start(f16[512,256]{1,0:T(8,128)(2,1)S(1)} %get-tuple-element.30), channel_id=1, source_target_pairs={{0,32},{8,40},{16,48},{24,56},{4,36},{12,44},{20,52},{28,60},{1,33... | collective-permute-start | bytes 786440 | tf_op jit(solution)/shard_map/ppermute | solution.py:50
  82.0 17.1 %collective-permute-start.19 = (f16[512,256]{1,0:T(8,128)(2,1)S(1)}, f16[512,256]{1,0:T(8,128)(2,1)S(1)}, u32[]{:S(2)}, u32[]{:S(2)}) collective-permute-start(f16[512,256]{1,0:T(8,128)(2,1)S(1)} %get-tuple-element.40), channel_id=1, source_target_pairs={{0,64},{8,72},{16,80},{24,88},{4,68},{12,76},{20,84},{28,92},{1,65... | collective-permute-start | bytes 786440 | tf_op jit(solution)/shard_map/ppermute | solution.py:50
  84.4 19.8 %collective-permute-start.18 = (f16[512,256]{1,0:T(8,128)(2,1)S(1)}, f16[512,256]{1,0:T(8,128)(2,1)S(1)}, u32[]{:S(2)}, u32[]{:S(2)}) collective-permute-start(f16[512,256]{1,0:T(8,128)(2,1)S(1)} %get-tuple-element.39), channel_id=1, source_target_pairs={{0,96},{8,104},{16,112},{24,120},{4,100},{12,108},{20,116},{28,124... | collective-permute-start | bytes 786440 | tf_op jit(solution)/shard_map/ppermute | solution.py:50
  87.8 18.2 %collective-permute-start.17 = (f16[512,256]{1,0:T(8,128)(2,1)S(1)}, f16[512,256]{1,0:T(8,128)(2,1)S(1)}, u32[]{:S(2)}, u32[]{:S(2)}) collective-permute-start(f16[512,256]{1,0:T(8,128)(2,1)S(1)} %get-tuple-element.38), channel_id=1, source_target_pairs={{0,32},{8,40},{16,48},{24,56},{4,36},{12,44},{20,52},{28,60},{1,33... | collective-permute-start | bytes 786440 | tf_op jit(solution)/shard_map/ppermute | solution.py:50
  106.3 7.5 %collective-permute-start.20 = (f16[512,256]{1,0:T(8,128)(2,1)S(1)}, f16[512,256]{1,0:T(8,128)(2,1)S(1)}, u32[]{:S(2)}, u32[]{:S(2)}) collective-permute-start(f16[512,256]{1,0:T(8,128)(2,1)S(1)} %select_convert_fusion), channel_id=1, source_target_pairs={{0,16},{8,24},{16,0},{24,8},{4,20},{12,28},{20,4},{28,12},{1,17},{... | collective-permute-start | bytes 786440 | tf_op jit(solution)/shard_map/ppermute | solution.py:55
  114.0 13.4 %collective-permute-start.21 = (f16[512,256]{1,0:T(8,128)(2,1)S(1)}, f16[512,256]{1,0:T(8,128)(2,1)S(1)}, u32[]{:S(2)}, u32[]{:S(2)}) collective-permute-start(f16[512,256]{1,0:T(8,128)(2,1)S(1)} %add_convert_fusion), channel_id=1, source_target_pairs={{0,19},{8,27},{16,5},{24,13},{4,116},{12,124},{20,20},{28,28},{1,2... | collective-permute-start | bytes 786440 | tf_op jit(solution)/shard_map/ppermute | solution.py:69

commit v3 on v2

--- a/solution.py
+++ b/solution.py
@@ -18,14 +18,14 @@
 EARLY = ((O, O), (O, N), (O, S), (S, N))
 LATE = ((O, Z), (Z, O), (Z, N), (S, Z))
 PLAN = (
-    ((3, 0, 2, 1), (1, 0, 3, 2), (0, 0, 1, 1)),
-    ((2, 3, 1, 0), (1, 2, 3, 0), (1, 0, 0, 1)),
-    ((1, 0, 3, 2), (3, 1, 2, 0), (0, 0, 1, 1)),
-    ((1, 2, 0, 3), (2, 1, 3, 0), (0, 0, 1, 0)),
-    ((2, 3, 1, 0), (0, 1, 2, 3), (0, 0, 1, 0)),
-    ((1, 2, 0, 3), (3, 0, 1, 2), (1, 1, 1, 0)),
-    ((1, 0, 2, 3), (0, 3, 1, 2), (1, 0, 0, 1)),
-    ((0, 3, 1, 2), (0, 3, 2, 1), (1, 1, 0, 1)),
+    ((3, 0, 2, 1), (2, 1, 0, 3), (1, 0, 1, 0)),
+    ((2, 3, 1, 0), (1, 2, 0, 3), (1, 0, 0, 1)),
+    ((0, 3, 1, 2), (0, 1, 2, 3), (0, 0, 1, 0)),
+    ((3, 2, 0, 1), (2, 1, 3, 0), (0, 1, 1, 1)),
+    ((2, 1, 3, 0), (3, 0, 2, 1), (1, 1, 1, 0)),
+    ((1, 0, 2, 3), (0, 3, 1, 2), (1, 1, 1, 0)),
+    ((1, 2, 0, 3), (2, 3, 0, 1), (1, 0, 0, 0)),
+    ((0, 1, 3, 2), (3, 0, 2, 1), (1, 1, 0, 1)),
 )
 
 
@@ -99,6 +99,7 @@
 
 
 COUNT = len(CUTS)
+TAIL = (256, 512)
 SPLIT = 2
 
 
@@ -237,15 +238,22 @@
     )
     late, late_got = over_x(*late)
 
-    early = early + sum(g.astype(jnp.float32) for g in early_got)
-    early = lax.optimization_barrier(early)
-    late = late + sum(g.astype(jnp.float32) for g in late_got)
+    def sum_of(kept, got):
+        return kept + sum(g.astype(jnp.float32) for g in got)
+
+    early = lax.optimization_barrier(sum_of(early, early_got))
+    late = sum_of(late, late_got)
     keeps = planned(pair, ga)[2]
     kept = jnp.where(keeps, early, late)
-    got = swap_z_lo(jnp.where(keeps, late, early).astype(jnp.float16))
-    total = kept + got.astype(jnp.float32)
-    total = to_owner(total.astype(jnp.float16))
-    return total.astype(jnp.float32) * (1.0 / GAIN)
+    sent = jnp.where(keeps, late, early).astype(jnp.float16)
+    parts, edges, total = [], (0, *TAIL), None
+    for h, part in enumerate(slice(u, v) for u, v in zip(edges, edges[1:])):
+        got = swap_z_lo(sent[part])
+        if h:
+            got = lax.optimization_barrier((got, total))[0]
+        total = (kept[part] + got.astype(jnp.float32)).astype(jnp.float16)
+        parts.append(to_owner(total))
+    return jnp.concatenate(parts, 0).astype(jnp.float32) * (1.0 / GAIN)
 
 
 def solution(mesh):

time: 130 us -> 128 us (0.985)
  starting transfers between devices: 40.1 us -> 35.8 us
  waiting for transfers between devices: 60.4 us -> 62.8 us
    ppermute x1 -> x2, starting transfers between devices: 5.94 us -> 1.23 us  [to_owner(): return lax.ppermute(value, AXES, pairs)]
    ppermute x1 -> x2, waiting for transfers between devices: 7.44 us -> 10.3 us  [to_owner(): return lax.ppermute(value, AXES, pairs)]
    ppermute x1 -> x2, waiting for transfers between devices: 6.36 us -> 5.85 us  [swap_z_lo(): return lax.ppermute(value, AXES, pairs)]
  transfers between devices with their start and end apart: 22 -> 24, of which waited for: 14 -> 16; matrix products, arithmetic and copies ran while one was open for 7% -> 8% of each run, Pallas kernels for 9% -> 9%
where the time goes in v3:
time: 128 us; the launch traced here: 126 us
  waiting for transfers between devices  62.8 us (49%)
  starting transfers between devices  35.8 us (28%)
  Pallas kernels  11.9 us (9%)
  other arithmetic  9.18 us (7%)
  local copies, waits for them, and re-layouts  6.49 us (5%)
    ppermute x20, waiting for transfers between devices, shift(): return lax.ppermute(value, AXES, pairs)  46.6 us
    ppermute x20, starting transfers between devices, shift(): return lax.ppermute(value, AXES, pairs)  33 us
    pallas_call x3, Pallas kernels, run_stage(): pl.pallas_call(functools.partial(stage_kernel, late, lo, hi, len(sources)...  11.9 us
    ppermute x2, waiting for transfers between devices, to_owner(): return lax.ppermute(value, AXES, pairs)  10.3 us
    ppermute x2, waiting for transfers between devices, swap_z_lo(): return lax.ppermute(value, AXES, pairs)  5.85 us
    slice x2, local copies, waits for them, and re-layouts, rows(): return block[starts[k]:starts[k + 1]]  4.09 us
    convert_element_type x2, other arithmetic, over_x(): theirs = shift(theirs.astype(jnp.float16), swap=True)  2.57 us
  transfers between devices with their start and end apart: 24, of which 16 were waited for; matrix products, arithmetic and copies ran while one was open for 8% of the time, Pallas kernels for 9%

profile of v3, /device:TPU:5, one launch (start us, length us, event | category | flops | bytes accessed | tf_op | source)
XLA Modules:
  0.0 126.3 jit_solution(2300986783877265821)
XLA Ops:
  0.0 1.9 %slice.72 = bf16[384,512]{1,0:T(8,128)(2,1)} slice(bf16[1536,512]{1,0:T(8,128)(2,1)} %refs_2_.5), slice={[0:384], [0:512]} | slice | bytes 786432 | tf_op jit(solution)/shard_map/slice | solution.py:201
  1.9 2.2 %fusion.9 = (bf16[384,512]{1,0:T(8,128)(2,1)}, bf16[384,512]{1,0:T(8,128)(2,1)S(1)}, bf16[384,512]{1,0:T(8,128)(2,1)}) fusion(bf16[1536,512]{1,0:T(8,128)(2,1)} %refs_2_.5), kind=kLoop, calls=%fused_computation.30 | loop fusion | bytes 2359296 | tf_op jit(solution)/shard_map/slice | solution.py:201
  4.1 2.7 %collective-permute-start = (bf16[384,512]{1,0:T(8,128)(2,1)}, bf16[384,512]{1,0:T(8,128)(2,1)S(1)}, u32[]{:S(2)}, u32[]{:S(2)}) collective-permute-start(bf16[384,512]{1,0:T(8,128)(2,1)} %get-tuple-element.55), channel_id=1, source_target_pairs={{0,3},{8,11},{16,19},{24,27},{4,7},{12,15},{20,23},{28,31},{1,0},{... | collective-permute-start | bytes 1179656 | tf_op jit(solution)/shard_map/ppermute | solution.py:50
  6.8 0.5 collective-permute-start.1
  7.3 1.0 collective-permute-start.2
  8.3 1.7 %collective-permute-start.4 = (bf16[384,512]{1,0:T(8,128)(2,1)}, bf16[384,512]{1,0:T(8,128)(2,1)S(1)}, u32[]{:S(2)}, u32[]{:S(2)}) collective-permute-start(bf16[384,512]{1,0:T(8,128)(2,1)} %slice.72), channel_id=1, source_target_pairs={{0,3},{8,11},{16,19},{24,27},{4,7},{12,15},{20,23},{28,31},{1,0},{... | collective-permute-start | bytes 1179656 | tf_op jit(solution)/shard_map/ppermute | solution.py:50
  10.0 5.0 %collective-permute-done.refs_3_.refs_5_ = bf16[384,512]{1,0:T(8,128)(2,1)S(1)} collective-permute-done((bf16[384,512]{1,0:T(8,128)(2,1)}, bf16[384,512]{1,0:T(8,128)(2,1)S(1)}, u32[]{:S(2)}, u32[]{:S(2)}) %collective-permute-start) | collective-permute-done | bytes 393248 | tf_op jit(solution)/shard_map/ppermute | solution.py:50
  15.0 3.3 %collective-permute-start.5 = (bf16[384,512]{1,0:T(8,128)(2,1)}, bf16[384,512]{1,0:T(8,128)(2,1)S(1)}, u32[]{:S(2)}, u32[]{:S(2)}) collective-permute-start(bf16[384,512]{1,0:T(8,128)(2,1)} %get-tuple-element.53), channel_id=1, source_target_pairs={{0,3},{8,11},{16,19},{24,27},{4,7},{12,15},{20,23},{28,31},{1,0},{... | collective-permute-start | bytes 1179656 | tf_op jit(solution)/shard_map/ppermute | solution.py:50
  18.3 5.0 %collective-permute-done.1.refs_4_.refs_6_ = bf16[384,512]{1,0:T(8,128)(2,1)S(1)} collective-permute-done((bf16[384,512]{1,0:T(8,128)(2,1)S(1)}, bf16[384,512]{1,0:T(8,128)(2,1)S(1)}, u32[]{:S(2)}, u32[]{:S(2)}) %collective-permute-start.1) | collective-permute-done | bytes 393248 | tf_op jit(solution)/shard_map/ppermute | solution.py:50
  23.3 0.9 collective-permute-start.7
  24.1 0.5 select_reduce_fusion.1
  24.7 1.6 %copy.7 = bf16[1536,512]{0,1:T(8,128)(2,1)} copy(bf16[1536,512]{1,0:T(8,128)(2,1)S(1)} %copy-done) | data formatting | bytes 3145728 | tf_op args[0]
  26.3 1.2 select_reduce_fusion
  27.5 1.4 %collective-permute-start.3 = (bf16[384,512]{1,0:T(8,128)(2,1)}, bf16[384,512]{1,0:T(8,128)(2,1)S(1)}, u32[]{:S(2)}, u32[]{:S(2)}) collective-permute-start(bf16[384,512]{1,0:T(8,128)(2,1)} %copy-done.5), channel_id=1, source_target_pairs={{0,1},{8,9},{16,17},{24,25},{4,5},{12,13},{20,21},{28,29},{1,2},{9... | collective-permute-start | bytes 1179656 | tf_op jit(solution)/shard_map/ppermute | solution.py:50
  28.8 3.0 %collective-permute-done.4.refs_3_ = bf16[384,512]{1,0:T(8,128)(2,1)S(1)} collective-permute-done((bf16[384,512]{1,0:T(8,128)(2,1)}, bf16[384,512]{1,0:T(8,128)(2,1)S(1)}, u32[]{:S(2)}, u32[]{:S(2)}) %collective-permute-start.4) | collective-permute-done | bytes 393248 | tf_op jit(solution)/shard_map/ppermute | solution.py:50
  31.8 3.6 %collective-permute-start.12 = (bf16[384,512]{1,0:T(8,128)(2,1)S(1)}, bf16[384,512]{1,0:T(8,128)(2,1)S(1)}, u32[]{:S(2)}, u32[]{:S(2)}) collective-permute-start(bf16[384,512]{1,0:T(8,128)(2,1)S(1)} %collective-permute-done.4.refs_3_), channel_id=1, source_target_pairs={{0,4},{8,12},{16,20},{24,28},{4,0},{12,8},{20,16},{28,24},{1,5},{9... | collective-permute-start | bytes 1179656 | tf_op jit(solution)/shard_map/ppermute | solution.py:50
  35.4 4.8 %collective-permute-done.5.refs_4_ = bf16[384,512]{1,0:T(8,128)(2,1)S(1)} collective-permute-done((bf16[384,512]{1,0:T(8,128)(2,1)}, bf16[384,512]{1,0:T(8,128)(2,1)S(1)}, u32[]{:S(2)}, u32[]{:S(2)}) %collective-permute-start.5) | collective-permute-done | bytes 393248 | tf_op jit(solution)/shard_map/ppermute | solution.py:50
  40.2 3.6 %collective-permute-start.13 = (bf16[384,512]{1,0:T(8,128)(2,1)S(1)}, bf16[384,512]{1,0:T(8,128)(2,1)S(1)}, u32[]{:S(2)}, u32[]{:S(2)}) collective-permute-start(bf16[384,512]{1,0:T(8,128)(2,1)S(1)} %collective-permute-done.5.refs_4_), channel_id=1, source_target_pairs={{0,4},{8,12},{16,20},{24,28},{4,0},{12,8},{20,16},{28,24},{1,5},{9... | collective-permute-start | bytes 1179656 | tf_op jit(solution)/shard_map/ppermute | solution.py:50
  43.9 3.0 %collective-permute-start.15 = (bf16[384,512]{1,0:T(8,128)(2,1)S(1)}, bf16[384,512]{1,0:T(8,128)(2,1)S(1)}, u32[]{:S(2)}, u32[]{:S(2)}) collective-permute-start(bf16[384,512]{1,0:T(8,128)(2,1)S(1)} %collective-permute-done.1.refs_4_.refs_6_), channel_id=1, source_target_pairs={{0,4},{8,12},{16,20},{24,28},{4,0},{12,8},{20,16},{28,24},{1,5},{9... | collective-permute-start | bytes 1179656 | tf_op jit(solution)/shard_map/ppermute | solution.py:50
  46.8 1.7 %fusion.refs_1_ = bf16[512,1536]{1,0:T(8,128)(2,1)S(1)} fusion(bf16[1536,512]{0,1:T(8,128)(2,1)} %copy.7, f32[1536]{0:T(1024)S(1)} %multiply_divide_fusion), kind=kLoop, calls=%fused_computation.1 | loop fusion | flops 2359296 | bytes 3151872 | tf_op jit(solution)/shard_map/convert_element_type | solution.py:226
  48.5 3.5 %shard_map.55 = (f32[4,512,512]{2,1,0:T(8,128)S(1)}, bf16[512,768]{1,0:T(8,128)(2,1)S(1)}) custom-call(f32[1,1536]{1,0:T(1,128)S(1)} %div.19.refs_0_, bf16[512,1536]{1,0:T(8,128)(2,1)S(1)} %fusion.refs_1_, bf16[1536,512]{1,0:T(8,128)(2,1)S(1)} %copy-done, bf16[384,512]{1,0:T(8,128)(2,1)S(1)} %collective-permute-done.4.refs_3_, ...), custom_call_target="tpu_custom_call" | custom-call | flops 1610612736 | bytes 8388608 | tf_op jit(solution)/shard_map/pallas_call | solution.py:179
  52.0 3.0 %shard_map.56 = (f32[4,512,256]{2,1,0:T(8,128)S(1)}, f32[4,512,256]{2,1,0:T(8,128)S(1)}, bf16[512,768]{1,0:T(8,128)(2,1)S(1)}) custom-call(f32[1,1536]{1,0:T(1,128)S(1)} %div.19.refs_0_, bf16[512,1536]{1,0:T(8,128)(2,1)S(1)} %fusion.refs_1_, bf16[1536,512]{1,0:T(8,128)(2,1)S(1)} %copy-done, bf16[384,512]{1,0:T(8,128)(2,1)S(1)} %collective-permute-done.refs_3_.refs_5_, ...), custom_call_target="tpu_custom_call" | custom-call | flops 1610612736 | bytes 8388608 | tf_op jit(solution)/shard_map/pallas_call | solution.py:179
  55.0 1.4 %convert_element_type.125 = f16[4,512,256]{2,1,0:T(8,128)(2,1)} convert(f32[4,512,256]{2,1,0:T(8,128)S(1)} %get-tuple-element.29) | non-fusion elementwise | flops 524288 | bytes 3145728 | tf_op jit(solution)/shard_map/convert_element_type | solution.py:213
  56.7 2.4 %collective-permute-start.8 = (f16[4,512,256]{2,1,0:T(8,128)(2,1)}, f16[4,512,256]{2,1,0:T(8,128)(2,1)}, u32[]{:S(2)}, u32[]{:S(2)}) collective-permute-start(f16[4,512,256]{2,1,0:T(8,128)(2,1)} %convert_element_type.125), channel_id=1, source_target_pairs={{0,8},{8,0},{16,24},{24,16},{4,12},{12,4},{20,28},{28,20},{1,9},{9... | collective-permute-start | bytes 3145736 | tf_op jit(solution)/shard_map/ppermute | solution.py:50
  59.0 1.2 collective-permute-done.14.refs_9_
  60.2 8.4 %collective-permute-done.15.refs_10_ = bf16[384,512]{1,0:T(8,128)(2,1)S(1)} collective-permute-done((bf16[384,512]{1,0:T(8,128)(2,1)S(1)}, bf16[384,512]{1,0:T(8,128)(2,1)S(1)}, u32[]{:S(2)}, u32[]{:S(2)}) %collective-permute-start.15) | collective-permute-done | bytes 393248 | tf_op jit(solution)/shard_map/ppermute | solution.py:50
  68.6 5.4 %shard_map.57 = (f32[4,512,256]{2,1,0:T(8,128)S(1)}, f32[4,512,256]{2,1,0:T(8,128)S(1)}) custom-call(f32[1,1536]{1,0:T(1,128)S(1)} %div.19.refs_0_, bf16[512,1536]{1,0:T(8,128)(2,1)S(1)} %fusion.refs_1_, bf16[1536,512]{1,0:T(8,128)(2,1)S(1)} %copy-done, bf16[384,512]{1,0:T(8,128)(2,1)S(1)} %collective-permute-done.4.refs_3_, ...), custom_call_target="tpu_custom_call" | custom-call | flops 3221225472 | bytes 8388608 | tf_op jit(solution)/shard_map/pallas_call | solution.py:179
  74.1 1.2 convert_element_type.139
  75.2 0.5 copy-done.3
  75.7 2.1 %collective-permute-start.16 = (f16[4,512,256]{2,1,0:T(8,128)(2,1)}, f16[4,512,256]{2,1,0:T(8,128)(2,1)S(1)}, u32[]{:S(2)}, u32[]{:S(2)}) collective-permute-start(f16[4,512,256]{2,1,0:T(8,128)(2,1)} %convert_element_type.139), channel_id=1, source_target_pairs={{0,8},{8,0},{16,24},{24,16},{4,12},{12,4},{20,28},{28,20},{1,9},{9... | collective-permute-start | bytes 3145736 | tf_op jit(solution)/shard_map/ppermute | solution.py:50
  77.8 1.6 %fusion.3 = (f16[512,256]{1,0:T(8,128)(2,1)S(1)}, f16[512,256]{1,0:T(8,128)(2,1)S(1)}, f16[512,256]{1,0:T(8,128)(2,1)S(1)}, f32[512,256]{1,0:T(8,128)S(1)}) fusion(f32[4,512,256]{2,1,0:T(8,128)S(1)} %copy-done.2, f16[4,512,256]{2,1,0:T(8,128)(2,1)} %collective-permute-done.8), kind=kLoop, calls=%fused_computation.20 | loop fusion | flops 1441792 | bytes 4456448 | tf_op jit(solution)/shard_map/convert_element_type | solution.py:216
  79.8 1.9 %collective-permute-start.10 = (f16[512,256]{1,0:T(8,128)(2,1)S(1)}, f16[512,256]{1,0:T(8,128)(2,1)S(1)}, u32[]{:S(2)}, u32[]{:S(2)}) collective-permute-start(f16[512,256]{1,0:T(8,128)(2,1)S(1)} %get-tuple-element.32), channel_id=1, source_target_pairs={{0,96},{8,104},{16,112},{24,120},{4,100},{12,108},{20,116},{28,124... | collective-permute-start | bytes 786440 | tf_op jit(solution)/shard_map/ppermute | solution.py:50
  82.0 2.4 %collective-permute-start.19 = (f16[512,256]{1,0:T(8,128)(2,1)S(1)}, f16[512,256]{1,0:T(8,128)(2,1)S(1)}, u32[]{:S(2)}, u32[]{:S(2)}) collective-permute-start(f16[512,256]{1,0:T(8,128)(2,1)S(1)} %get-tuple-element.41), channel_id=1, source_target_pairs={{0,64},{8,72},{16,80},{24,88},{4,68},{12,76},{20,84},{28,92},{1,65... | collective-permute-start | bytes 786440 | tf_op jit(solution)/shard_map/ppermute | solution.py:50
  84.4 1.5 %collective-permute-start.18 = (f16[512,256]{1,0:T(8,128)(2,1)S(1)}, f16[512,256]{1,0:T(8,128)(2,1)S(1)}, u32[]{:S(2)}, u32[]{:S(2)}) collective-permute-start(f16[512,256]{1,0:T(8,128)(2,1)S(1)} %get-tuple-element.40), channel_id=1, source_target_pairs={{0,96},{8,104},{16,112},{24,120},{4,100},{12,108},{20,116},{28,124... | collective-permute-start | bytes 786440 | tf_op jit(solution)/shard_map/ppermute | solution.py:50
  85.9 2.0 %collective-permute-done.11 = f16[512,256]{1,0:T(8,128)(2,1)S(1)} collective-permute-done((f16[512,256]{1,0:T(8,128)(2,1)S(1)}, f16[512,256]{1,0:T(8,128)(2,1)S(1)}, u32[]{:S(2)}, u32[]{:S(2)}) %collective-permute-start.11) | collective-permute-done | bytes 262176 | tf_op jit(solution)/shard_map/ppermute | solution.py:50
  87.9 0.9 collective-permute-start.17
  88.8 5.0 %collective-permute-done.10 = f16[512,256]{1,0:T(8,128)(2,1)S(1)} collective-permute-done((f16[512,256]{1,0:T(8,128)(2,1)S(1)}, f16[512,256]{1,0:T(8,128)(2,1)S(1)}, u32[]{:S(2)}, u32[]{:S(2)}) %collective-permute-start.10) | collective-permute-done | bytes 262176 | tf_op jit(solution)/shard_map/ppermute | solution.py:50
  93.8 2.4 %collective-permute-done.9 = f16[512,256]{1,0:T(8,128)(2,1)S(1)} collective-permute-done((f16[512,256]{1,0:T(8,128)(2,1)S(1)}, f16[512,256]{1,0:T(8,128)(2,1)S(1)}, u32[]{:S(2)}, u32[]{:S(2)}) %collective-permute-start.9) | collective-permute-done | bytes 262176 | tf_op jit(solution)/shard_map/ppermute | solution.py:50
  96.4 2.8 %collective-permute-done.19 = f16[512,256]{1,0:T(8,128)(2,1)S(1)} collective-permute-done((f16[512,256]{1,0:T(8,128)(2,1)S(1)}, f16[512,256]{1,0:T(8,128)(2,1)S(1)}, u32[]{:S(2)}, u32[]{:S(2)}) %collective-permute-start.19) | collective-permute-done | bytes 262176 | tf_op jit(solution)/shard_map/ppermute | solution.py:50
  99.2 5.0 %collective-permute-done.18 = f16[512,256]{1,0:T(8,128)(2,1)S(1)} collective-permute-done((f16[512,256]{1,0:T(8,128)(2,1)S(1)}, f16[512,256]{1,0:T(8,128)(2,1)S(1)}, u32[]{:S(2)}, u32[]{:S(2)}) %collective-permute-start.18) | collective-permute-done | bytes 262176 | tf_op jit(solution)/shard_map/ppermute | solution.py:50
  104.2 1.9 %collective-permute-done.17 = f16[512,256]{1,0:T(8,128)(2,1)S(1)} collective-permute-done((f16[512,256]{1,0:T(8,128)(2,1)S(1)}, f16[512,256]{1,0:T(8,128)(2,1)S(1)}, u32[]{:S(2)}, u32[]{:S(2)}) %collective-permute-start.17) | collective-permute-done | bytes 262176 | tf_op jit(solution)/shard_map/ppermute | solution.py:50
  106.4 1.1 collective-permute-start.20
  108.0 3.1 %collective-permute-done.20 = f16[256,256]{1,0:T(8,128)(2,1)S(1)} collective-permute-done((f16[256,256]{1,0:T(8,128)(2,1)S(1)}, f16[256,256]{1,0:T(8,128)(2,1)S(1)}, u32[]{:S(2)}, u32[]{:S(2)}) %collective-permute-start.20) | collective-permute-done | bytes 131104 | tf_op jit(solution)/shard_map/ppermute | solution.py:55
  111.1 2.8 %collective-permute-done.22 = f16[256,256]{1,0:T(8,128)(2,1)S(1)} collective-permute-done((f16[256,256]{1,0:T(8,128)(2,1)S(1)}, f16[256,256]{1,0:T(8,128)(2,1)S(1)}, u32[]{:S(2)}, u32[]{:S(2)}) %collective-permute-start.22) | collective-permute-done | bytes 131104 | tf_op jit(solution)/shard_map/ppermute | solution.py:55
  113.9 1.1 collective-permute-start.23
  115.1 7.3 %collective-permute-done.23 = f16[256,256]{1,0:T(8,128)(2,1)S(1)} collective-permute-done((f16[256,256]{1,0:T(8,128)(2,1)S(1)}, f16[256,256]{1,0:T(8,128)(2,1)S(1)}, u32[]{:S(2)}, u32[]{:S(2)}) %collective-permute-start.23) | collective-permute-done | bytes 131104 | tf_op jit(solution)/shard_map/ppermute | solution.py:69
  122.5 3.0 %collective-permute-done.21 = f16[256,256]{1,0:T(8,128)(2,1)S(1)} collective-permute-done((f16[256,256]{1,0:T(8,128)(2,1)S(1)}, f16[256,256]{1,0:T(8,128)(2,1)S(1)}, u32[]{:S(2)}, u32[]{:S(2)}) %collective-permute-start.21) | collective-permute-done | bytes 131104 | tf_op jit(solution)/shard_map/ppermute | solution.py:69
  125.5 0.8 convert_multiply_fusion
  (39 shorter events, 2.1 us)
Async XLA Ops:
  0.0 24.6 %copy-start = (bf16[1536,512]{1,0:T(8,128)(2,1)S(1)}, bf16[1536,512]{1,0:T(8,128)(2,1)}, u32[]{:S(2)}) copy-start(bf16[1536,512]{1,0:T(8,128)(2,1)} %refs_2_.5) | copy-start | bytes 4718596
  0.0 24.1 %copy-start.8 = (f32[128]{0:T(128)S(1)}, f32[128]{0:T(128)}, u32[]{:S(2)}) copy-start(f32[128]{0:T(128)} %param.8) | copy-start | bytes 1540
  0.0 24.1 %copy-start.6 = (s32[1536]{0:T(1024)S(1)}, s32[1536]{0:T(1024)}, u32[]{:S(2)}) copy-start(s32[1536]{0:T(1024)} %param.6) | copy-start | bytes 18436
  4.1 19.2 %copy-start.5 = (bf16[384,512]{1,0:T(8,128)(2,1)}, bf16[384,512]{1,0:T(8,128)(2,1)S(1)}, u32[]{:S(2)}) copy-start(bf16[384,512]{1,0:T(8,128)(2,1)S(1)} %get-tuple-element.54) | copy-start | bytes 1179652
  4.1 10.8 %collective-permute-start = (bf16[384,512]{1,0:T(8,128)(2,1)}, bf16[384,512]{1,0:T(8,128)(2,1)S(1)}, u32[]{:S(2)}, u32[]{:S(2)}) collective-permute-start(bf16[384,512]{1,0:T(8,128)(2,1)} %get-tuple-element.55), channel_id=1, source_target_pairs={{0,3},{8,11},{16,19},{24,27},{4,7},{12,15},{20,23},{28,31},{1,0},{... | collective-permute-start | bytes 1179656 | tf_op jit(solution)/shard_map/ppermute | solution.py:50
  6.8 16.4 %collective-permute-start.1 = (bf16[384,512]{1,0:T(8,128)(2,1)S(1)}, bf16[384,512]{1,0:T(8,128)(2,1)S(1)}, u32[]{:S(2)}, u32[]{:S(2)}) collective-permute-start(bf16[384,512]{1,0:T(8,128)(2,1)S(1)} %get-tuple-element.54), channel_id=1, source_target_pairs={{0,3},{8,11},{16,19},{24,27},{4,7},{12,15},{20,23},{28,31},{1,0},{... | collective-permute-start | bytes 1179656 | tf_op jit(solution)/shard_map/ppermute | solution.py:50
  7.3 20.2 %collective-permute-start.2 = (bf16[384,512]{1,0:T(8,128)(2,1)}, bf16[384,512]{1,0:T(8,128)(2,1)S(1)}, u32[]{:S(2)}, u32[]{:S(2)}) collective-permute-start(bf16[384,512]{1,0:T(8,128)(2,1)} %get-tuple-element.55), channel_id=1, source_target_pairs={{0,1},{8,9},{16,17},{24,25},{4,5},{12,13},{20,21},{28,29},{1,2},{9... | collective-permute-start | bytes 1179656 | tf_op jit(solution)/shard_map/ppermute | solution.py:50
  8.3 23.5 %collective-permute-start.4 = (bf16[384,512]{1,0:T(8,128)(2,1)}, bf16[384,512]{1,0:T(8,128)(2,1)S(1)}, u32[]{:S(2)}, u32[]{:S(2)}) collective-permute-start(bf16[384,512]{1,0:T(8,128)(2,1)} %slice.72), channel_id=1, source_target_pairs={{0,3},{8,11},{16,19},{24,27},{4,7},{12,15},{20,23},{28,31},{1,0},{... | collective-permute-start | bytes 1179656 | tf_op jit(solution)/shard_map/ppermute | solution.py:50
  10.0 33.9 %collective-permute-start.6 = (bf16[384,512]{1,0:T(8,128)(2,1)}, bf16[384,512]{1,0:T(8,128)(2,1)}, u32[]{:S(2)}, u32[]{:S(2)}) collective-permute-start(bf16[384,512]{1,0:T(8,128)(2,1)} %slice.72), channel_id=1, source_target_pairs={{0,1},{8,9},{16,17},{24,25},{4,5},{12,13},{20,21},{28,29},{1,2},{9... | collective-permute-start | bytes 1179656 | tf_op jit(solution)/shard_map/ppermute | solution.py:50
  15.0 25.3 %collective-permute-start.5 = (bf16[384,512]{1,0:T(8,128)(2,1)}, bf16[384,512]{1,0:T(8,128)(2,1)S(1)}, u32[]{:S(2)}, u32[]{:S(2)}) collective-permute-start(bf16[384,512]{1,0:T(8,128)(2,1)} %get-tuple-element.53), channel_id=1, source_target_pairs={{0,3},{8,11},{16,19},{24,27},{4,7},{12,15},{20,23},{28,31},{1,0},{... | collective-permute-start | bytes 1179656 | tf_op jit(solution)/shard_map/ppermute | solution.py:50
  23.3 20.6 %collective-permute-start.7 = (bf16[384,512]{1,0:T(8,128)(2,1)}, bf16[384,512]{1,0:T(8,128)(2,1)}, u32[]{:S(2)}, u32[]{:S(2)}) collective-permute-start(bf16[384,512]{1,0:T(8,128)(2,1)} %get-tuple-element.53), channel_id=1, source_target_pairs={{0,1},{8,9},{16,17},{24,25},{4,5},{12,13},{20,21},{28,29},{1,2},{9... | collective-permute-start | bytes 1179656 | tf_op jit(solution)/shard_map/ppermute | solution.py:50
  24.7 1.6 %copy-start.7 = (s32[1536]{0:T(1024)S(1)}, s32[1536]{0:T(1024)}, u32[]{:S(2)}) copy-start(s32[1536]{0:T(1024)} %param.7) | copy-start | bytes 18436
  27.5 24.5 %collective-permute-start.3 = (bf16[384,512]{1,0:T(8,128)(2,1)}, bf16[384,512]{1,0:T(8,128)(2,1)S(1)}, u32[]{:S(2)}, u32[]{:S(2)}) collective-permute-start(bf16[384,512]{1,0:T(8,128)(2,1)} %copy-done.5), channel_id=1, source_target_pairs={{0,1},{8,9},{16,17},{24,25},{4,5},{12,13},{20,21},{28,29},{1,2},{9... | collective-permute-start | bytes 1179656 | tf_op jit(solution)/shard_map/ppermute | solution.py:50
  31.8 27.2 %collective-permute-start.12 = (bf16[384,512]{1,0:T(8,128)(2,1)S(1)}, bf16[384,512]{1,0:T(8,128)(2,1)S(1)}, u32[]{:S(2)}, u32[]{:S(2)}) collective-permute-start(bf16[384,512]{1,0:T(8,128)(2,1)S(1)} %collective-permute-done.4.refs_3_), channel_id=1, source_target_pairs={{0,4},{8,12},{16,20},{24,28},{4,0},{12,8},{20,16},{28,24},{1,5},{9... | collective-permute-start | bytes 1179656 | tf_op jit(solution)/shard_map/ppermute | solution.py:50
  40.2 18.8 %collective-permute-start.13 = (bf16[384,512]{1,0:T(8,128)(2,1)S(1)}, bf16[384,512]{1,0:T(8,128)(2,1)S(1)}, u32[]{:S(2)}, u32[]{:S(2)}) collective-permute-start(bf16[384,512]{1,0:T(8,128)(2,1)S(1)} %collective-permute-done.5.refs_4_), channel_id=1, source_target_pairs={{0,4},{8,12},{16,20},{24,28},{4,0},{12,8},{20,16},{28,24},{1,5},{9... | collective-permute-start | bytes 1179656 | tf_op jit(solution)/shard_map/ppermute | solution.py:50
  43.8 16.4 %collective-permute-start.14 = (bf16[384,512]{1,0:T(8,128)(2,1)S(1)}, bf16[384,512]{1,0:T(8,128)(2,1)S(1)}, u32[]{:S(2)}, u32[]{:S(2)}) collective-permute-start(bf16[384,512]{1,0:T(8,128)(2,1)S(1)} %collective-permute-done.refs_3_.refs_5_), channel_id=1, source_target_pairs={{0,4},{8,12},{16,20},{24,28},{4,0},{12,8},{20,16},{28,24},{1,5},{9... | collective-permute-start | bytes 1179656 | tf_op jit(solution)/shard_map/ppermute | solution.py:50
  43.9 24.8 %collective-permute-start.15 = (bf16[384,512]{1,0:T(8,128)(2,1)S(1)}, bf16[384,512]{1,0:T(8,128)(2,1)S(1)}, u32[]{:S(2)}, u32[]{:S(2)}) collective-permute-start(bf16[384,512]{1,0:T(8,128)(2,1)S(1)} %collective-permute-done.1.refs_4_.refs_6_), channel_id=1, source_target_pairs={{0,4},{8,12},{16,20},{24,28},{4,0},{12,8},{20,16},{28,24},{1,5},{9... | collective-permute-start | bytes 1179656 | tf_op jit(solution)/shard_map/ppermute | solution.py:50
  55.0 1.6 %copy-start.1 = (f32[4,512,256]{2,1,0:T(8,128)}, f32[4,512,256]{2,1,0:T(8,128)S(1)}, u32[]{:S(2)}) copy-start(f32[4,512,256]{2,1,0:T(8,128)S(1)} %get-tuple-element.28) | copy-start | bytes 6291460
  56.7 21.2 %collective-permute-start.8 = (f16[4,512,256]{2,1,0:T(8,128)(2,1)}, f16[4,512,256]{2,1,0:T(8,128)(2,1)}, u32[]{:S(2)}, u32[]{:S(2)}) collective-permute-start(f16[4,512,256]{2,1,0:T(8,128)(2,1)} %convert_element_type.125), channel_id=1, source_target_pairs={{0,8},{8,0},{16,24},{24,16},{4,12},{12,4},{20,28},{28,20},{1,9},{9... | collective-permute-start | bytes 3145736 | tf_op jit(solution)/shard_map/ppermute | solution.py:50
  74.0 1.7 %copy-start.3 = (f32[4,512,256]{2,1,0:T(8,128)}, f32[4,512,256]{2,1,0:T(8,128)S(1)}, u32[]{:S(2)}) copy-start(f32[4,512,256]{2,1,0:T(8,128)S(1)} %get-tuple-element.36) | copy-start | bytes 6291460
  74.1 3.8 %copy-start.2 = (f32[4,512,256]{2,1,0:T(8,128)S(1)}, f32[4,512,256]{2,1,0:T(8,128)}, u32[]{:S(2)}) copy-start(f32[4,512,256]{2,1,0:T(8,128)} %copy-done.1) | copy-start | bytes 6291460
  75.7 5.9 %collective-permute-start.16 = (f16[4,512,256]{2,1,0:T(8,128)(2,1)}, f16[4,512,256]{2,1,0:T(8,128)(2,1)S(1)}, u32[]{:S(2)}, u32[]{:S(2)}) collective-permute-start(f16[4,512,256]{2,1,0:T(8,128)(2,1)} %convert_element_type.139), channel_id=1, source_target_pairs={{0,8},{8,0},{16,24},{24,16},{4,12},{12,4},{20,28},{28,20},{1,9},{9... | collective-permute-start | bytes 3145736 | tf_op jit(solution)/shard_map/ppermute | solution.py:50
  77.8 3.8 %copy-start.4 = (f32[4,512,256]{2,1,0:T(8,128)S(1)}, f32[4,512,256]{2,1,0:T(8,128)}, u32[]{:S(2)}) copy-start(f32[4,512,256]{2,1,0:T(8,128)} %copy-done.3) | copy-start | bytes 6291460
  79.5 8.4 %collective-permute-start.11 = (f16[512,256]{1,0:T(8,128)(2,1)S(1)}, f16[512,256]{1,0:T(8,128)(2,1)S(1)}, u32[]{:S(2)}, u32[]{:S(2)}) collective-permute-start(f16[512,256]{1,0:T(8,128)(2,1)S(1)} %get-tuple-element.33), channel_id=1, source_target_pairs={{0,64},{8,72},{16,80},{24,88},{4,68},{12,76},{20,84},{28,92},{1,65... | collective-permute-start | bytes 786440 | tf_op jit(solution)/shard_map/ppermute | solution.py:50
  79.8 14.1 %collective-permute-start.10 = (f16[512,256]{1,0:T(8,128)(2,1)S(1)}, f16[512,256]{1,0:T(8,128)(2,1)S(1)}, u32[]{:S(2)}, u32[]{:S(2)}) collective-permute-start(f16[512,256]{1,0:T(8,128)(2,1)S(1)} %get-tuple-element.32), channel_id=1, source_target_pairs={{0,96},{8,104},{16,112},{24,120},{4,100},{12,108},{20,116},{28,124... | collective-permute-start | bytes 786440 | tf_op jit(solution)/shard_map/ppermute | solution.py:50
  81.6 14.6 %collective-permute-start.9 = (f16[512,256]{1,0:T(8,128)(2,1)S(1)}, f16[512,256]{1,0:T(8,128)(2,1)S(1)}, u32[]{:S(2)}, u32[]{:S(2)}) collective-permute-start(f16[512,256]{1,0:T(8,128)(2,1)S(1)} %get-tuple-element.31), channel_id=1, source_target_pairs={{0,32},{8,40},{16,48},{24,56},{4,36},{12,44},{20,52},{28,60},{1,33... | collective-permute-start | bytes 786440 | tf_op jit(solution)/shard_map/ppermute | solution.py:50
  82.0 17.2 %collective-permute-start.19 = (f16[512,256]{1,0:T(8,128)(2,1)S(1)}, f16[512,256]{1,0:T(8,128)(2,1)S(1)}, u32[]{:S(2)}, u32[]{:S(2)}) collective-permute-start(f16[512,256]{1,0:T(8,128)(2,1)S(1)} %get-tuple-element.41), channel_id=1, source_target_pairs={{0,64},{8,72},{16,80},{24,88},{4,68},{12,76},{20,84},{28,92},{1,65... | collective-permute-start | bytes 786440 | tf_op jit(solution)/shard_map/ppermute | solution.py:50
  84.4 19.8 %collective-permute-start.18 = (f16[512,256]{1,0:T(8,128)(2,1)S(1)}, f16[512,256]{1,0:T(8,128)(2,1)S(1)}, u32[]{:S(2)}, u32[]{:S(2)}) collective-permute-start(f16[512,256]{1,0:T(8,128)(2,1)S(1)} %get-tuple-element.40), channel_id=1, source_target_pairs={{0,96},{8,104},{16,112},{24,120},{4,100},{12,108},{20,116},{28,124... | collective-permute-start | bytes 786440 | tf_op jit(solution)/shard_map/ppermute | solution.py:50
  87.9 18.2 %collective-permute-start.17 = (f16[512,256]{1,0:T(8,128)(2,1)S(1)}, f16[512,256]{1,0:T(8,128)(2,1)S(1)}, u32[]{:S(2)}, u32[]{:S(2)}) collective-permute-start(f16[512,256]{1,0:T(8,128)(2,1)S(1)} %get-tuple-element.39), channel_id=1, source_target_pairs={{0,32},{8,40},{16,48},{24,56},{4,36},{12,44},{20,52},{28,60},{1,33... | collective-permute-start | bytes 786440 | tf_op jit(solution)/shard_map/ppermute | solution.py:50
  106.4 4.6 %collective-permute-start.20 = (f16[256,256]{1,0:T(8,128)(2,1)S(1)}, f16[256,256]{1,0:T(8,128)(2,1)S(1)}, u32[]{:S(2)}, u32[]{:S(2)}) collective-permute-start(f16[256,256]{1,0:T(8,128)(2,1)S(1)} %get-tuple-element.56), channel_id=1, source_target_pairs={{0,16},{8,24},{16,0},{24,8},{4,20},{12,28},{20,4},{28,12},{1,17},{... | collective-permute-start | bytes 393224 | tf_op jit(solution)/shard_map/ppermute | solution.py:55
  107.5 6.4 %collective-permute-start.22 = (f16[256,256]{1,0:T(8,128)(2,1)S(1)}, f16[256,256]{1,0:T(8,128)(2,1)S(1)}, u32[]{:S(2)}, u32[]{:S(2)}) collective-permute-start(f16[256,256]{1,0:T(8,128)(2,1)S(1)} %get-tuple-element.57), channel_id=1, source_target_pairs={{0,16},{8,24},{16,0},{24,8},{4,20},{12,28},{20,4},{28,12},{1,17},{... | collective-permute-start | bytes 393224 | tf_op jit(solution)/shard_map/ppermute | solution.py:55
  113.9 8.6 %collective-permute-start.23 = (f16[256,256]{1,0:T(8,128)(2,1)S(1)}, f16[256,256]{1,0:T(8,128)(2,1)S(1)}, u32[]{:S(2)}, u32[]{:S(2)}) collective-permute-start(f16[256,256]{1,0:T(8,128)(2,1)S(1)} %fusion.7), channel_id=1, source_target_pairs={{0,21},{8,29},{16,19},{24,27},{4,23},{12,31},{20,116},{28,124},{1,... | collective-permute-start | bytes 393224 | tf_op jit(solution)/shard_map/ppermute | solution.py:69
  115.0 10.5 %collective-permute-start.21 = (f16[256,256]{1,0:T(8,128)(2,1)S(1)}, f16[256,256]{1,0:T(8,128)(2,1)S(1)}, u32[]{:S(2)}, u32[]{:S(2)}) collective-permute-start(f16[256,256]{1,0:T(8,128)(2,1)S(1)} %fusion.8), channel_id=1, source_target_pairs={{0,21},{8,29},{16,19},{24,27},{4,23},{12,31},{20,116},{28,124},{1,... | collective-permute-start | bytes 393224 | tf_op jit(solution)/shard_map/ppermute | solution.py:69

commit v4 on v3

--- a/solution.py
+++ b/solution.py
@@ -119,9 +119,13 @@
     ]
     extra = sources[len(pairs) :]
     if late:
-        south_t, flipped = rest
-        edge = chunk(SPLIT).start
-        pairs += [(extra[0], south_t.at[:, :edge]), (extra[1], south_t.at[:, edge:])]
+        left, flipped = own_t, rest[0]
+        size, edge = own.shape[1], chunk(SPLIT).start
+        pairs[1] = (sources[1], left.at[:size])
+        pairs += [
+            (extra[0], left.at[size:, :edge]),
+            (extra[1], left.at[size:, edge:]),
+        ]
     else:
         flipped = outs[-1]
         pairs += zip(extra, rest)
@@ -135,7 +139,9 @@
     half = own.shape[1] // 2
 
     def put(i, left, right):
-        total = jnp.dot(left[...], right[...], preferred_element_type=jnp.float32)
+        keep(i, jnp.dot(left[...], right[...], preferred_element_type=jnp.float32))
+
+    def keep(i, total):
         if not first:
             total = total + rest[0][i]
         if last:
@@ -148,7 +154,10 @@
     for copy in copies:
         copy.wait()
     if late:
-        put(0, own_t, far)
+        total = jnp.dot(left[...], far[...], preferred_element_type=jnp.float32)
+        size = own.shape[1]
+        keep(0, total[:size])
+        keep(3, total[size:])
     else:
         put(0, own_t, own)
         put(1, own_t, north)
@@ -157,7 +166,6 @@
     if late:
         put(1, flipped, own)
         put(2, flipped, north)
-        put(3, south_t, far)
     else:
         put(3, flipped, north)
 
@@ -169,7 +177,8 @@
     held = [((1, rows), jnp.float32), wide, tall, tall, tall]
     outs = [((4, size, size), jnp.float32)]
     if late:
-        held += [wide, wide]
+        held[1] = ((2 * size, rows), jnp.bfloat16)
+        held.append(wide)
     elif lo:
         held += outs
     if hi == COUNT:
@@ -209,15 +218,21 @@
         souths.append(shift(piece, dy=1))
         farther.append(shift(norths[k], dz=2))
 
-    def over_x(theirs, mine):
-        theirs = shift(theirs.astype(jnp.float16), swap=True)
-        joined = [mine[d] + theirs[d].astype(jnp.float32) for d in range(4)]
+    def over_x(theirs, mine, parts):
+        theirs, mine = lax.optimization_barrier(
+            (theirs.astype(jnp.float16), mine.astype(jnp.float16))
+        )
+        theirs = shift(theirs, swap=True)
+        theirs, mine = theirs.astype(jnp.float32), mine.astype(jnp.float32)
+        joined = [mine[d] + theirs[d] for d in range(4)]
         kept, *sent = lax.optimization_barrier(
             [joined[0]] + [joined[d].astype(jnp.float16) for d in (1, 3, 2)]
         )
         got = []
-        for d, value in zip((1, 3, 2), sent):
-            got.append(shift(value, dx=d))
+        for part in parts:
+            got.append([])
+            for d, value in zip((1, 3, 2), sent):
+                got[-1].append(shift(value[part], dx=d))
         return kept, got
 
     gap = lookup(val_band, val_energy) - lookup(cond_band, cond_energy)
@@ -226,34 +241,38 @@
     own_t = (row * own.T.astype(jnp.float32)).astype(jnp.bfloat16)
     row, own_t = lax.optimization_barrier((row, own_t))
     base = [row, own_t, own]
+    tail = [slice(u, v) for u, v in zip((0, *TAIL), TAIL)]
     one, two = slice(0, SPLIT), slice(SPLIT, COUNT)
 
     early_sum, south_a = run_stage(False, 0, SPLIT, base + norths[one] + souths[one])
     *early, south_b = run_stage(
         False, SPLIT, COUNT, base + norths[two] + souths[two] + [early_sum]
     )
-    early, early_got = over_x(*early)
+    early, early_got = over_x(*early, [slice(None)])
     late = run_stage(
         True, 0, COUNT, base + norths + farther + [south_a, south_b]
     )
-    late, late_got = over_x(*late)
+    late, late_got = over_x(*late, tail)
 
     def sum_of(kept, got):
         return kept + sum(g.astype(jnp.float32) for g in got)
 
-    early = lax.optimization_barrier(sum_of(early, early_got))
-    late = sum_of(late, late_got)
+    def after(value, other):
+        return value if other is None else lax.optimization_barrier((value, other))[0]
+
+    early = lax.optimization_barrier(sum_of(early, early_got[0]))
     keeps = planned(pair, ga)[2]
-    kept = jnp.where(keeps, early, late)
-    sent = jnp.where(keeps, late, early).astype(jnp.float16)
-    parts, edges, total = [], (0, *TAIL), None
-    for h, part in enumerate(slice(u, v) for u, v in zip(edges, edges[1:])):
-        got = swap_z_lo(sent[part])
-        if h:
-            got = lax.optimization_barrier((got, total))[0]
-        total = (kept[part] + got.astype(jnp.float32)).astype(jnp.float16)
-        parts.append(to_owner(total))
-    return jnp.concatenate(parts, 0).astype(jnp.float32) * (1.0 / GAIN)
+    pieces, sent, total = [], None, None
+    for h, part in enumerate(tail):
+        whole = sum_of(late[part], after(late_got[h], sent))
+        kept = jnp.where(keeps, early[part], whole)
+        sent = jnp.where(keeps, whole, early[part]).astype(jnp.float16)
+        pieces.append((kept, swap_z_lo(sent)))
+    done = []
+    for kept, got in pieces:
+        total = (kept + after(got, total).astype(jnp.float32)).astype(jnp.float16)
+        done.append(to_owner(total))
+    return jnp.concatenate(done, 0).astype(jnp.float32) * (1.0 / GAIN)
 
 
 def solution(mesh):

time: 128 us -> 124 us (0.969)
  the two profiles are of different devices: /device:TPU:5 before, /device:TPU:4 now
where the time goes in v4:
time: 124 us; the launch traced here: 123 us
  waiting for transfers between devices  49.8 us (40%)
  starting transfers between devices  43.5 us (35%)
  Pallas kernels  11.9 us (10%)
  other arithmetic  11.4 us (9%)
  local copies, waits for them, and re-layouts  6.58 us (5%)
    ppermute x23, starting transfers between devices, shift(): return lax.ppermute(value, AXES, pairs)  37.8 us
    ppermute x23, waiting for transfers between devices, shift(): return lax.ppermute(value, AXES, pairs)  37.4 us
    pallas_call x3, Pallas kernels, run_stage(): pl.pallas_call(functools.partial(stage_kernel, late, lo, hi, len(sources)...  11.9 us
    ppermute x2, waiting for transfers between devices, to_owner(): return lax.ppermute(value, AXES, pairs)  9.36 us
    slice x2, local copies, waits for them, and re-layouts, rows(): return block[starts[k]:starts[k + 1]]  4.11 us
    convert_element_type x4, other arithmetic, over_x(): theirs, mine = (theirs.astype(jnp.float32), mine.astype(jnp.float32))  3.17 us
    ppermute x2, waiting for transfers between devices, swap_z_lo(): return lax.ppermute(value, AXES, pairs)  3.01 us
    ppermute x2, starting transfers between devices, to_owner(): return lax.ppermute(value, AXES, pairs)  2.99 us
  transfers between devices with their start and end apart: 27, of which 16 were waited for; matrix products, arithmetic and copies ran while one was open for 10% of the time, Pallas kernels for 10%

profile of v4, /device:TPU:4, one launch (start us, length us, event | category | flops | bytes accessed | tf_op | source)
XLA Modules:
  0.0 123.5 jit_solution(6637510804740316738)
XLA Ops:
  0.0 1.9 %slice.92 = bf16[384,512]{1,0:T(8,128)(2,1)} slice(bf16[1536,512]{1,0:T(8,128)(2,1)} %refs_2_.5), slice={[0:384], [0:512]} | slice | bytes 786432 | tf_op jit(solution)/shard_map/slice | solution.py:210
  1.9 2.2 %fusion.15 = (bf16[384,512]{1,0:T(8,128)(2,1)}, bf16[384,512]{1,0:T(8,128)(2,1)S(1)}, bf16[384,512]{1,0:T(8,128)(2,1)}) fusion(bf16[1536,512]{1,0:T(8,128)(2,1)} %refs_2_.5), kind=kLoop, calls=%fused_computation.37 | loop fusion | bytes 2359296 | tf_op jit(solution)/shard_map/slice | solution.py:210
  4.1 3.0 %collective-permute-start = (bf16[384,512]{1,0:T(8,128)(2,1)}, bf16[384,512]{1,0:T(8,128)(2,1)S(1)}, u32[]{:S(2)}, u32[]{:S(2)}) collective-permute-start(bf16[384,512]{1,0:T(8,128)(2,1)} %get-tuple-element.67), channel_id=1, source_target_pairs={{0,3},{8,11},{16,19},{24,27},{4,7},{12,15},{20,23},{28,31},{1,0},{... | collective-permute-start | bytes 1179656 | tf_op jit(solution)/shard_map/ppermute | solution.py:50
  7.1 0.7 collective-permute-start.1
  7.9 1.3 %collective-permute-start.2 = (bf16[384,512]{1,0:T(8,128)(2,1)}, bf16[384,512]{1,0:T(8,128)(2,1)S(1)}, u32[]{:S(2)}, u32[]{:S(2)}) collective-permute-start(bf16[384,512]{1,0:T(8,128)(2,1)} %get-tuple-element.67), channel_id=1, source_target_pairs={{0,1},{8,9},{16,17},{24,25},{4,5},{12,13},{20,21},{28,29},{1,2},{9... | collective-permute-start | bytes 1179656 | tf_op jit(solution)/shard_map/ppermute | solution.py:50
  9.2 2.0 %collective-permute-start.4 = (bf16[384,512]{1,0:T(8,128)(2,1)}, bf16[384,512]{1,0:T(8,128)(2,1)S(1)}, u32[]{:S(2)}, u32[]{:S(2)}) collective-permute-start(bf16[384,512]{1,0:T(8,128)(2,1)} %slice.92), channel_id=1, source_target_pairs={{0,3},{8,11},{16,19},{24,27},{4,7},{12,15},{20,23},{28,31},{1,0},{... | collective-permute-start | bytes 1179656 | tf_op jit(solution)/shard_map/ppermute | solution.py:50
  11.2 5.8 %collective-permute-done.refs_3_.refs_5_ = bf16[384,512]{1,0:T(8,128)(2,1)S(1)} collective-permute-done((bf16[384,512]{1,0:T(8,128)(2,1)}, bf16[384,512]{1,0:T(8,128)(2,1)S(1)}, u32[]{:S(2)}, u32[]{:S(2)}) %collective-permute-start) | collective-permute-done | bytes 393248 | tf_op jit(solution)/shard_map/ppermute | solution.py:50
  17.0 3.6 %collective-permute-start.5 = (bf16[384,512]{1,0:T(8,128)(2,1)}, bf16[384,512]{1,0:T(8,128)(2,1)S(1)}, u32[]{:S(2)}, u32[]{:S(2)}) collective-permute-start(bf16[384,512]{1,0:T(8,128)(2,1)} %get-tuple-element.65), channel_id=1, source_target_pairs={{0,3},{8,11},{16,19},{24,27},{4,7},{12,15},{20,23},{28,31},{1,0},{... | collective-permute-start | bytes 1179656 | tf_op jit(solution)/shard_map/ppermute | solution.py:50
  20.5 4.7 %collective-permute-done.1.refs_4_.refs_6_ = bf16[384,512]{1,0:T(8,128)(2,1)S(1)} collective-permute-done((bf16[384,512]{1,0:T(8,128)(2,1)S(1)}, bf16[384,512]{1,0:T(8,128)(2,1)S(1)}, u32[]{:S(2)}, u32[]{:S(2)}) %collective-permute-start.1) | collective-permute-done | bytes 393248 | tf_op jit(solution)/shard_map/ppermute | solution.py:50
  25.3 1.0 collective-permute-start.7
  26.8 1.6 %copy.7 = bf16[1536,512]{0,1:T(8,128)(2,1)} copy(bf16[1536,512]{1,0:T(8,128)(2,1)S(1)} %copy-done) | data formatting | bytes 3145728 | tf_op args[0]
  28.4 1.2 select_reduce_fusion
  29.6 1.6 %collective-permute-start.3 = (bf16[384,512]{1,0:T(8,128)(2,1)}, bf16[384,512]{1,0:T(8,128)(2,1)S(1)}, u32[]{:S(2)}, u32[]{:S(2)}) collective-permute-start(bf16[384,512]{1,0:T(8,128)(2,1)} %copy-done.2), channel_id=1, source_target_pairs={{0,1},{8,9},{16,17},{24,25},{4,5},{12,13},{20,21},{28,29},{1,2},{9... | collective-permute-start | bytes 1179656 | tf_op jit(solution)/shard_map/ppermute | solution.py:50
  31.3 2.5 %collective-permute-done.4.refs_3_ = bf16[384,512]{1,0:T(8,128)(2,1)S(1)} collective-permute-done((bf16[384,512]{1,0:T(8,128)(2,1)}, bf16[384,512]{1,0:T(8,128)(2,1)S(1)}, u32[]{:S(2)}, u32[]{:S(2)}) %collective-permute-start.4) | collective-permute-done | bytes 393248 | tf_op jit(solution)/shard_map/ppermute | solution.py:50
  33.8 3.9 %collective-permute-start.12 = (bf16[384,512]{1,0:T(8,128)(2,1)S(1)}, bf16[384,512]{1,0:T(8,128)(2,1)S(1)}, u32[]{:S(2)}, u32[]{:S(2)}) collective-permute-start(bf16[384,512]{1,0:T(8,128)(2,1)S(1)} %collective-permute-done.4.refs_3_), channel_id=1, source_target_pairs={{0,4},{8,12},{16,20},{24,28},{4,0},{12,8},{20,16},{28,24},{1,5},{9... | collective-permute-start | bytes 1179656 | tf_op jit(solution)/shard_map/ppermute | solution.py:50
  37.7 3.4 %collective-permute-done.5.refs_4_ = bf16[384,512]{1,0:T(8,128)(2,1)S(1)} collective-permute-done((bf16[384,512]{1,0:T(8,128)(2,1)}, bf16[384,512]{1,0:T(8,128)(2,1)S(1)}, u32[]{:S(2)}, u32[]{:S(2)}) %collective-permute-start.5) | collective-permute-done | bytes 393248 | tf_op jit(solution)/shard_map/ppermute | solution.py:50
  41.1 3.9 %collective-permute-start.13 = (bf16[384,512]{1,0:T(8,128)(2,1)S(1)}, bf16[384,512]{1,0:T(8,128)(2,1)S(1)}, u32[]{:S(2)}, u32[]{:S(2)}) collective-permute-start(bf16[384,512]{1,0:T(8,128)(2,1)S(1)} %collective-permute-done.5.refs_4_), channel_id=1, source_target_pairs={{0,4},{8,12},{16,20},{24,28},{4,0},{12,8},{20,16},{28,24},{1,5},{9... | collective-permute-start | bytes 1179656 | tf_op jit(solution)/shard_map/ppermute | solution.py:50
  45.0 3.5 %collective-permute-start.15 = (bf16[384,512]{1,0:T(8,128)(2,1)S(1)}, bf16[384,512]{1,0:T(8,128)(2,1)S(1)}, u32[]{:S(2)}, u32[]{:S(2)}) collective-permute-start(bf16[384,512]{1,0:T(8,128)(2,1)S(1)} %collective-permute-done.1.refs_4_.refs_6_), channel_id=1, source_target_pairs={{0,4},{8,12},{16,20},{24,28},{4,0},{12,8},{20,16},{28,24},{1,5},{9... | collective-permute-start | bytes 1179656 | tf_op jit(solution)/shard_map/ppermute | solution.py:50
  48.5 1.7 %fusion.refs_1_ = bf16[512,1536]{1,0:T(8,128)(2,1)S(1)} fusion(bf16[1536,512]{0,1:T(8,128)(2,1)} %copy.7, f32[1536]{0:T(1024)S(1)} %multiply_divide_fusion), kind=kLoop, calls=%fused_computation.1 | loop fusion | flops 2359296 | bytes 3151872 | tf_op jit(solution)/shard_map/convert_element_type | solution.py:241
  50.2 3.5 %shard_map.55 = (f32[4,512,512]{2,1,0:T(8,128)S(1)}, bf16[512,768]{1,0:T(8,128)(2,1)S(1)}) custom-call(f32[1,1536]{1,0:T(1,128)S(1)} %div.19.refs_0_, bf16[512,1536]{1,0:T(8,128)(2,1)S(1)} %fusion.refs_1_, bf16[1536,512]{1,0:T(8,128)(2,1)S(1)} %copy-done, bf16[384,512]{1,0:T(8,128)(2,1)S(1)} %collective-permute-done.4.refs_3_, ...), custom_call_target="tpu_custom_call" | custom-call | flops 1610612736 | bytes 8388608 | tf_op jit(solution)/shard_map/pallas_call | solution.py:188
  53.7 3.0 %shard_map.56 = (f32[4,512,256]{2,1,0:T(8,128)S(1)}, f32[4,512,256]{2,1,0:T(8,128)S(1)}, bf16[512,768]{1,0:T(8,128)(2,1)S(1)}) custom-call(f32[1,1536]{1,0:T(1,128)S(1)} %div.19.refs_0_, bf16[512,1536]{1,0:T(8,128)(2,1)S(1)} %fusion.refs_1_, bf16[1536,512]{1,0:T(8,128)(2,1)S(1)} %copy-done, bf16[384,512]{1,0:T(8,128)(2,1)S(1)} %collective-permute-done.refs_3_.refs_5_, ...), custom_call_target="tpu_custom_call" | custom-call | flops 1610612736 | bytes 8388608 | tf_op jit(solution)/shard_map/pallas_call | solution.py:188
  56.7 1.2 convert_element_type.123
  57.9 1.2 convert_element_type.124
  59.1 4.2 %collective-permute-done.14.refs_9_ = bf16[384,512]{1,0:T(8,128)(2,1)S(1)} collective-permute-done((bf16[384,512]{1,0:T(8,128)(2,1)S(1)}, bf16[384,512]{1,0:T(8,128)(2,1)S(1)}, u32[]{:S(2)}, u32[]{:S(2)}) %collective-permute-start.14) | collective-permute-done | bytes 393248 | tf_op jit(solution)/shard_map/ppermute | solution.py:50
  63.4 6.7 %collective-permute-done.15.refs_10_ = bf16[384,512]{1,0:T(8,128)(2,1)S(1)} collective-permute-done((bf16[384,512]{1,0:T(8,128)(2,1)S(1)}, bf16[384,512]{1,0:T(8,128)(2,1)S(1)}, u32[]{:S(2)}, u32[]{:S(2)}) %collective-permute-start.15) | collective-permute-done | bytes 393248 | tf_op jit(solution)/shard_map/ppermute | solution.py:50
  70.1 5.4 %shard_map.57 = (f32[4,512,256]{2,1,0:T(8,128)S(1)}, f32[4,512,256]{2,1,0:T(8,128)S(1)}) custom-call(f32[1,1536]{1,0:T(1,128)S(1)} %div.19.refs_0_, bf16[512,1536]{1,0:T(8,128)(2,1)S(1)} %fusion.refs_1_, bf16[1536,512]{1,0:T(8,128)(2,1)S(1)} %copy-done, bf16[384,512]{1,0:T(8,128)(2,1)S(1)} %collective-permute-done.4.refs_3_, ...), custom_call_target="tpu_custom_call" | custom-call | flops 3221225472 | bytes 8388608 | tf_op jit(solution)/shard_map/pallas_call | solution.py:188
  77.3 1.4 %convert_element_type.126 = f32[4,512,256]{2,1,0:T(8,128)S(1)} convert(f16[4,512,256]{2,1,0:T(8,128)(2,1)} %collective-permute-done.8) | non-fusion elementwise | flops 524288 | bytes 3145728 | tf_op jit(solution)/shard_map/convert_element_type | solution.py:226
  79.7 2.2 %collective-permute-start.10 = (f16[512,256]{1,0:T(8,128)(2,1)S(1)}, f16[512,256]{1,0:T(8,128)(2,1)S(1)}, u32[]{:S(2)}, u32[]{:S(2)}) collective-permute-start(f16[512,256]{1,0:T(8,128)(2,1)S(1)} %get-tuple-element.41), channel_id=1, source_target_pairs={{0,96},{8,104},{16,112},{24,120},{4,100},{12,108},{20,116},{28,124... | collective-permute-start | bytes 786440 | tf_op jit(solution)/shard_map/ppermute | solution.py:50
  81.8 1.4 %convert_element_type.139 = f32[4,512,256]{2,1,0:T(8,128)S(1)} convert(f16[4,512,256]{2,1,0:T(8,128)(2,1)} %collective-permute-done.16) | non-fusion elementwise | flops 524288 | bytes 3145728 | tf_op jit(solution)/shard_map/convert_element_type | solution.py:226
  83.7 3.0 %collective-permute-start.19 = (f16[256,256]{1,0:T(8,128)(2,1)S(1)}, f16[256,256]{1,0:T(8,128)(2,1)S(1)}, u32[]{:S(2)}, u32[]{:S(2)}) collective-permute-start(f16[256,256]{1,0:T(8,128)(2,1)S(1)} %get-tuple-element.74), channel_id=1, source_target_pairs={{0,64},{8,72},{16,80},{24,88},{4,68},{12,76},{20,84},{28,92},{1,65... | collective-permute-start | bytes 393224 | tf_op jit(solution)/shard_map/ppermute | solution.py:50
  86.7 1.8 %collective-permute-start.18 = (f16[256,256]{1,0:T(8,128)(2,1)S(1)}, f16[256,256]{1,0:T(8,128)(2,1)S(1)}, u32[]{:S(2)}, u32[]{:S(2)}) collective-permute-start(f16[256,256]{1,0:T(8,128)(2,1)S(1)} %get-tuple-element.72), channel_id=1, source_target_pairs={{0,96},{8,104},{16,112},{24,120},{4,100},{12,108},{20,116},{28,124... | collective-permute-start | bytes 393224 | tf_op jit(solution)/shard_map/ppermute | solution.py:50
  88.6 1.3 %collective-permute-done.11 = f16[512,256]{1,0:T(8,128)(2,1)S(1)} collective-permute-done((f16[512,256]{1,0:T(8,128)(2,1)S(1)}, f16[512,256]{1,0:T(8,128)(2,1)S(1)}, u32[]{:S(2)}, u32[]{:S(2)}) %collective-permute-start.11) | collective-permute-done | bytes 262176 | tf_op jit(solution)/shard_map/ppermute | solution.py:50
  89.9 1.2 collective-permute-start.17
  91.1 3.5 %collective-permute-done.10 = f16[512,256]{1,0:T(8,128)(2,1)S(1)} collective-permute-done((f16[512,256]{1,0:T(8,128)(2,1)S(1)}, f16[512,256]{1,0:T(8,128)(2,1)S(1)}, u32[]{:S(2)}, u32[]{:S(2)}) %collective-permute-start.10) | collective-permute-done | bytes 262176 | tf_op jit(solution)/shard_map/ppermute | solution.py:50
  94.6 1.0 collective-permute-done.9
  95.7 1.3 %collective-permute-start.22 = (f16[256,256]{1,0:T(8,128)(2,1)S(1)}, f16[256,256]{1,0:T(8,128)(2,1)S(1)}, u32[]{:S(2)}, u32[]{:S(2)}) collective-permute-start(f16[256,256]{1,0:T(8,128)(2,1)S(1)} %get-tuple-element.71), channel_id=1, source_target_pairs={{0,32},{8,40},{16,48},{24,56},{4,36},{12,44},{20,52},{28,60},{1,33... | collective-permute-start | bytes 393224 | tf_op jit(solution)/shard_map/ppermute | solution.py:50
  96.9 0.8 collective-permute-start.23
  98.3 2.1 %collective-permute-start.24 = (f16[256,256]{1,0:T(8,128)(2,1)S(1)}, f16[256,256]{1,0:T(8,128)(2,1)S(1)}, u32[]{:S(2)}, u32[]{:S(2)}) collective-permute-start(f16[256,256]{1,0:T(8,128)(2,1)S(1)} %get-tuple-element.75), channel_id=1, source_target_pairs={{0,64},{8,72},{16,80},{24,88},{4,68},{12,76},{20,84},{28,92},{1,65... | collective-permute-start | bytes 393224 | tf_op jit(solution)/shard_map/ppermute | solution.py:50
  100.6 1.4 %collective-permute-start.20 = (f16[256,256]{1,0:T(8,128)(2,1)S(1)}, f16[256,256]{1,0:T(8,128)(2,1)S(1)}, u32[]{:S(2)}, u32[]{:S(2)}) collective-permute-start(f16[256,256]{1,0:T(8,128)(2,1)S(1)} %select_convert_fusion.1), channel_id=1, source_target_pairs={{0,16},{8,24},{16,0},{24,8},{4,20},{12,28},{20,4},{28,12},{1,17},{... | collective-permute-start | bytes 393224 | tf_op jit(solution)/shard_map/ppermute | solution.py:55
  101.9 1.9 %collective-permute-done.22 = f16[256,256]{1,0:T(8,128)(2,1)S(1)} collective-permute-done((f16[256,256]{1,0:T(8,128)(2,1)S(1)}, f16[256,256]{1,0:T(8,128)(2,1)S(1)}, u32[]{:S(2)}, u32[]{:S(2)}) %collective-permute-start.22) | collective-permute-done | bytes 131104 | tf_op jit(solution)/shard_map/ppermute | solution.py:50
  103.9 1.7 %collective-permute-done.24 = f16[256,256]{1,0:T(8,128)(2,1)S(1)} collective-permute-done((f16[256,256]{1,0:T(8,128)(2,1)S(1)}, f16[256,256]{1,0:T(8,128)(2,1)S(1)}, u32[]{:S(2)}, u32[]{:S(2)}) %collective-permute-start.24) | collective-permute-done | bytes 131104 | tf_op jit(solution)/shard_map/ppermute | solution.py:50
  105.8 1.4 %collective-permute-start.25 = (f16[256,256]{1,0:T(8,128)(2,1)S(1)}, f16[256,256]{1,0:T(8,128)(2,1)S(1)}, u32[]{:S(2)}, u32[]{:S(2)}) collective-permute-start(f16[256,256]{1,0:T(8,128)(2,1)S(1)} %get-tuple-element.69), channel_id=1, source_target_pairs={{0,16},{8,24},{16,0},{24,8},{4,20},{12,28},{20,4},{28,12},{1,17},{... | collective-permute-start | bytes 393224 | tf_op jit(solution)/shard_map/ppermute | solution.py:55
  107.2 0.7 collective-permute-start.21
  107.9 2.9 %collective-permute-done.25 = f16[256,256]{1,0:T(8,128)(2,1)S(1)} collective-permute-done((f16[256,256]{1,0:T(8,128)(2,1)S(1)}, f16[256,256]{1,0:T(8,128)(2,1)S(1)}, u32[]{:S(2)}, u32[]{:S(2)}) %collective-permute-start.25) | collective-permute-done | bytes 131104 | tf_op jit(solution)/shard_map/ppermute | solution.py:55
  111.0 2.2 %collective-permute-start.26 = (f16[256,256]{1,0:T(8,128)(2,1)S(1)}, f16[256,256]{1,0:T(8,128)(2,1)S(1)}, u32[]{:S(2)}, u32[]{:S(2)}) collective-permute-start(f16[256,256]{1,0:T(8,128)(2,1)S(1)} %add_convert_fusion), channel_id=1, source_target_pairs={{0,21},{8,29},{16,19},{24,27},{4,23},{12,31},{20,116},{28,124},{1,... | collective-permute-start | bytes 393224 | tf_op jit(solution)/shard_map/ppermute | solution.py:69
  113.2 2.4 %collective-permute-done.21 = f16[256,256]{1,0:T(8,128)(2,1)S(1)} collective-permute-done((f16[256,256]{1,0:T(8,128)(2,1)S(1)}, f16[256,256]{1,0:T(8,128)(2,1)S(1)}, u32[]{:S(2)}, u32[]{:S(2)}) %collective-permute-start.21) | collective-permute-done | bytes 131104 | tf_op jit(solution)/shard_map/ppermute | solution.py:69
  115.7 6.9 %collective-permute-done.26 = f16[256,256]{1,0:T(8,128)(2,1)S(1)} collective-permute-done((f16[256,256]{1,0:T(8,128)(2,1)S(1)}, f16[256,256]{1,0:T(8,128)(2,1)S(1)}, u32[]{:S(2)}, u32[]{:S(2)}) %collective-permute-start.26) | collective-permute-done | bytes 131104 | tf_op jit(solution)/shard_map/ppermute | solution.py:69
  122.6 0.8 convert_multiply_fusion
  (47 shorter events, 5.0 us)
Async XLA Ops:
  0.0 26.8 %copy-start = (bf16[1536,512]{1,0:T(8,128)(2,1)S(1)}, bf16[1536,512]{1,0:T(8,128)(2,1)}, u32[]{:S(2)}) copy-start(bf16[1536,512]{1,0:T(8,128)(2,1)} %refs_2_.5) | copy-start | bytes 4718596
  0.0 26.3 %copy-start.5 = (f32[128]{0:T(128)S(1)}, f32[128]{0:T(128)}, u32[]{:S(2)}) copy-start(f32[128]{0:T(128)} %param.8) | copy-start | bytes 1540
  0.0 26.3 %copy-start.3 = (s32[1536]{0:T(1024)S(1)}, s32[1536]{0:T(1024)}, u32[]{:S(2)}) copy-start(s32[1536]{0:T(1024)} %param.6) | copy-start | bytes 18436
  4.1 21.2 %copy-start.2 = (bf16[384,512]{1,0:T(8,128)(2,1)}, bf16[384,512]{1,0:T(8,128)(2,1)S(1)}, u32[]{:S(2)}) copy-start(bf16[384,512]{1,0:T(8,128)(2,1)S(1)} %get-tuple-element.66) | copy-start | bytes 1179652
  4.1 24.3 %copy-start.4 = (s32[1536]{0:T(1024)S(1)}, s32[1536]{0:T(1024)}, u32[]{:S(2)}) copy-start(s32[1536]{0:T(1024)} %param.7) | copy-start | bytes 18436
  4.1 12.8 %collective-permute-start = (bf16[384,512]{1,0:T(8,128)(2,1)}, bf16[384,512]{1,0:T(8,128)(2,1)S(1)}, u32[]{:S(2)}, u32[]{:S(2)}) collective-permute-start(bf16[384,512]{1,0:T(8,128)(2,1)} %get-tuple-element.67), channel_id=1, source_target_pairs={{0,3},{8,11},{16,19},{24,27},{4,7},{12,15},{20,23},{28,31},{1,0},{... | collective-permute-start | bytes 1179656 | tf_op jit(solution)/shard_map/ppermute | solution.py:50
  7.1 18.1 %collective-permute-start.1 = (bf16[384,512]{1,0:T(8,128)(2,1)S(1)}, bf16[384,512]{1,0:T(8,128)(2,1)S(1)}, u32[]{:S(2)}, u32[]{:S(2)}) collective-permute-start(bf16[384,512]{1,0:T(8,128)(2,1)S(1)} %get-tuple-element.66), channel_id=1, source_target_pairs={{0,3},{8,11},{16,19},{24,27},{4,7},{12,15},{20,23},{28,31},{1,0},{... | collective-permute-start | bytes 1179656 | tf_op jit(solution)/shard_map/ppermute | solution.py:50
  7.9 21.8 %collective-permute-start.2 = (bf16[384,512]{1,0:T(8,128)(2,1)}, bf16[384,512]{1,0:T(8,128)(2,1)S(1)}, u32[]{:S(2)}, u32[]{:S(2)}) collective-permute-start(bf16[384,512]{1,0:T(8,128)(2,1)} %get-tuple-element.67), channel_id=1, source_target_pairs={{0,1},{8,9},{16,17},{24,25},{4,5},{12,13},{20,21},{28,29},{1,2},{9... | collective-permute-start | bytes 1179656 | tf_op jit(solution)/shard_map/ppermute | solution.py:50
  9.2 24.6 %collective-permute-start.4 = (bf16[384,512]{1,0:T(8,128)(2,1)}, bf16[384,512]{1,0:T(8,128)(2,1)S(1)}, u32[]{:S(2)}, u32[]{:S(2)}) collective-permute-start(bf16[384,512]{1,0:T(8,128)(2,1)} %slice.92), channel_id=1, source_target_pairs={{0,3},{8,11},{16,19},{24,27},{4,7},{12,15},{20,23},{28,31},{1,0},{... | collective-permute-start | bytes 1179656 | tf_op jit(solution)/shard_map/ppermute | solution.py:50
  11.1 33.9 %collective-permute-start.6 = (bf16[384,512]{1,0:T(8,128)(2,1)}, bf16[384,512]{1,0:T(8,128)(2,1)}, u32[]{:S(2)}, u32[]{:S(2)}) collective-permute-start(bf16[384,512]{1,0:T(8,128)(2,1)} %slice.92), channel_id=1, source_target_pairs={{0,1},{8,9},{16,17},{24,25},{4,5},{12,13},{20,21},{28,29},{1,2},{9... | collective-permute-start | bytes 1179656 | tf_op jit(solution)/shard_map/ppermute | solution.py:50
  17.0 24.1 %collective-permute-start.5 = (bf16[384,512]{1,0:T(8,128)(2,1)}, bf16[384,512]{1,0:T(8,128)(2,1)S(1)}, u32[]{:S(2)}, u32[]{:S(2)}) collective-permute-start(bf16[384,512]{1,0:T(8,128)(2,1)} %get-tuple-element.65), channel_id=1, source_target_pairs={{0,3},{8,11},{16,19},{24,27},{4,7},{12,15},{20,23},{28,31},{1,0},{... | collective-permute-start | bytes 1179656 | tf_op jit(solution)/shard_map/ppermute | solution.py:50
  25.3 19.7 %collective-permute-start.7 = (bf16[384,512]{1,0:T(8,128)(2,1)}, bf16[384,512]{1,0:T(8,128)(2,1)}, u32[]{:S(2)}, u32[]{:S(2)}) collective-permute-start(bf16[384,512]{1,0:T(8,128)(2,1)} %get-tuple-element.65), channel_id=1, source_target_pairs={{0,1},{8,9},{16,17},{24,25},{4,5},{12,13},{20,21},{28,29},{1,2},{9... | collective-permute-start | bytes 1179656 | tf_op jit(solution)/shard_map/ppermute | solution.py:50
  29.6 24.0 %collective-permute-start.3 = (bf16[384,512]{1,0:T(8,128)(2,1)}, bf16[384,512]{1,0:T(8,128)(2,1)S(1)}, u32[]{:S(2)}, u32[]{:S(2)}) collective-permute-start(bf16[384,512]{1,0:T(8,128)(2,1)} %copy-done.2), channel_id=1, source_target_pairs={{0,1},{8,9},{16,17},{24,25},{4,5},{12,13},{20,21},{28,29},{1,2},{9... | collective-permute-start | bytes 1179656 | tf_op jit(solution)/shard_map/ppermute | solution.py:50
  33.8 25.3 %collective-permute-start.12 = (bf16[384,512]{1,0:T(8,128)(2,1)S(1)}, bf16[384,512]{1,0:T(8,128)(2,1)S(1)}, u32[]{:S(2)}, u32[]{:S(2)}) collective-permute-start(bf16[384,512]{1,0:T(8,128)(2,1)S(1)} %collective-permute-done.4.refs_3_), channel_id=1, source_target_pairs={{0,4},{8,12},{16,20},{24,28},{4,0},{12,8},{20,16},{28,24},{1,5},{9... | collective-permute-start | bytes 1179656 | tf_op jit(solution)/shard_map/ppermute | solution.py:50
  41.1 18.0 %collective-permute-start.13 = (bf16[384,512]{1,0:T(8,128)(2,1)S(1)}, bf16[384,512]{1,0:T(8,128)(2,1)S(1)}, u32[]{:S(2)}, u32[]{:S(2)}) collective-permute-start(bf16[384,512]{1,0:T(8,128)(2,1)S(1)} %collective-permute-done.5.refs_4_), channel_id=1, source_target_pairs={{0,4},{8,12},{16,20},{24,28},{4,0},{12,8},{20,16},{28,24},{1,5},{9... | collective-permute-start | bytes 1179656 | tf_op jit(solution)/shard_map/ppermute | solution.py:50
  45.0 18.4 %collective-permute-start.14 = (bf16[384,512]{1,0:T(8,128)(2,1)S(1)}, bf16[384,512]{1,0:T(8,128)(2,1)S(1)}, u32[]{:S(2)}, u32[]{:S(2)}) collective-permute-start(bf16[384,512]{1,0:T(8,128)(2,1)S(1)} %collective-permute-done.refs_3_.refs_5_), channel_id=1, source_target_pairs={{0,4},{8,12},{16,20},{24,28},{4,0},{12,8},{20,16},{28,24},{1,5},{9... | collective-permute-start | bytes 1179656 | tf_op jit(solution)/shard_map/ppermute | solution.py:50
  45.0 25.1 %collective-permute-start.15 = (bf16[384,512]{1,0:T(8,128)(2,1)S(1)}, bf16[384,512]{1,0:T(8,128)(2,1)S(1)}, u32[]{:S(2)}, u32[]{:S(2)}) collective-permute-start(bf16[384,512]{1,0:T(8,128)(2,1)S(1)} %collective-permute-done.1.refs_4_.refs_6_), channel_id=1, source_target_pairs={{0,4},{8,12},{16,20},{24,28},{4,0},{12,8},{20,16},{28,24},{1,5},{9... | collective-permute-start | bytes 1179656 | tf_op jit(solution)/shard_map/ppermute | solution.py:50
  59.1 18.2 %collective-permute-start.8 = (f16[4,512,256]{2,1,0:T(8,128)(2,1)}, f16[4,512,256]{2,1,0:T(8,128)(2,1)}, u32[]{:S(2)}, u32[]{:S(2)}) collective-permute-start(f16[4,512,256]{2,1,0:T(8,128)(2,1)} %convert_element_type.123), channel_id=1, source_target_pairs={{0,8},{8,0},{16,24},{24,16},{4,12},{12,4},{20,28},{28,20},{1,9},{9... | collective-permute-start | bytes 3145736 | tf_op jit(solution)/shard_map/ppermute | solution.py:50
  75.7 1.2 copy-start.1
  75.9 5.9 %collective-permute-start.16 = (f16[4,512,256]{2,1,0:T(8,128)(2,1)S(1)}, f16[4,512,256]{2,1,0:T(8,128)(2,1)}, u32[]{:S(2)}, u32[]{:S(2)}) collective-permute-start(f16[4,512,256]{2,1,0:T(8,128)(2,1)S(1)} %convert_element_type.136), channel_id=1, source_target_pairs={{0,8},{8,0},{16,24},{24,16},{4,12},{12,4},{20,28},{28,20},{1,9},{9... | collective-permute-start | bytes 3145736 | tf_op jit(solution)/shard_map/ppermute | solution.py:50
  79.1 10.8 %collective-permute-start.11 = (f16[512,256]{1,0:T(8,128)(2,1)S(1)}, f16[512,256]{1,0:T(8,128)(2,1)S(1)}, u32[]{:S(2)}, u32[]{:S(2)}) collective-permute-start(f16[512,256]{1,0:T(8,128)(2,1)S(1)} %get-tuple-element.42), channel_id=1, source_target_pairs={{0,64},{8,72},{16,80},{24,88},{4,68},{12,76},{20,84},{28,92},{1,65... | collective-permute-start | bytes 786440 | tf_op jit(solution)/shard_map/ppermute | solution.py:50
  79.7 14.9 %collective-permute-start.10 = (f16[512,256]{1,0:T(8,128)(2,1)S(1)}, f16[512,256]{1,0:T(8,128)(2,1)S(1)}, u32[]{:S(2)}, u32[]{:S(2)}) collective-permute-start(f16[512,256]{1,0:T(8,128)(2,1)S(1)} %get-tuple-element.41), channel_id=1, source_target_pairs={{0,96},{8,104},{16,112},{24,120},{4,100},{12,108},{20,116},{28,124... | collective-permute-start | bytes 786440 | tf_op jit(solution)/shard_map/ppermute | solution.py:50
  81.8 13.7 %collective-permute-start.9 = (f16[512,256]{1,0:T(8,128)(2,1)S(1)}, f16[512,256]{1,0:T(8,128)(2,1)S(1)}, u32[]{:S(2)}, u32[]{:S(2)}) collective-permute-start(f16[512,256]{1,0:T(8,128)(2,1)S(1)} %get-tuple-element.40), channel_id=1, source_target_pairs={{0,32},{8,40},{16,48},{24,56},{4,36},{12,44},{20,52},{28,60},{1,33... | collective-permute-start | bytes 786440 | tf_op jit(solution)/shard_map/ppermute | solution.py:50
  83.7 14.7 %collective-permute-start.19 = (f16[256,256]{1,0:T(8,128)(2,1)S(1)}, f16[256,256]{1,0:T(8,128)(2,1)S(1)}, u32[]{:S(2)}, u32[]{:S(2)}) collective-permute-start(f16[256,256]{1,0:T(8,128)(2,1)S(1)} %get-tuple-element.74), channel_id=1, source_target_pairs={{0,64},{8,72},{16,80},{24,88},{4,68},{12,76},{20,84},{28,92},{1,65... | collective-permute-start | bytes 393224 | tf_op jit(solution)/shard_map/ppermute | solution.py:50
  86.7 13.8 %collective-permute-start.18 = (f16[256,256]{1,0:T(8,128)(2,1)S(1)}, f16[256,256]{1,0:T(8,128)(2,1)S(1)}, u32[]{:S(2)}, u32[]{:S(2)}) collective-permute-start(f16[256,256]{1,0:T(8,128)(2,1)S(1)} %get-tuple-element.72), channel_id=1, source_target_pairs={{0,96},{8,104},{16,112},{24,120},{4,100},{12,108},{20,116},{28,124... | collective-permute-start | bytes 393224 | tf_op jit(solution)/shard_map/ppermute | solution.py:50
  89.9 10.6 %collective-permute-start.17 = (f16[256,256]{1,0:T(8,128)(2,1)S(1)}, f16[256,256]{1,0:T(8,128)(2,1)S(1)}, u32[]{:S(2)}, u32[]{:S(2)}) collective-permute-start(f16[256,256]{1,0:T(8,128)(2,1)S(1)} %get-tuple-element.70), channel_id=1, source_target_pairs={{0,32},{8,40},{16,48},{24,56},{4,36},{12,44},{20,52},{28,60},{1,33... | collective-permute-start | bytes 393224 | tf_op jit(solution)/shard_map/ppermute | solution.py:50
  95.7 8.2 %collective-permute-start.22 = (f16[256,256]{1,0:T(8,128)(2,1)S(1)}, f16[256,256]{1,0:T(8,128)(2,1)S(1)}, u32[]{:S(2)}, u32[]{:S(2)}) collective-permute-start(f16[256,256]{1,0:T(8,128)(2,1)S(1)} %get-tuple-element.71), channel_id=1, source_target_pairs={{0,32},{8,40},{16,48},{24,56},{4,36},{12,44},{20,52},{28,60},{1,33... | collective-permute-start | bytes 393224 | tf_op jit(solution)/shard_map/ppermute | solution.py:50
  96.9 6.9 %collective-permute-start.23 = (f16[256,256]{1,0:T(8,128)(2,1)S(1)}, f16[256,256]{1,0:T(8,128)(2,1)S(1)}, u32[]{:S(2)}, u32[]{:S(2)}) collective-permute-start(f16[256,256]{1,0:T(8,128)(2,1)S(1)} %get-tuple-element.73), channel_id=1, source_target_pairs={{0,96},{8,104},{16,112},{24,120},{4,100},{12,108},{20,116},{28,124... | collective-permute-start | bytes 393224 | tf_op jit(solution)/shard_map/ppermute | solution.py:50
  98.3 7.2 %collective-permute-start.24 = (f16[256,256]{1,0:T(8,128)(2,1)S(1)}, f16[256,256]{1,0:T(8,128)(2,1)S(1)}, u32[]{:S(2)}, u32[]{:S(2)}) collective-permute-start(f16[256,256]{1,0:T(8,128)(2,1)S(1)} %get-tuple-element.75), channel_id=1, source_target_pairs={{0,64},{8,72},{16,80},{24,88},{4,68},{12,76},{20,84},{28,92},{1,65... | collective-permute-start | bytes 393224 | tf_op jit(solution)/shard_map/ppermute | solution.py:50
  100.6 5.0 %collective-permute-start.20 = (f16[256,256]{1,0:T(8,128)(2,1)S(1)}, f16[256,256]{1,0:T(8,128)(2,1)S(1)}, u32[]{:S(2)}, u32[]{:S(2)}) collective-permute-start(f16[256,256]{1,0:T(8,128)(2,1)S(1)} %select_convert_fusion.1), channel_id=1, source_target_pairs={{0,16},{8,24},{16,0},{24,8},{4,20},{12,28},{20,4},{28,12},{1,17},{... | collective-permute-start | bytes 393224 | tf_op jit(solution)/shard_map/ppermute | solution.py:55
  105.8 5.0 %collective-permute-start.25 = (f16[256,256]{1,0:T(8,128)(2,1)S(1)}, f16[256,256]{1,0:T(8,128)(2,1)S(1)}, u32[]{:S(2)}, u32[]{:S(2)}) collective-permute-start(f16[256,256]{1,0:T(8,128)(2,1)S(1)} %get-tuple-element.69), channel_id=1, source_target_pairs={{0,16},{8,24},{16,0},{24,8},{4,20},{12,28},{20,4},{28,12},{1,17},{... | collective-permute-start | bytes 393224 | tf_op jit(solution)/shard_map/ppermute | solution.py:55
  107.2 8.5 %collective-permute-start.21 = (f16[256,256]{1,0:T(8,128)(2,1)S(1)}, f16[256,256]{1,0:T(8,128)(2,1)S(1)}, u32[]{:S(2)}, u32[]{:S(2)}) collective-permute-start(f16[256,256]{1,0:T(8,128)(2,1)S(1)} %get-tuple-element.68), channel_id=1, source_target_pairs={{0,21},{8,29},{16,19},{24,27},{4,23},{12,31},{20,116},{28,124},{1,... | collective-permute-start | bytes 393224 | tf_op jit(solution)/shard_map/ppermute | solution.py:69
  111.0 11.6 %collective-permute-start.26 = (f16[256,256]{1,0:T(8,128)(2,1)S(1)}, f16[256,256]{1,0:T(8,128)(2,1)S(1)}, u32[]{:S(2)}, u32[]{:S(2)}) collective-permute-start(f16[256,256]{1,0:T(8,128)(2,1)S(1)} %add_convert_fusion), channel_id=1, source_target_pairs={{0,21},{8,29},{16,19},{24,27},{4,23},{12,31},{20,116},{28,124},{1,... | collective-permute-start | bytes 393224 | tf_op jit(solution)/shard_map/ppermute | solution.py:69

commit v5 on v4

--- a/solution.py
+++ b/solution.py
@@ -99,8 +99,8 @@
 
 
 COUNT = len(CUTS)
-TAIL = (256, 512)
-SPLIT = 2
+TAIL = (320, 512)
+SPLIT = 3
 
 
 def stage_kernel(late, lo, hi, n_in, *refs):
@@ -223,8 +223,10 @@
             (theirs.astype(jnp.float16), mine.astype(jnp.float16))
         )
         theirs = shift(theirs, swap=True)
-        theirs, mine = theirs.astype(jnp.float32), mine.astype(jnp.float32)
-        joined = [mine[d] + theirs[d] for d in range(4)]
+        joined = [
+            mine[d].astype(jnp.float32) + theirs[d].astype(jnp.float32)
+            for d in range(4)
+        ]
         kept, *sent = lax.optimization_barrier(
             [joined[0]] + [joined[d].astype(jnp.float16) for d in (1, 3, 2)]
         )

time: 124 us -> 130 us (1.048)
  the two profiles are of different devices: /device:TPU:4 before, /device:TPU:24 now
where the time goes in v5:
time: 130 us; the launch traced here: 129 us
  waiting for transfers between devices  66.6 us (51%)
  starting transfers between devices  32.4 us (25%)
  Pallas kernels  12.8 us (10%)
  other arithmetic  10.5 us (8%)
  local copies, waits for them, and re-layouts  6.75 us (5%)
    ppermute x23, waiting for transfers between devices, shift(): return lax.ppermute(value, AXES, pairs)  55 us
    ppermute x23, starting transfers between devices, shift(): return lax.ppermute(value, AXES, pairs)  29.5 us
    pallas_call x3, Pallas kernels, run_stage(): pl.pallas_call(functools.partial(stage_kernel, late, lo, hi, len(sources)...  12.8 us
    ppermute x2, waiting for transfers between devices, to_owner(): return lax.ppermute(value, AXES, pairs)  6.72 us
    ppermute x2, waiting for transfers between devices, swap_z_lo(): return lax.ppermute(value, AXES, pairs)  4.86 us
    slice x2, local copies, waits for them, and re-layouts, rows(): return block[starts[k]:starts[k + 1]]  4.09 us
    convert_element_type x2, other arithmetic, over_x(): joined[d].astype(jnp.float16)  2.96 us
    ppermute x2, starting transfers between devices, swap_z_lo(): return lax.ppermute(value, AXES, pairs)  2.74 us
  transfers between devices with their start and end apart: 27, of which 16 were waited for; matrix products, arithmetic and copies ran while one was open for 9% of the time, Pallas kernels for 10%

profile of v5, /device:TPU:24, one launch (start us, length us, event | category | flops | bytes accessed | tf_op | source)
XLA Modules:
  0.0 129.2 jit_solution(2180002937201760235)
XLA Ops:
  0.0 1.9 %slice.92 = bf16[384,512]{1,0:T(8,128)(2,1)} slice(bf16[1536,512]{1,0:T(8,128)(2,1)} %refs_2_.5), slice={[0:384], [0:512]} | slice | bytes 786432 | tf_op jit(solution)/shard_map/slice | solution.py:210
  1.9 2.2 %fusion.7 = (bf16[384,512]{1,0:T(8,128)(2,1)}, bf16[384,512]{1,0:T(8,128)(2,1)}, bf16[384,512]{1,0:T(8,128)(2,1)S(1)}) fusion(bf16[1536,512]{1,0:T(8,128)(2,1)} %refs_2_.5), kind=kLoop, calls=%fused_computation.29 | loop fusion | bytes 2359296 | tf_op jit(solution)/shard_map/slice | solution.py:210
  4.1 0.7 collective-permute-start
  4.8 0.4 collective-permute-start.2
  5.3 2.8 %collective-permute-start.5 = (bf16[384,512]{1,0:T(8,128)(2,1)}, bf16[384,512]{1,0:T(8,128)(2,1)S(1)}, u32[]{:S(2)}, u32[]{:S(2)}) collective-permute-start(bf16[384,512]{1,0:T(8,128)(2,1)} %slice.92), channel_id=1, source_target_pairs={{0,1},{8,9},{16,17},{24,25},{4,5},{12,13},{20,21},{28,29},{1,2},{9... | collective-permute-start | bytes 1179656 | tf_op jit(solution)/shard_map/ppermute | solution.py:50
  8.1 3.2 %collective-permute-start.6 = (bf16[384,512]{1,0:T(8,128)(2,1)}, bf16[384,512]{1,0:T(8,128)(2,1)}, u32[]{:S(2)}, u32[]{:S(2)}) collective-permute-start(bf16[384,512]{1,0:T(8,128)(2,1)} %get-tuple-element.66), channel_id=1, source_target_pairs={{0,1},{8,9},{16,17},{24,25},{4,5},{12,13},{20,21},{28,29},{1,2},{9... | collective-permute-start | bytes 1179656 | tf_op jit(solution)/shard_map/ppermute | solution.py:50
  11.3 6.0 %collective-permute-done.refs_3_.refs_6_ = bf16[384,512]{1,0:T(8,128)(2,1)S(1)} collective-permute-done((bf16[384,512]{1,0:T(8,128)(2,1)S(1)}, bf16[384,512]{1,0:T(8,128)(2,1)S(1)}, u32[]{:S(2)}, u32[]{:S(2)}) %collective-permute-start) | collective-permute-done | bytes 393248 | tf_op jit(solution)/shard_map/ppermute | solution.py:50
  17.3 8.4 %collective-permute-done.2.refs_3_ = bf16[384,512]{1,0:T(8,128)(2,1)S(1)} collective-permute-done((bf16[384,512]{1,0:T(8,128)(2,1)}, bf16[384,512]{1,0:T(8,128)(2,1)S(1)}, u32[]{:S(2)}, u32[]{:S(2)}) %collective-permute-start.2) | collective-permute-done | bytes 393248 | tf_op jit(solution)/shard_map/ppermute | solution.py:50
  25.7 0.5 select_reduce_fusion.1
  26.3 1.6 %copy.7 = bf16[1536,512]{0,1:T(8,128)(2,1)} copy(bf16[1536,512]{1,0:T(8,128)(2,1)S(1)} %copy-done) | data formatting | bytes 3145728 | tf_op args[0]
  27.9 1.2 select_reduce_fusion
  29.1 5.1 %collective-permute-done.3.refs_4_ = bf16[384,512]{1,0:T(8,128)(2,1)S(1)} collective-permute-done((bf16[384,512]{1,0:T(8,128)(2,1)}, bf16[384,512]{1,0:T(8,128)(2,1)S(1)}, u32[]{:S(2)}, u32[]{:S(2)}) %collective-permute-start.3) | collective-permute-done | bytes 393248 | tf_op jit(solution)/shard_map/ppermute | solution.py:50
  34.2 7.3 %collective-permute-done.4.refs_5_ = bf16[384,512]{1,0:T(8,128)(2,1)S(1)} collective-permute-done((bf16[384,512]{1,0:T(8,128)(2,1)}, bf16[384,512]{1,0:T(8,128)(2,1)S(1)}, u32[]{:S(2)}, u32[]{:S(2)}) %collective-permute-start.4) | collective-permute-done | bytes 393248 | tf_op jit(solution)/shard_map/ppermute | solution.py:50
  41.4 3.9 %collective-permute-start.12 = (bf16[384,512]{1,0:T(8,128)(2,1)S(1)}, bf16[384,512]{1,0:T(8,128)(2,1)S(1)}, u32[]{:S(2)}, u32[]{:S(2)}) collective-permute-start(bf16[384,512]{1,0:T(8,128)(2,1)S(1)} %collective-permute-done.2.refs_3_), channel_id=1, source_target_pairs={{0,4},{8,12},{16,20},{24,28},{4,0},{12,8},{20,16},{28,24},{1,5},{9... | collective-permute-start | bytes 1179656 | tf_op jit(solution)/shard_map/ppermute | solution.py:50
  45.4 3.5 %collective-permute-start.14 = (bf16[384,512]{1,0:T(8,128)(2,1)S(1)}, bf16[384,512]{1,0:T(8,128)(2,1)S(1)}, u32[]{:S(2)}, u32[]{:S(2)}) collective-permute-start(bf16[384,512]{1,0:T(8,128)(2,1)S(1)} %collective-permute-done.4.refs_5_), channel_id=1, source_target_pairs={{0,4},{8,12},{16,20},{24,28},{4,0},{12,8},{20,16},{28,24},{1,5},{9... | collective-permute-start | bytes 1179656 | tf_op jit(solution)/shard_map/ppermute | solution.py:50
  49.0 1.7 %fusion.refs_1_ = bf16[512,1536]{1,0:T(8,128)(2,1)S(1)} fusion(bf16[1536,512]{0,1:T(8,128)(2,1)} %copy.7, f32[1536]{0:T(1024)S(1)} %multiply_divide_fusion), kind=kLoop, calls=%fused_computation.1 | loop fusion | flops 2359296 | bytes 3151872 | tf_op jit(solution)/shard_map/convert_element_type | solution.py:243
  50.6 5.2 %shard_map.55 = (f32[4,512,512]{2,1,0:T(8,128)S(1)}, bf16[512,1152]{1,0:T(8,128)(2,1)S(1)}) custom-call(f32[1,1536]{1,0:T(1,128)S(1)} %div.19.refs_0_, bf16[512,1536]{1,0:T(8,128)(2,1)S(1)} %fusion.refs_1_, bf16[1536,512]{1,0:T(8,128)(2,1)S(1)} %copy-done, bf16[384,512]{1,0:T(8,128)(2,1)S(1)} %collective-permute-done.2.refs_3_, ...), custom_call_target="tpu_custom_call" | custom-call | flops 2415919104 | bytes 8388608 | tf_op jit(solution)/shard_map/pallas_call | solution.py:188
  55.8 2.2 %shard_map.56 = (f32[4,512,256]{2,1,0:T(8,128)S(1)}, f32[4,512,256]{2,1,0:T(8,128)S(1)}, bf16[512,384]{1,0:T(8,128)(2,1)S(1)}) custom-call(f32[1,1536]{1,0:T(1,128)S(1)} %div.19.refs_0_, bf16[512,1536]{1,0:T(8,128)(2,1)S(1)} %fusion.refs_1_, bf16[1536,512]{1,0:T(8,128)(2,1)S(1)} %copy-done, bf16[384,512]{1,0:T(8,128)(2,1)S(1)} %collective-permute-done.refs_3_.refs_6_, ...), custom_call_target="tpu_custom_call" | custom-call | flops 805306368 | bytes 8388608 | tf_op jit(solution)/shard_map/pallas_call | solution.py:188
  58.0 1.2 convert_element_type.175
  59.2 1.2 convert_element_type.176
  60.5 3.3 %collective-permute-done.13.refs_8_ = bf16[384,512]{1,0:T(8,128)(2,1)S(1)} collective-permute-done((bf16[384,512]{1,0:T(8,128)(2,1)S(1)}, bf16[384,512]{1,0:T(8,128)(2,1)S(1)}, u32[]{:S(2)}, u32[]{:S(2)}) %collective-permute-start.13) | collective-permute-done | bytes 393248 | tf_op jit(solution)/shard_map/ppermute | solution.py:50
  63.7 8.4 %collective-permute-done.14.refs_9_ = bf16[384,512]{1,0:T(8,128)(2,1)S(1)} collective-permute-done((bf16[384,512]{1,0:T(8,128)(2,1)S(1)}, bf16[384,512]{1,0:T(8,128)(2,1)S(1)}, u32[]{:S(2)}, u32[]{:S(2)}) %collective-permute-start.14) | collective-permute-done | bytes 393248 | tf_op jit(solution)/shard_map/ppermute | solution.py:50
  72.1 6.7 %collective-permute-done.15.refs_10_ = bf16[384,512]{1,0:T(8,128)(2,1)S(1)} collective-permute-done((bf16[384,512]{1,0:T(8,128)(2,1)S(1)}, bf16[384,512]{1,0:T(8,128)(2,1)S(1)}, u32[]{:S(2)}, u32[]{:S(2)}) %collective-permute-start.15) | collective-permute-done | bytes 393248 | tf_op jit(solution)/shard_map/ppermute | solution.py:50
  78.9 5.4 %shard_map.57 = (f32[4,512,256]{2,1,0:T(8,128)S(1)}, f32[4,512,256]{2,1,0:T(8,128)S(1)}) custom-call(f32[1,1536]{1,0:T(1,128)S(1)} %div.19.refs_0_, bf16[512,1536]{1,0:T(8,128)(2,1)S(1)} %fusion.refs_1_, bf16[1536,512]{1,0:T(8,128)(2,1)S(1)} %copy-done, bf16[384,512]{1,0:T(8,128)(2,1)S(1)} %collective-permute-done.2.refs_3_, ...), custom_call_target="tpu_custom_call" | custom-call | flops 3221225472 | bytes 8388608 | tf_op jit(solution)/shard_map/pallas_call | solution.py:188
  84.3 0.2 convert_element_type.194
  84.9 0.9 copy-done.1
  85.7 1.5 %fusion.3 = (f16[512,256]{1,0:T(8,128)(2,1)S(1)}, f16[512,256]{1,0:T(8,128)(2,1)S(1)}, f16[512,256]{1,0:T(8,128)(2,1)S(1)}, f32[512,256]{1,0:T(8,128)S(1)}) fusion(f16[4,512,256]{2,1,0:T(8,128)(2,1)} %collective-permute-done.8, f16[4,512,256]{2,1,0:T(8,128)(2,1)S(1)} %copy-done.1), kind=kLoop, calls=%fused_computation.21 | loop fusion | flops 1966080 | bytes 3407872 | tf_op jit(solution)/shard_map/convert_element_type | solution.py:231
  87.2 3.1 %collective-permute-start.11 = (f16[512,256]{1,0:T(8,128)(2,1)S(1)}, f16[512,256]{1,0:T(8,128)(2,1)S(1)}, u32[]{:S(2)}, u32[]{:S(2)}) collective-permute-start(f16[512,256]{1,0:T(8,128)(2,1)S(1)} %get-tuple-element.42), channel_id=1, source_target_pairs={{0,64},{8,72},{16,80},{24,88},{4,68},{12,76},{20,84},{28,92},{1,65... | collective-permute-start | bytes 786440 | tf_op jit(solution)/shard_map/ppermute | solution.py:50
  90.3 1.1 collective-permute-start.10
  91.4 0.9 collective-permute-start.9
  92.3 1.5 %fusion.6 = (f16[512,256]{1,0:T(8,128)(2,1)S(1)}, f16[512,256]{1,0:T(8,128)(2,1)S(1)}, f16[512,256]{1,0:T(8,128)(2,1)S(1)}, f32[512,256]{1,0:T(8,128)S(1)}) fusion(f16[4,512,256]{2,1,0:T(8,128)(2,1)} %collective-permute-done.16, f16[4,512,256]{2,1,0:T(8,128)(2,1)S(1)} %convert_element_type.195), kind=kLoop, calls=%fused_computation.24 | loop fusion | flops 1966080 | bytes 3407872 | tf_op jit(solution)/shard_map/convert_element_type | solution.py:231
  93.8 0.7 collective-permute-start.19
  94.6 2.7 %collective-permute-start.18 = (f16[320,256]{1,0:T(8,128)(2,1)S(1)}, f16[320,256]{1,0:T(8,128)(2,1)S(1)}, u32[]{:S(2)}, u32[]{:S(2)}) collective-permute-start(f16[320,256]{1,0:T(8,128)(2,1)S(1)} %slice.115), channel_id=1, source_target_pairs={{0,96},{8,104},{16,112},{24,120},{4,100},{12,108},{20,116},{28,124... | collective-permute-start | bytes 491528 | tf_op jit(solution)/shard_map/ppermute | solution.py:50
  97.3 0.6 collective-permute-done.11
  98.0 1.5 %collective-permute-start.17 = (f16[320,256]{1,0:T(8,128)(2,1)S(1)}, f16[320,256]{1,0:T(8,128)(2,1)S(1)}, u32[]{:S(2)}, u32[]{:S(2)}) collective-permute-start(f16[320,256]{1,0:T(8,128)(2,1)S(1)} %slice.114), channel_id=1, source_target_pairs={{0,32},{8,40},{16,48},{24,56},{4,36},{12,44},{20,52},{28,60},{1,33... | collective-permute-start | bytes 491528 | tf_op jit(solution)/shard_map/ppermute | solution.py:50
  99.5 4.2 %collective-permute-done.10 = f16[512,256]{1,0:T(8,128)(2,1)S(1)} collective-permute-done((f16[512,256]{1,0:T(8,128)(2,1)S(1)}, f16[512,256]{1,0:T(8,128)(2,1)S(1)}, u32[]{:S(2)}, u32[]{:S(2)}) %collective-permute-start.10) | collective-permute-done | bytes 262176 | tf_op jit(solution)/shard_map/ppermute | solution.py:50
  103.7 1.6 %collective-permute-done.9 = f16[512,256]{1,0:T(8,128)(2,1)S(1)} collective-permute-done((f16[512,256]{1,0:T(8,128)(2,1)S(1)}, f16[512,256]{1,0:T(8,128)(2,1)S(1)}, u32[]{:S(2)}, u32[]{:S(2)}) %collective-permute-start.9) | collective-permute-done | bytes 262176 | tf_op jit(solution)/shard_map/ppermute | solution.py:50
  105.6 3.2 %collective-permute-start.23 = (f16[192,256]{1,0:T(8,128)(2,1)S(1)}, f16[192,256]{1,0:T(8,128)(2,1)S(1)}, u32[]{:S(2)}, u32[]{:S(2)}) collective-permute-start(f16[192,256]{1,0:T(8,128)(2,1)S(1)} %slice.120), channel_id=1, source_target_pairs={{0,96},{8,104},{16,112},{24,120},{4,100},{12,108},{20,116},{28,124... | collective-permute-start | bytes 294920 | tf_op jit(solution)/shard_map/ppermute | solution.py:50
  108.8 1.3 %collective-permute-start.24 = (f16[192,256]{1,0:T(8,128)(2,1)S(1)}, f16[192,256]{1,0:T(8,128)(2,1)S(1)}, u32[]{:S(2)}, u32[]{:S(2)}) collective-permute-start(f16[192,256]{1,0:T(8,128)(2,1)S(1)} %slice.121), channel_id=1, source_target_pairs={{0,64},{8,72},{16,80},{24,88},{4,68},{12,76},{20,84},{28,92},{1,65... | collective-permute-start | bytes 294920 | tf_op jit(solution)/shard_map/ppermute | solution.py:50
  110.2 0.6 collective-permute-done.18
  110.8 1.4 %collective-permute-start.20 = (f16[320,256]{1,0:T(8,128)(2,1)S(1)}, f16[320,256]{1,0:T(8,128)(2,1)S(1)}, u32[]{:S(2)}, u32[]{:S(2)}) collective-permute-start(f16[320,256]{1,0:T(8,128)(2,1)S(1)} %select_convert_fusion), channel_id=1, source_target_pairs={{0,16},{8,24},{16,0},{24,8},{4,20},{12,28},{20,4},{28,12},{1,17},{... | collective-permute-start | bytes 491528 | tf_op jit(solution)/shard_map/ppermute | solution.py:55
  112.2 0.3 collective-permute-done.23
  112.5 2.4 %collective-permute-done.24 = f16[192,256]{1,0:T(8,128)(2,1)S(1)} collective-permute-done((f16[192,256]{1,0:T(8,128)(2,1)S(1)}, f16[192,256]{1,0:T(8,128)(2,1)S(1)}, u32[]{:S(2)}, u32[]{:S(2)}) %collective-permute-start.24) | collective-permute-done | bytes 98336 | tf_op jit(solution)/shard_map/ppermute | solution.py:50
  115.0 1.4 %collective-permute-start.25 = (f16[192,256]{1,0:T(8,128)(2,1)S(1)}, f16[192,256]{1,0:T(8,128)(2,1)S(1)}, u32[]{:S(2)}, u32[]{:S(2)}) collective-permute-start(f16[192,256]{1,0:T(8,128)(2,1)S(1)} %select_convert_fusion.1), channel_id=1, source_target_pairs={{0,16},{8,24},{16,0},{24,8},{4,20},{12,28},{20,4},{28,12},{1,17},{... | collective-permute-start | bytes 294920 | tf_op jit(solution)/shard_map/ppermute | solution.py:55
  116.4 0.9 collective-permute-done.20
  117.5 4.0 %collective-permute-done.25 = f16[192,256]{1,0:T(8,128)(2,1)S(1)} collective-permute-done((f16[192,256]{1,0:T(8,128)(2,1)S(1)}, f16[192,256]{1,0:T(8,128)(2,1)S(1)}, u32[]{:S(2)}, u32[]{:S(2)}) %collective-permute-start.25) | collective-permute-done | bytes 98336 | tf_op jit(solution)/shard_map/ppermute | solution.py:55
  121.6 6.7 %collective-permute-done.26 = f16[192,256]{1,0:T(8,128)(2,1)S(1)} collective-permute-done((f16[192,256]{1,0:T(8,128)(2,1)S(1)}, f16[192,256]{1,0:T(8,128)(2,1)S(1)}, u32[]{:S(2)}, u32[]{:S(2)}) %collective-permute-start.26) | collective-permute-done | bytes 98336 | tf_op jit(solution)/shard_map/ppermute | solution.py:69
  128.4 0.8 convert_multiply_fusion
  (47 shorter events, 1.4 us)
Async XLA Ops:
  0.0 26.2 %copy-start = (bf16[1536,512]{1,0:T(8,128)(2,1)S(1)}, bf16[1536,512]{1,0:T(8,128)(2,1)}, u32[]{:S(2)}) copy-start(bf16[1536,512]{1,0:T(8,128)(2,1)} %refs_2_.5) | copy-start | bytes 4718596
  0.0 25.7 %copy-start.5 = (f32[128]{0:T(128)S(1)}, f32[128]{0:T(128)}, u32[]{:S(2)}) copy-start(f32[128]{0:T(128)} %param.8) | copy-start | bytes 1540
  0.0 25.7 %copy-start.3 = (s32[1536]{0:T(1024)S(1)}, s32[1536]{0:T(1024)}, u32[]{:S(2)}) copy-start(s32[1536]{0:T(1024)} %param.6) | copy-start | bytes 18436
  4.1 13.2 %copy-start.2 = (bf16[384,512]{1,0:T(8,128)(2,1)}, bf16[384,512]{1,0:T(8,128)(2,1)S(1)}, u32[]{:S(2)}) copy-start(bf16[384,512]{1,0:T(8,128)(2,1)S(1)} %get-tuple-element.67) | copy-start | bytes 1179652
  4.1 13.2 %collective-permute-start = (bf16[384,512]{1,0:T(8,128)(2,1)S(1)}, bf16[384,512]{1,0:T(8,128)(2,1)S(1)}, u32[]{:S(2)}, u32[]{:S(2)}) collective-permute-start(bf16[384,512]{1,0:T(8,128)(2,1)S(1)} %get-tuple-element.67), channel_id=1, source_target_pairs={{0,3},{8,11},{16,19},{24,27},{4,7},{12,15},{20,23},{28,31},{1,0},{... | collective-permute-start | bytes 1179656 | tf_op jit(solution)/shard_map/ppermute | solution.py:50
  4.8 20.9 %collective-permute-start.2 = (bf16[384,512]{1,0:T(8,128)(2,1)}, bf16[384,512]{1,0:T(8,128)(2,1)S(1)}, u32[]{:S(2)}, u32[]{:S(2)}) collective-permute-start(bf16[384,512]{1,0:T(8,128)(2,1)} %slice.92), channel_id=1, source_target_pairs={{0,3},{8,11},{16,19},{24,27},{4,7},{12,15},{20,23},{28,31},{1,0},{... | collective-permute-start | bytes 1179656 | tf_op jit(solution)/shard_map/ppermute | solution.py:50
  5.3 40.0 %collective-permute-start.5 = (bf16[384,512]{1,0:T(8,128)(2,1)}, bf16[384,512]{1,0:T(8,128)(2,1)S(1)}, u32[]{:S(2)}, u32[]{:S(2)}) collective-permute-start(bf16[384,512]{1,0:T(8,128)(2,1)} %slice.92), channel_id=1, source_target_pairs={{0,1},{8,9},{16,17},{24,25},{4,5},{12,13},{20,21},{28,29},{1,2},{9... | collective-permute-start | bytes 1179656 | tf_op jit(solution)/shard_map/ppermute | solution.py:50
  8.1 26.1 %collective-permute-start.3 = (bf16[384,512]{1,0:T(8,128)(2,1)}, bf16[384,512]{1,0:T(8,128)(2,1)S(1)}, u32[]{:S(2)}, u32[]{:S(2)}) collective-permute-start(bf16[384,512]{1,0:T(8,128)(2,1)} %get-tuple-element.66), channel_id=1, source_target_pairs={{0,3},{8,11},{16,19},{24,27},{4,7},{12,15},{20,23},{28,31},{1,0},{... | collective-permute-start | bytes 1179656 | tf_op jit(solution)/shard_map/ppermute | solution.py:50
  8.1 37.3 %collective-permute-start.6 = (bf16[384,512]{1,0:T(8,128)(2,1)}, bf16[384,512]{1,0:T(8,128)(2,1)}, u32[]{:S(2)}, u32[]{:S(2)}) collective-permute-start(bf16[384,512]{1,0:T(8,128)(2,1)} %get-tuple-element.66), channel_id=1, source_target_pairs={{0,1},{8,9},{16,17},{24,25},{4,5},{12,13},{20,21},{28,29},{1,2},{9... | collective-permute-start | bytes 1179656 | tf_op jit(solution)/shard_map/ppermute | solution.py:50
  17.3 24.1 %collective-permute-start.4 = (bf16[384,512]{1,0:T(8,128)(2,1)}, bf16[384,512]{1,0:T(8,128)(2,1)S(1)}, u32[]{:S(2)}, u32[]{:S(2)}) collective-permute-start(bf16[384,512]{1,0:T(8,128)(2,1)} %get-tuple-element.65), channel_id=1, source_target_pairs={{0,3},{8,11},{16,19},{24,27},{4,7},{12,15},{20,23},{28,31},{1,0},{... | collective-permute-start | bytes 1179656 | tf_op jit(solution)/shard_map/ppermute | solution.py:50
  25.7 23.1 %collective-permute-start.7 = (bf16[384,512]{1,0:T(8,128)(2,1)}, bf16[384,512]{1,0:T(8,128)(2,1)}, u32[]{:S(2)}, u32[]{:S(2)}) collective-permute-start(bf16[384,512]{1,0:T(8,128)(2,1)} %get-tuple-element.65), channel_id=1, source_target_pairs={{0,1},{8,9},{16,17},{24,25},{4,5},{12,13},{20,21},{28,29},{1,2},{9... | collective-permute-start | bytes 1179656 | tf_op jit(solution)/shard_map/ppermute | solution.py:50
  26.2 1.6 %copy-start.4 = (s32[1536]{0:T(1024)S(1)}, s32[1536]{0:T(1024)}, u32[]{:S(2)}) copy-start(s32[1536]{0:T(1024)} %param.7) | copy-start | bytes 18436
  34.2 21.7 %collective-permute-start.1 = (bf16[384,512]{1,0:T(8,128)(2,1)}, bf16[384,512]{1,0:T(8,128)(2,1)S(1)}, u32[]{:S(2)}, u32[]{:S(2)}) collective-permute-start(bf16[384,512]{1,0:T(8,128)(2,1)} %copy-done.2), channel_id=1, source_target_pairs={{0,1},{8,9},{16,17},{24,25},{4,5},{12,13},{20,21},{28,29},{1,2},{9... | collective-permute-start | bytes 1179656 | tf_op jit(solution)/shard_map/ppermute | solution.py:50
  41.4 19.0 %collective-permute-start.12 = (bf16[384,512]{1,0:T(8,128)(2,1)S(1)}, bf16[384,512]{1,0:T(8,128)(2,1)S(1)}, u32[]{:S(2)}, u32[]{:S(2)}) collective-permute-start(bf16[384,512]{1,0:T(8,128)(2,1)S(1)} %collective-permute-done.2.refs_3_), channel_id=1, source_target_pairs={{0,4},{8,12},{16,20},{24,28},{4,0},{12,8},{20,16},{28,24},{1,5},{9... | collective-permute-start | bytes 1179656 | tf_op jit(solution)/shard_map/ppermute | solution.py:50
  45.3 18.4 %collective-permute-start.13 = (bf16[384,512]{1,0:T(8,128)(2,1)S(1)}, bf16[384,512]{1,0:T(8,128)(2,1)S(1)}, u32[]{:S(2)}, u32[]{:S(2)}) collective-permute-start(bf16[384,512]{1,0:T(8,128)(2,1)S(1)} %collective-permute-done.3.refs_4_), channel_id=1, source_target_pairs={{0,4},{8,12},{16,20},{24,28},{4,0},{12,8},{20,16},{28,24},{1,5},{9... | collective-permute-start | bytes 1179656 | tf_op jit(solution)/shard_map/ppermute | solution.py:50
  45.4 26.8 %collective-permute-start.14 = (bf16[384,512]{1,0:T(8,128)(2,1)S(1)}, bf16[384,512]{1,0:T(8,128)(2,1)S(1)}, u32[]{:S(2)}, u32[]{:S(2)}) collective-permute-start(bf16[384,512]{1,0:T(8,128)(2,1)S(1)} %collective-permute-done.4.refs_5_), channel_id=1, source_target_pairs={{0,4},{8,12},{16,20},{24,28},{4,0},{12,8},{20,16},{28,24},{1,5},{9... | collective-permute-start | bytes 1179656 | tf_op jit(solution)/shard_map/ppermute | solution.py:50
  48.9 30.0 %collective-permute-start.15 = (bf16[384,512]{1,0:T(8,128)(2,1)S(1)}, bf16[384,512]{1,0:T(8,128)(2,1)S(1)}, u32[]{:S(2)}, u32[]{:S(2)}) collective-permute-start(bf16[384,512]{1,0:T(8,128)(2,1)S(1)} %collective-permute-done.refs_3_.refs_6_), channel_id=1, source_target_pairs={{0,4},{8,12},{16,20},{24,28},{4,0},{12,8},{20,16},{28,24},{1,5},{9... | collective-permute-start | bytes 1179656 | tf_op jit(solution)/shard_map/ppermute | solution.py:50
  60.4 24.4 %collective-permute-start.8 = (f16[4,512,256]{2,1,0:T(8,128)(2,1)}, f16[4,512,256]{2,1,0:T(8,128)(2,1)}, u32[]{:S(2)}, u32[]{:S(2)}) collective-permute-start(f16[4,512,256]{2,1,0:T(8,128)(2,1)} %convert_element_type.175), channel_id=1, source_target_pairs={{0,8},{8,0},{16,24},{24,16},{4,12},{12,4},{20,28},{28,20},{1,9},{9... | collective-permute-start | bytes 3145736 | tf_op jit(solution)/shard_map/ppermute | solution.py:50
  84.5 1.2 copy-start.1
  84.7 7.6 %collective-permute-start.16 = (f16[4,512,256]{2,1,0:T(8,128)(2,1)S(1)}, f16[4,512,256]{2,1,0:T(8,128)(2,1)}, u32[]{:S(2)}, u32[]{:S(2)}) collective-permute-start(f16[4,512,256]{2,1,0:T(8,128)(2,1)S(1)} %convert_element_type.194), channel_id=1, source_target_pairs={{0,8},{8,0},{16,24},{24,16},{4,12},{12,4},{20,28},{28,20},{1,9},{9... | collective-permute-start | bytes 3145736 | tf_op jit(solution)/shard_map/ppermute | solution.py:50
  87.2 10.8 %collective-permute-start.11 = (f16[512,256]{1,0:T(8,128)(2,1)S(1)}, f16[512,256]{1,0:T(8,128)(2,1)S(1)}, u32[]{:S(2)}, u32[]{:S(2)}) collective-permute-start(f16[512,256]{1,0:T(8,128)(2,1)S(1)} %get-tuple-element.42), channel_id=1, source_target_pairs={{0,64},{8,72},{16,80},{24,88},{4,68},{12,76},{20,84},{28,92},{1,65... | collective-permute-start | bytes 786440 | tf_op jit(solution)/shard_map/ppermute | solution.py:50
  90.3 13.4 %collective-permute-start.10 = (f16[512,256]{1,0:T(8,128)(2,1)S(1)}, f16[512,256]{1,0:T(8,128)(2,1)S(1)}, u32[]{:S(2)}, u32[]{:S(2)}) collective-permute-start(f16[512,256]{1,0:T(8,128)(2,1)S(1)} %get-tuple-element.41), channel_id=1, source_target_pairs={{0,96},{8,104},{16,112},{24,120},{4,100},{12,108},{20,116},{28,124... | collective-permute-start | bytes 786440 | tf_op jit(solution)/shard_map/ppermute | solution.py:50
  91.4 13.9 %collective-permute-start.9 = (f16[512,256]{1,0:T(8,128)(2,1)S(1)}, f16[512,256]{1,0:T(8,128)(2,1)S(1)}, u32[]{:S(2)}, u32[]{:S(2)}) collective-permute-start(f16[512,256]{1,0:T(8,128)(2,1)S(1)} %get-tuple-element.40), channel_id=1, source_target_pairs={{0,32},{8,40},{16,48},{24,56},{4,36},{12,44},{20,52},{28,60},{1,33... | collective-permute-start | bytes 786440 | tf_op jit(solution)/shard_map/ppermute | solution.py:50
  93.8 15.0 %collective-permute-start.19 = (f16[320,256]{1,0:T(8,128)(2,1)S(1)}, f16[320,256]{1,0:T(8,128)(2,1)S(1)}, u32[]{:S(2)}, u32[]{:S(2)}) collective-permute-start(f16[320,256]{1,0:T(8,128)(2,1)S(1)} %slice.116), channel_id=1, source_target_pairs={{0,64},{8,72},{16,80},{24,88},{4,68},{12,76},{20,84},{28,92},{1,65... | collective-permute-start | bytes 491528 | tf_op jit(solution)/shard_map/ppermute | solution.py:50
  94.6 16.1 %collective-permute-start.18 = (f16[320,256]{1,0:T(8,128)(2,1)S(1)}, f16[320,256]{1,0:T(8,128)(2,1)S(1)}, u32[]{:S(2)}, u32[]{:S(2)}) collective-permute-start(f16[320,256]{1,0:T(8,128)(2,1)S(1)} %slice.115), channel_id=1, source_target_pairs={{0,96},{8,104},{16,112},{24,120},{4,100},{12,108},{20,116},{28,124... | collective-permute-start | bytes 491528 | tf_op jit(solution)/shard_map/ppermute | solution.py:50
  98.0 12.8 %collective-permute-start.17 = (f16[320,256]{1,0:T(8,128)(2,1)S(1)}, f16[320,256]{1,0:T(8,128)(2,1)S(1)}, u32[]{:S(2)}, u32[]{:S(2)}) collective-permute-start(f16[320,256]{1,0:T(8,128)(2,1)S(1)} %slice.114), channel_id=1, source_target_pairs={{0,32},{8,40},{16,48},{24,56},{4,36},{12,44},{20,52},{28,60},{1,33... | collective-permute-start | bytes 491528 | tf_op jit(solution)/shard_map/ppermute | solution.py:50
  105.5 6.7 %collective-permute-start.22 = (f16[192,256]{1,0:T(8,128)(2,1)S(1)}, f16[192,256]{1,0:T(8,128)(2,1)S(1)}, u32[]{:S(2)}, u32[]{:S(2)}) collective-permute-start(f16[192,256]{1,0:T(8,128)(2,1)S(1)} %slice.119), channel_id=1, source_target_pairs={{0,32},{8,40},{16,48},{24,56},{4,36},{12,44},{20,52},{28,60},{1,33... | collective-permute-start | bytes 294920 | tf_op jit(solution)/shard_map/ppermute | solution.py:50
  105.6 6.9 %collective-permute-start.23 = (f16[192,256]{1,0:T(8,128)(2,1)S(1)}, f16[192,256]{1,0:T(8,128)(2,1)S(1)}, u32[]{:S(2)}, u32[]{:S(2)}) collective-permute-start(f16[192,256]{1,0:T(8,128)(2,1)S(1)} %slice.120), channel_id=1, source_target_pairs={{0,96},{8,104},{16,112},{24,120},{4,100},{12,108},{20,116},{28,124... | collective-permute-start | bytes 294920 | tf_op jit(solution)/shard_map/ppermute | solution.py:50
  108.8 6.1 %collective-permute-start.24 = (f16[192,256]{1,0:T(8,128)(2,1)S(1)}, f16[192,256]{1,0:T(8,128)(2,1)S(1)}, u32[]{:S(2)}, u32[]{:S(2)}) collective-permute-start(f16[192,256]{1,0:T(8,128)(2,1)S(1)} %slice.121), channel_id=1, source_target_pairs={{0,64},{8,72},{16,80},{24,88},{4,68},{12,76},{20,84},{28,92},{1,65... | collective-permute-start | bytes 294920 | tf_op jit(solution)/shard_map/ppermute | solution.py:50
  110.8 6.5 %collective-permute-start.20 = (f16[320,256]{1,0:T(8,128)(2,1)S(1)}, f16[320,256]{1,0:T(8,128)(2,1)S(1)}, u32[]{:S(2)}, u32[]{:S(2)}) collective-permute-start(f16[320,256]{1,0:T(8,128)(2,1)S(1)} %select_convert_fusion), channel_id=1, source_target_pairs={{0,16},{8,24},{16,0},{24,8},{4,20},{12,28},{20,4},{28,12},{1,17},{... | collective-permute-start | bytes 491528 | tf_op jit(solution)/shard_map/ppermute | solution.py:55
  115.0 6.5 %collective-permute-start.25 = (f16[192,256]{1,0:T(8,128)(2,1)S(1)}, f16[192,256]{1,0:T(8,128)(2,1)S(1)}, u32[]{:S(2)}, u32[]{:S(2)}) collective-permute-start(f16[192,256]{1,0:T(8,128)(2,1)S(1)} %select_convert_fusion.1), channel_id=1, source_target_pairs={{0,16},{8,24},{16,0},{24,8},{4,20},{12,28},{20,4},{28,12},{1,17},{... | collective-permute-start | bytes 294920 | tf_op jit(solution)/shard_map/ppermute | solution.py:55
  117.4 10.9 %collective-permute-start.21 = (f16[320,256]{1,0:T(8,128)(2,1)S(1)}, f16[320,256]{1,0:T(8,128)(2,1)S(1)}, u32[]{:S(2)}, u32[]{:S(2)}) collective-permute-start(f16[320,256]{1,0:T(8,128)(2,1)S(1)} %add_convert_fusion.6), channel_id=1, source_target_pairs={{0,21},{8,29},{16,19},{24,27},{4,23},{12,31},{20,116},{28,124},{1,... | collective-permute-start | bytes 491528 | tf_op jit(solution)/shard_map/ppermute | solution.py:69
  121.6 6.8 %collective-permute-start.26 = (f16[192,256]{1,0:T(8,128)(2,1)S(1)}, f16[192,256]{1,0:T(8,128)(2,1)S(1)}, u32[]{:S(2)}, u32[]{:S(2)}) collective-permute-start(f16[192,256]{1,0:T(8,128)(2,1)S(1)} %add_convert_fusion.7), channel_id=1, source_target_pairs={{0,21},{8,29},{16,19},{24,27},{4,23},{12,31},{20,116},{28,124},{1,... | collective-permute-start | bytes 294920 | tf_op jit(solution)/shard_map/ppermute | solution.py:69

commit v6 on v5

--- a/solution.py
+++ b/solution.py
@@ -104,46 +104,30 @@
 
 
 def stage_kernel(late, lo, hi, n_in, *refs):
-    first, last = lo == 0, hi == COUNT
+    first, last, n = lo == 0, hi == COUNT, hi - lo
     sources, refs = refs[:n_in], refs[n_in:]
     n_out = (2 if last else 1) + (not late)
-    outs, (row, own_t, own, north, far, *rest, sems) = refs[:n_out], refs[n_out:]
+    outs, (*flipped, north_held, far_held) = refs[:n_out], refs[n_out:]
+    flipped = flipped[0] if late else outs[-1]
     rows = slice(chunk(lo).start, chunk(hi - 1).stop)
-    spans = [slice(chunk(k).start - rows.start, chunk(k).stop - rows.start) for k in range(lo, hi)]
-    pairs = [
-        (sources[0].at[:, rows], row),
-        (sources[1].at[:, rows], own_t),
-        (sources[2].at[rows, :], own),
-        *((s, north.at[c]) for s, c in zip(sources[3:], spans)),
-        *((s, far.at[c]) for s, c in zip(sources[3 + hi - lo :], spans)),
-    ]
-    extra = sources[len(pairs) :]
-    if late:
-        left, flipped = own_t, rest[0]
-        size, edge = own.shape[1], chunk(SPLIT).start
-        pairs[1] = (sources[1], left.at[:size])
-        pairs += [
-            (extra[0], left.at[size:, :edge]),
-            (extra[1], left.at[size:, edge:]),
-        ]
-    else:
-        flipped = outs[-1]
-        pairs += zip(extra, rest)
-    copies = [
-        pltpu.make_async_copy(s, t, sems.at[i]) for i, (s, t) in enumerate(pairs)
-    ]
-    for copy in copies:
-        copy.start()
+    row, own_t, own = sources[0][:, rows], sources[1], sources[2]
+    extra = sources[3 + 2 * n :]
+
+    def joined(blocks, held):
+        if n == 1:
+            return blocks[0]
+        for k, block in zip(range(lo, hi), blocks):
+            held[chunk(k).start - rows.start : chunk(k).stop - rows.start] = block[...]
+        return held
+
     pair, ga = lax.axis_index("pair"), lax.axis_index("ga")
     core, at = pair & 1, placing(planned(pair, ga)[int(late)])
     half = own.shape[1] // 2
 
-    def put(i, left, right):
-        keep(i, jnp.dot(left[...], right[...], preferred_element_type=jnp.float32))
-
-    def keep(i, total):
+    def keep(i, *pairs):
+        total = sum(jnp.dot(u, v, preferred_element_type=jnp.float32) for u, v in pairs)
         if not first:
-            total = total + rest[0][i]
+            total = total + extra[0][i]
         if last:
             low, high = total[:, :half], total[:, half:]
             outs[0][at[i]] = jnp.where(core == 0, high, low)
@@ -151,36 +135,26 @@
         else:
             outs[0][i] = total
 
-    for copy in copies:
-        copy.wait()
+    far = joined(sources[3 + n : 3 + 2 * n], far_held)
+    keep(0 if late else 2, (own_t[:, rows], far[...]))
+    flipped[...] = (row * far[...].T.astype(jnp.float32)).astype(flipped.dtype)
+    north = joined(sources[3 : 3 + n], north_held)
     if late:
-        total = jnp.dot(left[...], far[...], preferred_element_type=jnp.float32)
-        size = own.shape[1]
-        keep(0, total[:size])
-        keep(3, total[size:])
+        edge = chunk(SPLIT).start
+        keep(3, (extra[0][...], far[:edge, :]), (extra[1][...], far[edge:, :]))
+        keep(1, (flipped[...], own[...]))
+        keep(2, (flipped[...], north[...]))
     else:
-        put(0, own_t, own)
-        put(1, own_t, north)
-        put(2, own_t, far)
-    flipped[...] = (row[...] * far[...].T.astype(jnp.float32)).astype(flipped.dtype)
-    if late:
-        put(1, flipped, own)
-        put(2, flipped, north)
-    else:
-        put(3, flipped, north)
+        keep(0, (own_t[:, rows], own[rows, :]))
+        keep(1, (own_t[:, rows], north[...]))
+        keep(3, (flipped[...], north[...]))
 
 
 def run_stage(late, lo, hi, sources):
     size, _ = sources[1].shape
     rows = sum(CUTS[lo:hi])
     tall, wide = ((rows, size), jnp.bfloat16), ((size, rows), jnp.bfloat16)
-    held = [((1, rows), jnp.float32), wide, tall, tall, tall]
     outs = [((4, size, size), jnp.float32)]
-    if late:
-        held[1] = ((2 * size, rows), jnp.bfloat16)
-        held.append(wide)
-    elif lo:
-        held += outs
     if hi == COUNT:
         outs = [((4, size, size // 2), jnp.float32)] * 2
     if not late:
@@ -188,13 +162,10 @@
     return pl.pallas_call(
         functools.partial(stage_kernel, late, lo, hi, len(sources)),
         out_shape=[jax.ShapeDtypeStruct(*o) for o in outs],
-        in_specs=[pl.BlockSpec(memory_space=pl.ANY)] * len(sources),
+        in_specs=[pl.BlockSpec(memory_space=pltpu.VMEM)] * len(sources),
         out_specs=[pl.BlockSpec(memory_space=pltpu.VMEM)] * len(outs),
-        scratch_shapes=[
-            *(pltpu.VMEM(*h) for h in held),
-            pltpu.SemaphoreType.DMA((len(sources),)),
-        ],
-        compiler_params=pltpu.CompilerParams(vmem_limit_bytes=28 * 2**20),
+        scratch_shapes=[pltpu.VMEM(*h) for h in [wide] * late + [tall, tall]],
+        compiler_params=pltpu.CompilerParams(vmem_limit_bytes=40 * 2**20),
         cost_estimate=pl.CostEstimate(
             flops=8 * size * size * rows, bytes_accessed=2**23, transcendentals=0
         ),
@@ -228,7 +199,7 @@
             for d in range(4)
         ]
         kept, *sent = lax.optimization_barrier(
-            [joined[0]] + [joined[d].astype(jnp.float16) for d in (1, 3, 2)]
+            [joined[d].astype(jnp.float16) for d in (0, 1, 3, 2)]
         )
         got = []
         for part in parts:
@@ -257,7 +228,7 @@
     late, late_got = over_x(*late, tail)
 
     def sum_of(kept, got):
-        return kept + sum(g.astype(jnp.float32) for g in got)
+        return kept.astype(jnp.float32) + sum(g.astype(jnp.float32) for g in got)
 
     def after(value, other):
         return value if other is None else lax.optimization_barrier((value, other))[0]

time: 130 us -> 129 us (level)
  Pallas kernels: 12.8 us -> 8.81 us
  waiting for transfers between devices: 66.6 us -> 69.7 us
    pallas_call x3, Pallas kernels: 12.8 us -> 8.81 us  [run_stage(): pl.pallas_call(functools.partial(stage_kernel, late, lo, hi, len(sources)...]
    ppermute x23, waiting for transfers between devices: 55 us -> 58.2 us  [shift(): return lax.ppermute(value, AXES, pairs)]
  transfers between devices with their start and end apart: 27 -> 27, of which waited for: 16 -> 17; matrix products, arithmetic and copies ran while one was open for 9% -> 9% of each run, Pallas kernels for 10% -> 7%
where the time goes in v6:
time: 129 us; the launch traced here: 128 us
  waiting for transfers between devices  69.7 us (54%)
  starting transfers between devices  32.6 us (25%)
  other arithmetic  10.4 us (8%)
  Pallas kernels  8.81 us (7%)
  local copies, waits for them, and re-layouts  6.58 us (5%)
    ppermute x23, waiting for transfers between devices, shift(): return lax.ppermute(value, AXES, pairs)  58.2 us
    ppermute x23, starting transfers between devices, shift(): return lax.ppermute(value, AXES, pairs)  29.7 us
    pallas_call x3, Pallas kernels, run_stage(): pl.pallas_call(functools.partial(stage_kernel, late, lo, hi, len(sources)...  8.81 us
    ppermute x2, waiting for transfers between devices, to_owner(): return lax.ppermute(value, AXES, pairs)  6.72 us
    ppermute x2, waiting for transfers between devices, swap_z_lo(): return lax.ppermute(value, AXES, pairs)  4.86 us
    slice x2, local copies, waits for them, and re-layouts, rows(): return block[starts[k]:starts[k + 1]]  4.09 us
    ppermute x2, starting transfers between devices, swap_z_lo(): return lax.ppermute(value, AXES, pairs)  2.73 us
  transfers between devices with their start and end apart: 27, of which 17 were waited for; matrix products, arithmetic and copies ran while one was open for 9% of the time, Pallas kernels for 7%

profile of v6, /device:TPU:24, one launch (start us, length us, event | category | flops | bytes accessed | tf_op | source)
XLA Modules:
  0.0 128.4 jit_solution(4620855880193809566)
XLA Ops:
  0.0 1.9 %slice.92 = bf16[384,512]{1,0:T(8,128)(2,1)} slice(bf16[1536,512]{1,0:T(8,128)(2,1)} %refs_2_.5), slice={[0:384], [0:512]} | slice | bytes 786432 | tf_op jit(solution)/shard_map/slice | solution.py:181
  1.9 2.2 %fusion.9 = (bf16[384,512]{1,0:T(8,128)(2,1)}, bf16[384,512]{1,0:T(8,128)(2,1)}, bf16[384,512]{1,0:T(8,128)(2,1)S(1)}) fusion(bf16[1536,512]{1,0:T(8,128)(2,1)} %refs_2_.5), kind=kLoop, calls=%fused_computation.31 | loop fusion | bytes 2359296 | tf_op jit(solution)/shard_map/slice | solution.py:181
  4.1 0.7 collective-permute-start
  4.8 0.4 collective-permute-start.2
  5.3 2.8 %collective-permute-start.5 = (bf16[384,512]{1,0:T(8,128)(2,1)}, bf16[384,512]{1,0:T(8,128)(2,1)S(1)}, u32[]{:S(2)}, u32[]{:S(2)}) collective-permute-start(bf16[384,512]{1,0:T(8,128)(2,1)} %slice.92), channel_id=1, source_target_pairs={{0,1},{8,9},{16,17},{24,25},{4,5},{12,13},{20,21},{28,29},{1,2},{9... | collective-permute-start | bytes 1179656 | tf_op jit(solution)/shard_map/ppermute | solution.py:50
  8.1 3.2 %collective-permute-start.6 = (bf16[384,512]{1,0:T(8,128)(2,1)}, bf16[384,512]{1,0:T(8,128)(2,1)}, u32[]{:S(2)}, u32[]{:S(2)}) collective-permute-start(bf16[384,512]{1,0:T(8,128)(2,1)} %get-tuple-element.66), channel_id=1, source_target_pairs={{0,1},{8,9},{16,17},{24,25},{4,5},{12,13},{20,21},{28,29},{1,2},{9... | collective-permute-start | bytes 1179656 | tf_op jit(solution)/shard_map/ppermute | solution.py:50
  11.3 6.0 %collective-permute-done.refs_3_.refs_6_ = bf16[384,512]{1,0:T(8,128)(2,1)S(1)} collective-permute-done((bf16[384,512]{1,0:T(8,128)(2,1)S(1)}, bf16[384,512]{1,0:T(8,128)(2,1)S(1)}, u32[]{:S(2)}, u32[]{:S(2)}) %collective-permute-start) | collective-permute-done | bytes 393248 | tf_op jit(solution)/shard_map/ppermute | solution.py:50
  17.3 8.4 %collective-permute-done.2.refs_3_ = bf16[384,512]{1,0:T(8,128)(2,1)S(1)} collective-permute-done((bf16[384,512]{1,0:T(8,128)(2,1)}, bf16[384,512]{1,0:T(8,128)(2,1)S(1)}, u32[]{:S(2)}, u32[]{:S(2)}) %collective-permute-start.2) | collective-permute-done | bytes 393248 | tf_op jit(solution)/shard_map/ppermute | solution.py:50
  25.7 0.5 select_reduce_fusion.1
  26.3 1.6 %copy.7 = bf16[1536,512]{0,1:T(8,128)(2,1)} copy(bf16[1536,512]{1,0:T(8,128)(2,1)S(1)} %copy-done) | data formatting | bytes 3145728 | tf_op args[0]
  27.9 1.2 select_reduce_fusion
  29.1 5.1 %collective-permute-done.3.refs_4_ = bf16[384,512]{1,0:T(8,128)(2,1)S(1)} collective-permute-done((bf16[384,512]{1,0:T(8,128)(2,1)}, bf16[384,512]{1,0:T(8,128)(2,1)S(1)}, u32[]{:S(2)}, u32[]{:S(2)}) %collective-permute-start.3) | collective-permute-done | bytes 393248 | tf_op jit(solution)/shard_map/ppermute | solution.py:50
  34.2 7.3 %collective-permute-done.4.refs_5_ = bf16[384,512]{1,0:T(8,128)(2,1)S(1)} collective-permute-done((bf16[384,512]{1,0:T(8,128)(2,1)}, bf16[384,512]{1,0:T(8,128)(2,1)S(1)}, u32[]{:S(2)}, u32[]{:S(2)}) %collective-permute-start.4) | collective-permute-done | bytes 393248 | tf_op jit(solution)/shard_map/ppermute | solution.py:50
  41.4 3.9 %collective-permute-start.12 = (bf16[384,512]{1,0:T(8,128)(2,1)S(1)}, bf16[384,512]{1,0:T(8,128)(2,1)S(1)}, u32[]{:S(2)}, u32[]{:S(2)}) collective-permute-start(bf16[384,512]{1,0:T(8,128)(2,1)S(1)} %collective-permute-done.2.refs_3_), channel_id=1, source_target_pairs={{0,4},{8,12},{16,20},{24,28},{4,0},{12,8},{20,16},{28,24},{1,5},{9... | collective-permute-start | bytes 1179656 | tf_op jit(solution)/shard_map/ppermute | solution.py:50
  45.4 3.5 %collective-permute-start.14 = (bf16[384,512]{1,0:T(8,128)(2,1)S(1)}, bf16[384,512]{1,0:T(8,128)(2,1)S(1)}, u32[]{:S(2)}, u32[]{:S(2)}) collective-permute-start(bf16[384,512]{1,0:T(8,128)(2,1)S(1)} %collective-permute-done.4.refs_5_), channel_id=1, source_target_pairs={{0,4},{8,12},{16,20},{24,28},{4,0},{12,8},{20,16},{28,24},{1,5},{9... | collective-permute-start | bytes 1179656 | tf_op jit(solution)/shard_map/ppermute | solution.py:50
  49.0 1.7 %fusion.refs_1_ = bf16[512,1536]{1,0:T(8,128)(2,1)S(1)} fusion(bf16[1536,512]{0,1:T(8,128)(2,1)} %copy.7, f32[1536]{0:T(1024)S(1)} %multiply_divide_fusion), kind=kLoop, calls=%fused_computation.1 | loop fusion | flops 2359296 | bytes 3151872 | tf_op jit(solution)/shard_map/convert_element_type | solution.py:214
  50.6 4.0 %shard_map.55 = (f32[4,512,512]{2,1,0:T(8,128)S(1)}, bf16[512,1152]{1,0:T(8,128)(2,1)S(1)}) custom-call(f32[1,1536]{1,0:T(1,128)S(1)} %div.19.refs_0_, bf16[512,1536]{1,0:T(8,128)(2,1)S(1)} %fusion.refs_1_, bf16[1536,512]{1,0:T(8,128)(2,1)S(1)} %copy-done, bf16[384,512]{1,0:T(8,128)(2,1)S(1)} %collective-permute-done.2.refs_3_, ...), custom_call_target="tpu_custom_call" | custom-call | flops 2415919104 | bytes 8388608 | tf_op jit(solution)/shard_map/pallas_call | solution.py:162
  54.7 1.3 shard_map.56
  55.9 1.2 convert_element_type.196
  57.1 1.2 convert_element_type.197
  58.3 5.4 %collective-permute-done.13.refs_8_ = bf16[384,512]{1,0:T(8,128)(2,1)S(1)} collective-permute-done((bf16[384,512]{1,0:T(8,128)(2,1)S(1)}, bf16[384,512]{1,0:T(8,128)(2,1)S(1)}, u32[]{:S(2)}, u32[]{:S(2)}) %collective-permute-start.13) | collective-permute-done | bytes 393248 | tf_op jit(solution)/shard_map/ppermute | solution.py:50
  63.7 8.4 %collective-permute-done.14.refs_9_ = bf16[384,512]{1,0:T(8,128)(2,1)S(1)} collective-permute-done((bf16[384,512]{1,0:T(8,128)(2,1)S(1)}, bf16[384,512]{1,0:T(8,128)(2,1)S(1)}, u32[]{:S(2)}, u32[]{:S(2)}) %collective-permute-start.14) | collective-permute-done | bytes 393248 | tf_op jit(solution)/shard_map/ppermute | solution.py:50
  72.1 6.7 %collective-permute-done.15.refs_10_ = bf16[384,512]{1,0:T(8,128)(2,1)S(1)} collective-permute-done((bf16[384,512]{1,0:T(8,128)(2,1)S(1)}, bf16[384,512]{1,0:T(8,128)(2,1)S(1)}, u32[]{:S(2)}, u32[]{:S(2)}) %collective-permute-start.15) | collective-permute-done | bytes 393248 | tf_op jit(solution)/shard_map/ppermute | solution.py:50
  78.9 3.5 %shard_map.57 = (f32[4,512,256]{2,1,0:T(8,128)S(1)}, f32[4,512,256]{2,1,0:T(8,128)S(1)}) custom-call(f32[1,1536]{1,0:T(1,128)S(1)} %div.19.refs_0_, bf16[512,1536]{1,0:T(8,128)(2,1)S(1)} %fusion.refs_1_, bf16[1536,512]{1,0:T(8,128)(2,1)S(1)} %copy-done, bf16[384,512]{1,0:T(8,128)(2,1)S(1)} %collective-permute-done.2.refs_3_, ...), custom_call_target="tpu_custom_call" | custom-call | flops 3221225472 | bytes 8388608 | tf_op jit(solution)/shard_map/pallas_call | solution.py:162
  82.4 1.2 convert_element_type.218
  84.1 0.7 copy-done.1
  84.8 1.5 %fusion.4 = (f16[512,256]{1,0:T(8,128)(2,1)S(1)}, f16[512,256]{1,0:T(8,128)(2,1)S(1)}, f16[512,256]{1,0:T(8,128)(2,1)S(1)}, f16[512,256]{1,0:T(8,128)(2,1)S(1)}) fusion(f16[4,512,256]{2,1,0:T(8,128)(2,1)} %collective-permute-done.8, f16[4,512,256]{2,1,0:T(8,128)(2,1)S(1)} %copy-done.1), kind=kLoop, calls=%fused_computation.22 | loop fusion | flops 2097152 | bytes 3145728 | tf_op jit(solution)/shard_map/convert_element_type | solution.py:202
  86.4 3.1 %collective-permute-start.11 = (f16[512,256]{1,0:T(8,128)(2,1)S(1)}, f16[512,256]{1,0:T(8,128)(2,1)S(1)}, u32[]{:S(2)}, u32[]{:S(2)}) collective-permute-start(f16[512,256]{1,0:T(8,128)(2,1)S(1)} %get-tuple-element.42), channel_id=1, source_target_pairs={{0,64},{8,72},{16,80},{24,88},{4,68},{12,76},{20,84},{28,92},{1,65... | collective-permute-start | bytes 786440 | tf_op jit(solution)/shard_map/ppermute | solution.py:50
  89.5 1.1 collective-permute-start.10
  90.6 0.9 collective-permute-start.9
  91.5 0.3 fusion.8
  91.8 0.7 collective-permute-start.19
  92.6 2.7 %collective-permute-start.18 = (f16[320,256]{1,0:T(8,128)(2,1)S(1)}, f16[320,256]{1,0:T(8,128)(2,1)S(1)}, u32[]{:S(2)}, u32[]{:S(2)}) collective-permute-start(f16[320,256]{1,0:T(8,128)(2,1)S(1)} %slice.115), channel_id=1, source_target_pairs={{0,96},{8,104},{16,112},{24,120},{4,100},{12,108},{20,116},{28,124... | collective-permute-start | bytes 491528 | tf_op jit(solution)/shard_map/ppermute | solution.py:50
  95.3 1.8 %collective-permute-done.11 = f16[512,256]{1,0:T(8,128)(2,1)S(1)} collective-permute-done((f16[512,256]{1,0:T(8,128)(2,1)S(1)}, f16[512,256]{1,0:T(8,128)(2,1)S(1)}, u32[]{:S(2)}, u32[]{:S(2)}) %collective-permute-start.11) | collective-permute-done | bytes 262176 | tf_op jit(solution)/shard_map/ppermute | solution.py:50
  97.1 1.5 %collective-permute-start.17 = (f16[320,256]{1,0:T(8,128)(2,1)S(1)}, f16[320,256]{1,0:T(8,128)(2,1)S(1)}, u32[]{:S(2)}, u32[]{:S(2)}) collective-permute-start(f16[320,256]{1,0:T(8,128)(2,1)S(1)} %slice.114), channel_id=1, source_target_pairs={{0,32},{8,40},{16,48},{24,56},{4,36},{12,44},{20,52},{28,60},{1,33... | collective-permute-start | bytes 491528 | tf_op jit(solution)/shard_map/ppermute | solution.py:50
  98.6 4.2 %collective-permute-done.10 = f16[512,256]{1,0:T(8,128)(2,1)S(1)} collective-permute-done((f16[512,256]{1,0:T(8,128)(2,1)S(1)}, f16[512,256]{1,0:T(8,128)(2,1)S(1)}, u32[]{:S(2)}, u32[]{:S(2)}) %collective-permute-start.10) | collective-permute-done | bytes 262176 | tf_op jit(solution)/shard_map/ppermute | solution.py:50
  102.9 1.6 %collective-permute-done.9 = f16[512,256]{1,0:T(8,128)(2,1)S(1)} collective-permute-done((f16[512,256]{1,0:T(8,128)(2,1)S(1)}, f16[512,256]{1,0:T(8,128)(2,1)S(1)}, u32[]{:S(2)}, u32[]{:S(2)}) %collective-permute-start.9) | collective-permute-done | bytes 262176 | tf_op jit(solution)/shard_map/ppermute | solution.py:50
  104.7 3.2 %collective-permute-start.23 = (f16[192,256]{1,0:T(8,128)(2,1)S(1)}, f16[192,256]{1,0:T(8,128)(2,1)S(1)}, u32[]{:S(2)}, u32[]{:S(2)}) collective-permute-start(f16[192,256]{1,0:T(8,128)(2,1)S(1)} %slice.120), channel_id=1, source_target_pairs={{0,96},{8,104},{16,112},{24,120},{4,100},{12,108},{20,116},{28,124... | collective-permute-start | bytes 294920 | tf_op jit(solution)/shard_map/ppermute | solution.py:50
  108.0 1.4 %collective-permute-start.24 = (f16[192,256]{1,0:T(8,128)(2,1)S(1)}, f16[192,256]{1,0:T(8,128)(2,1)S(1)}, u32[]{:S(2)}, u32[]{:S(2)}) collective-permute-start(f16[192,256]{1,0:T(8,128)(2,1)S(1)} %slice.121), channel_id=1, source_target_pairs={{0,64},{8,72},{16,80},{24,88},{4,68},{12,76},{20,84},{28,92},{1,65... | collective-permute-start | bytes 294920 | tf_op jit(solution)/shard_map/ppermute | solution.py:50
  109.4 0.6 collective-permute-done.18
  110.0 1.4 %collective-permute-start.20 = (f16[320,256]{1,0:T(8,128)(2,1)S(1)}, f16[320,256]{1,0:T(8,128)(2,1)S(1)}, u32[]{:S(2)}, u32[]{:S(2)}) collective-permute-start(f16[320,256]{1,0:T(8,128)(2,1)S(1)} %select_convert_fusion), channel_id=1, source_target_pairs={{0,16},{8,24},{16,0},{24,8},{4,20},{12,28},{20,4},{28,12},{1,17},{... | collective-permute-start | bytes 491528 | tf_op jit(solution)/shard_map/ppermute | solution.py:55
  111.5 0.4 collective-permute-done.23
  111.9 2.2 %collective-permute-done.24 = f16[192,256]{1,0:T(8,128)(2,1)S(1)} collective-permute-done((f16[192,256]{1,0:T(8,128)(2,1)S(1)}, f16[192,256]{1,0:T(8,128)(2,1)S(1)}, u32[]{:S(2)}, u32[]{:S(2)}) %collective-permute-start.24) | collective-permute-done | bytes 98336 | tf_op jit(solution)/shard_map/ppermute | solution.py:50
  114.2 1.4 %collective-permute-start.25 = (f16[192,256]{1,0:T(8,128)(2,1)S(1)}, f16[192,256]{1,0:T(8,128)(2,1)S(1)}, u32[]{:S(2)}, u32[]{:S(2)}) collective-permute-start(f16[192,256]{1,0:T(8,128)(2,1)S(1)} %select_convert_fusion.1), channel_id=1, source_target_pairs={{0,16},{8,24},{16,0},{24,8},{4,20},{12,28},{20,4},{28,12},{1,17},{... | collective-permute-start | bytes 294920 | tf_op jit(solution)/shard_map/ppermute | solution.py:55
  115.5 1.0 collective-permute-done.20
  116.7 3.9 %collective-permute-done.25 = f16[192,256]{1,0:T(8,128)(2,1)S(1)} collective-permute-done((f16[192,256]{1,0:T(8,128)(2,1)S(1)}, f16[192,256]{1,0:T(8,128)(2,1)S(1)}, u32[]{:S(2)}, u32[]{:S(2)}) %collective-permute-start.25) | collective-permute-done | bytes 98336 | tf_op jit(solution)/shard_map/ppermute | solution.py:55
  120.8 6.7 %collective-permute-done.26 = f16[192,256]{1,0:T(8,128)(2,1)S(1)} collective-permute-done((f16[192,256]{1,0:T(8,128)(2,1)S(1)}, f16[192,256]{1,0:T(8,128)(2,1)S(1)}, u32[]{:S(2)}, u32[]{:S(2)}) %collective-permute-start.26) | collective-permute-done | bytes 98336 | tf_op jit(solution)/shard_map/ppermute | solution.py:69
  127.5 0.8 convert_multiply_fusion
  (47 shorter events, 1.7 us)
Async XLA Ops:
  0.0 26.2 %copy-start = (bf16[1536,512]{1,0:T(8,128)(2,1)S(1)}, bf16[1536,512]{1,0:T(8,128)(2,1)}, u32[]{:S(2)}) copy-start(bf16[1536,512]{1,0:T(8,128)(2,1)} %refs_2_.5) | copy-start | bytes 4718596
  0.0 25.7 %copy-start.5 = (f32[128]{0:T(128)S(1)}, f32[128]{0:T(128)}, u32[]{:S(2)}) copy-start(f32[128]{0:T(128)} %param.8) | copy-start | bytes 1540
  0.0 25.7 %copy-start.3 = (s32[1536]{0:T(1024)S(1)}, s32[1536]{0:T(1024)}, u32[]{:S(2)}) copy-start(s32[1536]{0:T(1024)} %param.6) | copy-start | bytes 18436
  4.1 13.2 %copy-start.2 = (bf16[384,512]{1,0:T(8,128)(2,1)}, bf16[384,512]{1,0:T(8,128)(2,1)S(1)}, u32[]{:S(2)}) copy-start(bf16[384,512]{1,0:T(8,128)(2,1)S(1)} %get-tuple-element.67) | copy-start | bytes 1179652
  4.1 13.2 %collective-permute-start = (bf16[384,512]{1,0:T(8,128)(2,1)S(1)}, bf16[384,512]{1,0:T(8,128)(2,1)S(1)}, u32[]{:S(2)}, u32[]{:S(2)}) collective-permute-start(bf16[384,512]{1,0:T(8,128)(2,1)S(1)} %get-tuple-element.67), channel_id=1, source_target_pairs={{0,3},{8,11},{16,19},{24,27},{4,7},{12,15},{20,23},{28,31},{1,0},{... | collective-permute-start | bytes 1179656 | tf_op jit(solution)/shard_map/ppermute | solution.py:50
  4.8 20.9 %collective-permute-start.2 = (bf16[384,512]{1,0:T(8,128)(2,1)}, bf16[384,512]{1,0:T(8,128)(2,1)S(1)}, u32[]{:S(2)}, u32[]{:S(2)}) collective-permute-start(bf16[384,512]{1,0:T(8,128)(2,1)} %slice.92), channel_id=1, source_target_pairs={{0,3},{8,11},{16,19},{24,27},{4,7},{12,15},{20,23},{28,31},{1,0},{... | collective-permute-start | bytes 1179656 | tf_op jit(solution)/shard_map/ppermute | solution.py:50
  5.3 40.0 %collective-permute-start.5 = (bf16[384,512]{1,0:T(8,128)(2,1)}, bf16[384,512]{1,0:T(8,128)(2,1)S(1)}, u32[]{:S(2)}, u32[]{:S(2)}) collective-permute-start(bf16[384,512]{1,0:T(8,128)(2,1)} %slice.92), channel_id=1, source_target_pairs={{0,1},{8,9},{16,17},{24,25},{4,5},{12,13},{20,21},{28,29},{1,2},{9... | collective-permute-start | bytes 1179656 | tf_op jit(solution)/shard_map/ppermute | solution.py:50
  8.1 26.1 %collective-permute-start.3 = (bf16[384,512]{1,0:T(8,128)(2,1)}, bf16[384,512]{1,0:T(8,128)(2,1)S(1)}, u32[]{:S(2)}, u32[]{:S(2)}) collective-permute-start(bf16[384,512]{1,0:T(8,128)(2,1)} %get-tuple-element.66), channel_id=1, source_target_pairs={{0,3},{8,11},{16,19},{24,27},{4,7},{12,15},{20,23},{28,31},{1,0},{... | collective-permute-start | bytes 1179656 | tf_op jit(solution)/shard_map/ppermute | solution.py:50
  8.1 37.3 %collective-permute-start.6 = (bf16[384,512]{1,0:T(8,128)(2,1)}, bf16[384,512]{1,0:T(8,128)(2,1)}, u32[]{:S(2)}, u32[]{:S(2)}) collective-permute-start(bf16[384,512]{1,0:T(8,128)(2,1)} %get-tuple-element.66), channel_id=1, source_target_pairs={{0,1},{8,9},{16,17},{24,25},{4,5},{12,13},{20,21},{28,29},{1,2},{9... | collective-permute-start | bytes 1179656 | tf_op jit(solution)/shard_map/ppermute | solution.py:50
  17.3 24.1 %collective-permute-start.4 = (bf16[384,512]{1,0:T(8,128)(2,1)}, bf16[384,512]{1,0:T(8,128)(2,1)S(1)}, u32[]{:S(2)}, u32[]{:S(2)}) collective-permute-start(bf16[384,512]{1,0:T(8,128)(2,1)} %get-tuple-element.65), channel_id=1, source_target_pairs={{0,3},{8,11},{16,19},{24,27},{4,7},{12,15},{20,23},{28,31},{1,0},{... | collective-permute-start | bytes 1179656 | tf_op jit(solution)/shard_map/ppermute | solution.py:50
  25.7 23.1 %collective-permute-start.7 = (bf16[384,512]{1,0:T(8,128)(2,1)}, bf16[384,512]{1,0:T(8,128)(2,1)}, u32[]{:S(2)}, u32[]{:S(2)}) collective-permute-start(bf16[384,512]{1,0:T(8,128)(2,1)} %get-tuple-element.65), channel_id=1, source_target_pairs={{0,1},{8,9},{16,17},{24,25},{4,5},{12,13},{20,21},{28,29},{1,2},{9... | collective-permute-start | bytes 1179656 | tf_op jit(solution)/shard_map/ppermute | solution.py:50
  26.2 1.6 %copy-start.4 = (s32[1536]{0:T(1024)S(1)}, s32[1536]{0:T(1024)}, u32[]{:S(2)}) copy-start(s32[1536]{0:T(1024)} %param.7) | copy-start | bytes 18436
  34.2 20.5 %collective-permute-start.1 = (bf16[384,512]{1,0:T(8,128)(2,1)}, bf16[384,512]{1,0:T(8,128)(2,1)S(1)}, u32[]{:S(2)}, u32[]{:S(2)}) collective-permute-start(bf16[384,512]{1,0:T(8,128)(2,1)} %copy-done.2), channel_id=1, source_target_pairs={{0,1},{8,9},{16,17},{24,25},{4,5},{12,13},{20,21},{28,29},{1,2},{9... | collective-permute-start | bytes 1179656 | tf_op jit(solution)/shard_map/ppermute | solution.py:50
  41.4 16.9 %collective-permute-start.12 = (bf16[384,512]{1,0:T(8,128)(2,1)S(1)}, bf16[384,512]{1,0:T(8,128)(2,1)S(1)}, u32[]{:S(2)}, u32[]{:S(2)}) collective-permute-start(bf16[384,512]{1,0:T(8,128)(2,1)S(1)} %collective-permute-done.2.refs_3_), channel_id=1, source_target_pairs={{0,4},{8,12},{16,20},{24,28},{4,0},{12,8},{20,16},{28,24},{1,5},{9... | collective-permute-start | bytes 1179656 | tf_op jit(solution)/shard_map/ppermute | solution.py:50
  45.3 18.4 %collective-permute-start.13 = (bf16[384,512]{1,0:T(8,128)(2,1)S(1)}, bf16[384,512]{1,0:T(8,128)(2,1)S(1)}, u32[]{:S(2)}, u32[]{:S(2)}) collective-permute-start(bf16[384,512]{1,0:T(8,128)(2,1)S(1)} %collective-permute-done.3.refs_4_), channel_id=1, source_target_pairs={{0,4},{8,12},{16,20},{24,28},{4,0},{12,8},{20,16},{28,24},{1,5},{9... | collective-permute-start | bytes 1179656 | tf_op jit(solution)/shard_map/ppermute | solution.py:50
  45.4 26.8 %collective-permute-start.14 = (bf16[384,512]{1,0:T(8,128)(2,1)S(1)}, bf16[384,512]{1,0:T(8,128)(2,1)S(1)}, u32[]{:S(2)}, u32[]{:S(2)}) collective-permute-start(bf16[384,512]{1,0:T(8,128)(2,1)S(1)} %collective-permute-done.4.refs_5_), channel_id=1, source_target_pairs={{0,4},{8,12},{16,20},{24,28},{4,0},{12,8},{20,16},{28,24},{1,5},{9... | collective-permute-start | bytes 1179656 | tf_op jit(solution)/shard_map/ppermute | solution.py:50
  48.9 30.0 %collective-permute-start.15 = (bf16[384,512]{1,0:T(8,128)(2,1)S(1)}, bf16[384,512]{1,0:T(8,128)(2,1)S(1)}, u32[]{:S(2)}, u32[]{:S(2)}) collective-permute-start(bf16[384,512]{1,0:T(8,128)(2,1)S(1)} %collective-permute-done.refs_3_.refs_6_), channel_id=1, source_target_pairs={{0,4},{8,12},{16,20},{24,28},{4,0},{12,8},{20,16},{28,24},{1,5},{9... | collective-permute-start | bytes 1179656 | tf_op jit(solution)/shard_map/ppermute | solution.py:50
  58.3 25.8 %collective-permute-start.8 = (f16[4,512,256]{2,1,0:T(8,128)(2,1)}, f16[4,512,256]{2,1,0:T(8,128)(2,1)}, u32[]{:S(2)}, u32[]{:S(2)}) collective-permute-start(f16[4,512,256]{2,1,0:T(8,128)(2,1)} %convert_element_type.196), channel_id=1, source_target_pairs={{0,8},{8,0},{16,24},{24,16},{4,12},{12,4},{20,28},{28,20},{1,9},{9... | collective-permute-start | bytes 3145736 | tf_op jit(solution)/shard_map/ppermute | solution.py:50
  83.6 1.2 copy-start.1
  83.8 7.7 %collective-permute-start.16 = (f16[4,512,256]{2,1,0:T(8,128)(2,1)}, f16[4,512,256]{2,1,0:T(8,128)(2,1)S(1)}, u32[]{:S(2)}, u32[]{:S(2)}) collective-permute-start(f16[4,512,256]{2,1,0:T(8,128)(2,1)} %convert_element_type.218), channel_id=1, source_target_pairs={{0,8},{8,0},{16,24},{24,16},{4,12},{12,4},{20,28},{28,20},{1,9},{9... | collective-permute-start | bytes 3145736 | tf_op jit(solution)/shard_map/ppermute | solution.py:50
  86.4 10.8 %collective-permute-start.11 = (f16[512,256]{1,0:T(8,128)(2,1)S(1)}, f16[512,256]{1,0:T(8,128)(2,1)S(1)}, u32[]{:S(2)}, u32[]{:S(2)}) collective-permute-start(f16[512,256]{1,0:T(8,128)(2,1)S(1)} %get-tuple-element.42), channel_id=1, source_target_pairs={{0,64},{8,72},{16,80},{24,88},{4,68},{12,76},{20,84},{28,92},{1,65... | collective-permute-start | bytes 786440 | tf_op jit(solution)/shard_map/ppermute | solution.py:50
  89.5 13.4 %collective-permute-start.10 = (f16[512,256]{1,0:T(8,128)(2,1)S(1)}, f16[512,256]{1,0:T(8,128)(2,1)S(1)}, u32[]{:S(2)}, u32[]{:S(2)}) collective-permute-start(f16[512,256]{1,0:T(8,128)(2,1)S(1)} %get-tuple-element.41), channel_id=1, source_target_pairs={{0,96},{8,104},{16,112},{24,120},{4,100},{12,108},{20,116},{28,124... | collective-permute-start | bytes 786440 | tf_op jit(solution)/shard_map/ppermute | solution.py:50
  90.6 13.9 %collective-permute-start.9 = (f16[512,256]{1,0:T(8,128)(2,1)S(1)}, f16[512,256]{1,0:T(8,128)(2,1)S(1)}, u32[]{:S(2)}, u32[]{:S(2)}) collective-permute-start(f16[512,256]{1,0:T(8,128)(2,1)S(1)} %get-tuple-element.40), channel_id=1, source_target_pairs={{0,32},{8,40},{16,48},{24,56},{4,36},{12,44},{20,52},{28,60},{1,33... | collective-permute-start | bytes 786440 | tf_op jit(solution)/shard_map/ppermute | solution.py:50
  91.8 16.1 %collective-permute-start.19 = (f16[320,256]{1,0:T(8,128)(2,1)S(1)}, f16[320,256]{1,0:T(8,128)(2,1)S(1)}, u32[]{:S(2)}, u32[]{:S(2)}) collective-permute-start(f16[320,256]{1,0:T(8,128)(2,1)S(1)} %slice.116), channel_id=1, source_target_pairs={{0,64},{8,72},{16,80},{24,88},{4,68},{12,76},{20,84},{28,92},{1,65... | collective-permute-start | bytes 491528 | tf_op jit(solution)/shard_map/ppermute | solution.py:50
  92.6 17.3 %collective-permute-start.18 = (f16[320,256]{1,0:T(8,128)(2,1)S(1)}, f16[320,256]{1,0:T(8,128)(2,1)S(1)}, u32[]{:S(2)}, u32[]{:S(2)}) collective-permute-start(f16[320,256]{1,0:T(8,128)(2,1)S(1)} %slice.115), channel_id=1, source_target_pairs={{0,96},{8,104},{16,112},{24,120},{4,100},{12,108},{20,116},{28,124... | collective-permute-start | bytes 491528 | tf_op jit(solution)/shard_map/ppermute | solution.py:50
  97.1 12.8 %collective-permute-start.17 = (f16[320,256]{1,0:T(8,128)(2,1)S(1)}, f16[320,256]{1,0:T(8,128)(2,1)S(1)}, u32[]{:S(2)}, u32[]{:S(2)}) collective-permute-start(f16[320,256]{1,0:T(8,128)(2,1)S(1)} %slice.114), channel_id=1, source_target_pairs={{0,32},{8,40},{16,48},{24,56},{4,36},{12,44},{20,52},{28,60},{1,33... | collective-permute-start | bytes 491528 | tf_op jit(solution)/shard_map/ppermute | solution.py:50
  104.7 6.9 %collective-permute-start.22 = (f16[192,256]{1,0:T(8,128)(2,1)S(1)}, f16[192,256]{1,0:T(8,128)(2,1)S(1)}, u32[]{:S(2)}, u32[]{:S(2)}) collective-permute-start(f16[192,256]{1,0:T(8,128)(2,1)S(1)} %slice.119), channel_id=1, source_target_pairs={{0,32},{8,40},{16,48},{24,56},{4,36},{12,44},{20,52},{28,60},{1,33... | collective-permute-start | bytes 294920 | tf_op jit(solution)/shard_map/ppermute | solution.py:50
  104.7 7.1 %collective-permute-start.23 = (f16[192,256]{1,0:T(8,128)(2,1)S(1)}, f16[192,256]{1,0:T(8,128)(2,1)S(1)}, u32[]{:S(2)}, u32[]{:S(2)}) collective-permute-start(f16[192,256]{1,0:T(8,128)(2,1)S(1)} %slice.120), channel_id=1, source_target_pairs={{0,96},{8,104},{16,112},{24,120},{4,100},{12,108},{20,116},{28,124... | collective-permute-start | bytes 294920 | tf_op jit(solution)/shard_map/ppermute | solution.py:50
  108.0 6.1 %collective-permute-start.24 = (f16[192,256]{1,0:T(8,128)(2,1)S(1)}, f16[192,256]{1,0:T(8,128)(2,1)S(1)}, u32[]{:S(2)}, u32[]{:S(2)}) collective-permute-start(f16[192,256]{1,0:T(8,128)(2,1)S(1)} %slice.121), channel_id=1, source_target_pairs={{0,64},{8,72},{16,80},{24,88},{4,68},{12,76},{20,84},{28,92},{1,65... | collective-permute-start | bytes 294920 | tf_op jit(solution)/shard_map/ppermute | solution.py:50
  110.0 6.5 %collective-permute-start.20 = (f16[320,256]{1,0:T(8,128)(2,1)S(1)}, f16[320,256]{1,0:T(8,128)(2,1)S(1)}, u32[]{:S(2)}, u32[]{:S(2)}) collective-permute-start(f16[320,256]{1,0:T(8,128)(2,1)S(1)} %select_convert_fusion), channel_id=1, source_target_pairs={{0,16},{8,24},{16,0},{24,8},{4,20},{12,28},{20,4},{28,12},{1,17},{... | collective-permute-start | bytes 491528 | tf_op jit(solution)/shard_map/ppermute | solution.py:55
  114.2 6.5 %collective-permute-start.25 = (f16[192,256]{1,0:T(8,128)(2,1)S(1)}, f16[192,256]{1,0:T(8,128)(2,1)S(1)}, u32[]{:S(2)}, u32[]{:S(2)}) collective-permute-start(f16[192,256]{1,0:T(8,128)(2,1)S(1)} %select_convert_fusion.1), channel_id=1, source_target_pairs={{0,16},{8,24},{16,0},{24,8},{4,20},{12,28},{20,4},{28,12},{1,17},{... | collective-permute-start | bytes 294920 | tf_op jit(solution)/shard_map/ppermute | solution.py:55
  116.6 10.9 %collective-permute-start.21 = (f16[320,256]{1,0:T(8,128)(2,1)S(1)}, f16[320,256]{1,0:T(8,128)(2,1)S(1)}, u32[]{:S(2)}, u32[]{:S(2)}) collective-permute-start(f16[320,256]{1,0:T(8,128)(2,1)S(1)} %add_convert_fusion.8), channel_id=1, source_target_pairs={{0,21},{8,29},{16,19},{24,27},{4,23},{12,31},{20,116},{28,124},{1,... | collective-permute-start | bytes 491528 | tf_op jit(solution)/shard_map/ppermute | solution.py:69
  120.7 6.8 %collective-permute-start.26 = (f16[192,256]{1,0:T(8,128)(2,1)S(1)}, f16[192,256]{1,0:T(8,128)(2,1)S(1)}, u32[]{:S(2)}, u32[]{:S(2)}) collective-permute-start(f16[192,256]{1,0:T(8,128)(2,1)S(1)} %add_convert_fusion.9), channel_id=1, source_target_pairs={{0,21},{8,29},{16,19},{24,27},{4,23},{12,31},{20,116},{28,124},{1,... | collective-permute-start | bytes 294920 | tf_op jit(solution)/shard_map/ppermute | solution.py:69
